TPU v7x, 32 devices: a whole 2x2x4 slice. The times are simulated.
32 devices in a mesh: band: 8 (over z, x), ens: 4 (over y, core).
Axes of the slice: x: 2, y: 2, z: 4, core: 2. Of those that a mesh axis runs over, the one named last changes fastest.
Arguments:
- grid_latent: bfloat16 [4, 1024, 1024], P('ens', 'band'), may hold values from -6 to 6
- hidden: bfloat16 [4, 256, 1024], P('ens', 'band'), may hold values from -6 to 6
- d_updated: bfloat16 [4, 256, 1024], P('ens', 'band'), may hold values from -6 to 6
- w_kv: bfloat16 [1024, 2048], replicated, may hold values from -0.1875 to 0.1875
- w_q: bfloat16 [1024, 1024], replicated, may hold values from -0.1875 to 0.1875
- src_gain: float32 [1024], replicated, may hold values from 0.1 to 1.9
- q_gain: float32 [1024], replicated, may hold values from 0.5 to 40
- src_index: int32 [256, 12], P('band'), may hold values from 0 to 1023, as said below
- edge_mask: int32 [256, 12], P('band'), may hold values from 0 to 1, as said below
Outputs:
- updated: bfloat16 [4, 256, 1024], P('ens', 'band')
- d_grid: bfloat16 [4, 1024, 1024], P('ens', 'band')
- d_wkv_t: float32 [2048, 1024], P(('band', 'ens'))
Inputs may be any that keep to these rules, and one draw needn't show every extreme that they name: `src_index`: every edge slot of hidden node h names a grid row from max(0, (h // 32) * 128 - 32) to min(1024, (h // 32 + 1) * 128 + 32) - 1, and in every band both ends of that range are named by a valid edge. `edge_mask`: the first slot of every hidden node is valid.
All inputs are finite; a program needn't handle non-finite values.
Results may differ from a plain program's by a relative error of at most 0.013.
The roundings to bfloat16 on the way count: a program that leaves them out, or rounds other values in their place, can miss the bound.
Values may be sent and summed in bfloat16 or wider, within the bound.
No kernel may reach another device: no remote copies, remote signals or barrier semaphores. Data moves between devices by JAX's collectives and lax.ppermute only.
A program may use at most 128 MiB of HBM per device.

v0:
```python
import math

import jax
import jax.numpy as jnp
from jax import lax
from jax.sharding import PartitionSpec as P

HEADS = 16
K = 12
R = 32


EPSILON = 1e-05


def extended(cells, sides, width):
    for axis, dim in sides:
        count = lax.axis_size(axis)
        ends = count - 1
        head = lax.slice_in_dim(cells, 0, width, axis=dim)
        tail = lax.slice_in_dim(cells, cells.shape[dim] - width, cells.shape[dim], axis=dim)
        cells = jnp.concatenate(
            [
                lax.ppermute(tail, axis, [(i, (i + 1) % count) for i in range(ends)]),
                cells,
                lax.ppermute(head, axis, [((i + 1) % count, i) for i in range(ends)]),
            ],
            axis=dim,
        )
    return cells


def passed_along(value, axis, by):
    peers = lax.axis_size(axis)
    pairs = [(i, i + by) for i in range(peers) if 0 <= i + by < peers]
    return lax.ppermute(value, axis, pairs)


def normalize(values):
    values = values.astype(jnp.float32)
    average = jnp.mean(values, axis=-1, keepdims=True)
    centred = values - average
    variance = jnp.mean(centred * centred, axis=-1, keepdims=True)
    inv_std = lax.rsqrt(variance + EPSILON)
    return (centred * inv_std, inv_std)


def times_transposed(left, right):
    return lax.dot_general(
        left, right, (((1,), (1,)), ((), ())), preferred_element_type=jnp.float32
    )


def rows_product(partial_rows, normed_rows):
    return lax.dot_general(
        partial_rows, normed_rows, (((0,), (0,)), ((), ())), preferred_element_type=jnp.float32
    )


def node_block(queries, hidden_rows, cotangent, kv_window, local_rows, valid_edges):
    node_count, features = queries.shape
    head_dim = features // HEADS
    score_scale = 1.0 / math.sqrt(head_dim)
    gathered = kv_window[local_rows]
    key_rows = gathered[..., :features].reshape(node_count, K, HEADS, head_dim)
    value_rows = gathered[..., features:].reshape(node_count, K, HEADS, head_dim)
    query_heads = queries.reshape(node_count, HEADS, head_dim)
    scores = (
        jnp.einsum("hnd,hknd->hkn", query_heads, key_rows, preferred_element_type=jnp.float32)
        * score_scale
    )
    valid = valid_edges[:, :, None] > 0
    shifted = jnp.where(valid, scores, -jnp.inf)
    row_max = jnp.max(shifted, axis=1, keepdims=True)
    exp_terms = jnp.exp(shifted - row_max)
    attn_probs = exp_terms / jnp.sum(exp_terms, axis=1, keepdims=True)
    probs_low = attn_probs.astype(jnp.bfloat16)
    attended = jnp.einsum(
        "hkn,hknd->hnd", probs_low, value_rows, preferred_element_type=jnp.float32
    )
    attended = attended.reshape(node_count, features)
    updated = (hidden_rows.astype(jnp.float32) + attended).astype(jnp.bfloat16)
    d_heads = cotangent.reshape(node_count, HEADS, head_dim)
    d_probs = jnp.einsum("hnd,hknd->hkn", d_heads, value_rows, preferred_element_type=jnp.float32)
    d_scores = attn_probs * (d_probs - jnp.sum(attn_probs * d_probs, axis=1, keepdims=True))
    d_keys = d_scores[..., None] * query_heads.astype(jnp.float32)[:, None] * score_scale
    d_values = probs_low.astype(jnp.float32)[..., None] * d_heads.astype(jnp.float32)[:, None]
    edge_grads = jnp.concatenate(
        [d_keys.reshape(node_count * K, features), d_values.reshape(node_count * K, features)],
        axis=1,
    )
    partial_value = (
        jnp.zeros((kv_window.shape[0], 2 * features), jnp.float32)
        .at[local_rows.reshape(-1)]
        .add(edge_grads)
    )
    return (updated, partial_value.astype(jnp.bfloat16))


def per_device(grid_latent, hidden, d_updated, w_kv, w_q, src_gain, q_gain, src_index, edge_mask):
    grid_rows = grid_latent.shape[1]
    standard, inv_std = normalize(grid_latent[0])
    normed = (standard * src_gain).astype(jnp.bfloat16)
    normed_window = extended(normed, (("band", 0),), R)
    kv_window = jnp.dot(normed_window, w_kv, preferred_element_type=jnp.float32).astype(
        jnp.bfloat16
    )
    hidden_hat, _ = normalize(hidden[0])
    hidden_normed = (hidden_hat * q_gain).astype(jnp.bfloat16)
    queries = jnp.dot(hidden_normed, w_q, preferred_element_type=jnp.float32).astype(jnp.bfloat16)
    offset = lax.axis_index("band") * grid_rows - R
    local_rows = src_index - offset
    updated, partial_value = node_block(
        queries, hidden[0], d_updated[0], kv_window, local_rows, edge_mask
    )
    factor = 1.0 / math.sqrt(lax.axis_size("ens") * grid_rows * lax.axis_size("band"))
    d_window = times_transposed(partial_value, w_kv)
    back_low = passed_along(d_window[:R].astype(jnp.bfloat16), "band", -1).astype(jnp.float32)
    back_high = passed_along(d_window[grid_rows + R :].astype(jnp.bfloat16), "band", 1).astype(
        jnp.float32
    )
    d_normed = d_window[R : R + grid_rows]
    d_normed = d_normed.at[:R].add(back_high)
    d_normed = d_normed.at[grid_rows - R :].add(back_low)
    d_wkv_t = lax.psum_scatter(
        rows_product(partial_value, normed_window) * factor,
        ("band", "ens"),
        scatter_dimension=0,
        tiled=True,
    )
    d_scaled = d_normed * src_gain
    d_grid = inv_std * (
        d_scaled
        - jnp.mean(d_scaled, axis=-1, keepdims=True)
        - standard * jnp.mean(d_scaled * standard, axis=-1, keepdims=True)
    )
    return (updated[None], d_grid.astype(jnp.bfloat16)[None], d_wkv_t)


def solution(mesh):
    return jax.shard_map(
        per_device,
        mesh=mesh,
        in_specs=(
            P("ens", "band", None),
            P("ens", "band", None),
            P("ens", "band", None),
            P(),
            P(),
            P(),
            P(),
            P("band", None),
            P("band", None),
        ),
        out_specs=(P("ens", "band", None), P("ens", "band", None), P(("band", "ens"), None)),
        check_vma=False,
    )
```

profile of v0, /device:TPU:0, one launch (start us, length us, event | category | flops | bytes accessed | tf_op | source)
XLA Modules:
  0.0 235.9 jit_solution(13413299441816603047)
XLA Ops:
  7.2 0.0 copy-start
  7.2 0.0 copy-start.5
  7.2 0.0 reduce-scatter.2.cloned.1.call-start
  7.2 1.2 convert_reduce_fusion
  8.5 1.2 fusion.22
  9.6 0.0 copy-start.12
  9.6 0.0 copy-start.11
  9.7 1.2 fusion.17
  10.9 4.9 %collective-permute-start = (bf16[32,1024]{1,0:T(8,128)(2,1)S(1)}, bf16[32,1024]{1,0:T(8,128)(2,1)S(1)}, u32[]{:S(2)}, u32[]{:S(2)}) collective-permute-start(bf16[32,1024]{1,0:T(8,128)(2,1)S(1)} %get-tuple-element.35), channel_id=1, source_target_pairs={{0,4},{4,8},{8,12},{12,16},{16,20},{20,24},{24,28},{1,5},{5,9},{9,... | collective-permute-start | bytes 196616 | tf_op jit(solution)/shard_map/ppermute | solution.py:24
  15.8 1.3 collective-permute-start.1
  17.1 1.0 convert_reduce_fusion.1
  18.0 1.0 fusion.30
  19.1 0.0 copy-done
  19.1 1.4 convolution_convert_fusion.1
  20.4 0.1 reshape.163
  20.6 0.9 reshape.193
  21.5 0.0 copy-done.5
  21.5 0.1 reshape_squeeze.3
  21.6 0.9 reshape.196
  22.5 0.0 copy-done.12
  22.5 0.1 copy.22
  22.6 0.1 reshape.169
  22.7 0.1 copy.25
  22.8 0.1 reshape.166
  22.9 0.7 convert_element_type.74
  23.7 0.7 convert_element_type.76
  24.4 0.0 collective-permute-done
  24.4 0.0 copy-start.6
  24.4 0.0 collective-permute-done.1
  24.4 0.0 copy-start.8
  24.4 3.2 %convolution_convert_fusion = bf16[192,2048]{1,0:T(8,128)(2,1)S(1)} fusion(bf16[1024,2048]{1,0:T(8,128)(2,1)} %param.16, bf16[32,1024]{1,0:T(8,128)(2,1)S(1)} %collective-permute-done.1, bf16[128,1024]{1,0:T(8,128)(2,1)S(1)} %fusion.17, bf16[32,1024]{1,0:T(8,128)(2,1)S(1)} %collective-permute-done), kind=kOutput, calls=%fused_computation.8 | convolution fusion | flops 806879232 | bytes 5373952 | tf_op jit(solution)/shard_map/dot_general | solution.py:105
  27.7 3.1 %gather_fusion = bf16[384,2048]{1,0:T(8,128)(2,1)} fusion(bf16[192,2048]{1,0:T(8,128)(2,1)S(1)} %convolution_convert_fusion, s32[1024]{0:T(1024)S(1)} %pad_clamp_fusion), kind=kCustom, calls=%fused_computation | custom fusion | bytes 3147264 | tf_op jit(solution)/shard_map/gather | solution.py:64
  30.8 3.6 %reshape.168 = bf16[32,12,2048]{2,1,0:T(8,128)(2,1)} reshape(bf16[384,2048]{1,0:T(8,128)(2,1)} %gather_fusion) | data formatting | bytes 3145728 | tf_op jit(solution)/shard_map/gather | solution.py:64
  34.4 2.8 %fusion.49 = (bf16[32,12,1024]{2,1,0:T(8,128)(2,1)}, bf16[32,12,1024]{2,1,0:T(8,128)(2,1)S(1)}) fusion(bf16[32,12,2048]{2,1,0:T(8,128)(2,1)} %reshape.168), kind=kLoop, calls=%fused_computation.82 | loop fusion | bytes 3145728 | tf_op jit(solution)/shard_map/slice | solution.py:66
  37.1 3.6 %reshape.194 = bf16[32,12,16,64]{3,2,1,0:T(8,128)(2,1)} reshape(bf16[32,12,1024]{2,1,0:T(8,128)(2,1)} %get-tuple-element.31) | data formatting | bytes 1572864 | tf_op jit(solution)/shard_map/reshape | solution.py:66
  40.8 3.3 %fusion.4 = f32[32,16,1,12]{3,2,1,0:T(1,128)} fusion(bf16[32,16,64,1]{2,3,1,0:T(2,128)(2,1)} %reshape.196, bf16[32,12,16,64]{3,2,1,0:T(8,128)(2,1)} %reshape.194), kind=kOutput, calls=%fused_computation.9 | convolution fusion | flops 786432 | bytes 876544 | tf_op jit(solution)/shard_map/hnd,hknd->hkn/dot_general | solution.py:84
  44.1 1.1 copy.35
  45.2 2.0 reshape.191
  47.2 2.6 %fusion.8 = f32[32,16,1,12]{3,2,1,0:T(1,128)S(1)} fusion(bf16[32,16,64,1]{2,3,1,0:T(2,128)(2,1)} %reshape.193, bf16[32,12,16,64]{3,2,1,0:T(8,128)(2,1)} %reshape.191), kind=kOutput, calls=%fused_computation.13 | convolution fusion | flops 786432 | bytes 876544 | tf_op jit(solution)/shard_map/hnd,hknd->hkn/dot_general | solution.py:69
  49.8 0.2 copy.30
  50.2 0.2 copy.26
  50.4 0.2 copy.27
  50.6 2.2 broadcast_multiply_fusion
  52.7 3.8 %mul.149 = f32[384,1024]{1,0:T(8,128)} reshape(f32[32,12,16,64]{3,2,1,0:T(8,128)} %broadcast_multiply_fusion) | data formatting | bytes 3145728 | tf_op jit(solution)/shard_map/mul | solution.py:87
  56.5 2.1 multiply_multiply_fusion
  58.6 3.7 %mul.145 = f32[384,1024]{1,0:T(8,128)} reshape(f32[32,12,16,64]{3,2,1,0:T(8,128)} %multiply_multiply_fusion) | data formatting | bytes 3145728 | tf_op jit(solution)/shard_map/mul | solution.py:86
  62.3 8.2 %scatter_custom_fusion = f32[192,2048]{1,0:T(8,128)} fusion(s32[384]{0:T(512)S(1)} %fusion.46, f32[384,1024]{1,0:T(8,128)} %mul.149, f32[]{:T(128)} %constant.92.clone.1, f32[384,1024]{1,0:T(8,128)} %mul.145, f32[]{:T(128)} %constant.83.clone.1), kind=kCustom, calls=%fused_computation.3 | custom fusion | flops 1572864 | bytes 4718600 | tf_op jit(solution)/shard_map/scatter-add | solution.py:95
  70.5 5.9 %convolution_multiply_fusion = f32[2048,1024]{1,0:T(8,128)} fusion(f32[192,2048]{1,0:T(8,128)} %scatter_custom_fusion, bf16[32,1024]{1,0:T(8,128)(2,1)S(1)} %copy-done.9, bf16[128,1024]{1,0:T(8,128)(2,1)S(1)} %fusion.17, bf16[32,1024]{1,0:T(8,128)(2,1)S(1)} %copy-done.7), kind=kOutput, calls=%fused_computation.2 | convolution fusion | flops 808976384 | bytes 10354688 | tf_op jit(solution)/shard_map/dot_general | solution.py:55
  76.4 0.0 reduce-scatter.2.cloned.1.call-update
  76.5 0.4 copy.31
  76.9 2.1 fusion.6
  79.0 0.1 reshape.165
  79.1 0.0 copy-start.4
  79.2 4.2 %fusion.52 = (bf16[192,1024]{1,0:T(8,128)(2,1)S(1)}, f32[192,1024]{1,0:T(8,128)S(1)}) fusion(bf16[1024,2048]{1,0:T(8,128)(2,1)} %param.16, f32[192,2048]{1,0:T(8,128)} %scatter_custom_fusion), kind=kOutput, calls=%fused_computation.85 | convolution fusion | flops 805896192 | bytes 6946816 | tf_op jit(solution)/shard_map/dot_general | solution.py:49
  83.4 0.0 copy-start.1
  83.4 0.0 copy-start.10
  83.4 4.7 %collective-permute-start.2 = (bf16[32,1024]{1,0:T(8,128)(2,1)S(1)}, bf16[32,1024]{1,0:T(8,128)(2,1)S(1)}, u32[]{:S(2)}, u32[]{:S(2)}) collective-permute-start(bf16[32,1024]{1,0:T(8,128)(2,1)S(1)} %get-tuple-element.34), channel_id=1, source_target_pairs={{0,4},{4,8},{8,12},{12,16},{16,20},{20,24},{24,28},{1,5},{5,9},{9,... | collective-permute-start | bytes 196616 | tf_op jit(solution)/shard_map/ppermute | solution.py:36
  88.1 0.6 fusion.33
  88.8 1.3 collective-permute-start.3
  90.1 0.0 collective-permute-done.2
  90.2 5.9 %collective-permute-done.3 = bf16[32,1024]{1,0:T(8,128)(2,1)S(1)} collective-permute-done((bf16[32,1024]{1,0:T(8,128)(2,1)S(1)}, bf16[32,1024]{1,0:T(8,128)(2,1)S(1)}, u32[]{:S(2)}, u32[]{:S(2)}) %collective-permute-start.3) | collective-permute-done | bytes 65568 | tf_op jit(solution)/shard_map/ppermute | solution.py:36
  96.1 0.2 multiply_reduce_fusion
  96.3 0.9 fusion.26
  97.2 131.8 %reduce-scatter.2.cloned.1.call-done = f32[64,1024]{1,0:T(8,128)} async-done(((f32[2048,1024]{1,0:T(8,128)}), f32[64,1024]{1,0:T(8,128)}) %reduce-scatter.2.cloned.1.call-update) | async-done | bytes 262160 | tf_op jit(solution)/shard_map/reduce_scatter | solution.py:125
  (32 shorter events, 0.4 us)
Async XLA Ops:
  7.2 11.9 %copy-start = (bf16[1024,1024]{1,0:T(8,128)(2,1)S(1)}, bf16[1024,1024]{1,0:T(8,128)(2,1)}, u32[]{:S(2)}) copy-start(bf16[1024,1024]{1,0:T(8,128)(2,1)} %param.17) | copy-start | bytes 6291460
  7.2 14.3 %copy-start.5 = (bf16[1,32,1024]{2,1,0:T(8,128)(2,1)S(1)}, bf16[1,32,1024]{2,1,0:T(8,128)(2,1)}, u32[]{:S(2)}) copy-start(bf16[1,32,1024]{2,1,0:T(8,128)(2,1)} %param.15) | copy-start | bytes 196612
  7.2 221.9 %reduce-scatter.2.cloned.1.call-start = ((), (), s32[]{:S(2)}) async-start(), calls=%async_computation.1 | async-start | bytes 8650752 | tf_op jit(solution)/shard_map/reduce_scatter | solution.py:125
  9.6 12.9 %copy-start.12 = (s32[32,12]{0,1:T(8,128)S(1)}, s32[32,12]{0,1:T(8,128)}, u32[]{:S(2)}) copy-start(s32[32,12]{0,1:T(8,128)} %param.21) | copy-start | bytes 4612
  9.6 12.9 %copy-start.11 = (s32[32,12]{0,1:T(8,128)S(1)}, s32[32,12]{0,1:T(8,128)}, u32[]{:S(2)}) copy-start(s32[32,12]{0,1:T(8,128)} %param.20) | copy-start | bytes 4612
  10.9 13.5 %collective-permute-start = (bf16[32,1024]{1,0:T(8,128)(2,1)S(1)}, bf16[32,1024]{1,0:T(8,128)(2,1)S(1)}, u32[]{:S(2)}, u32[]{:S(2)}) collective-permute-start(bf16[32,1024]{1,0:T(8,128)(2,1)S(1)} %get-tuple-element.35), channel_id=1, source_target_pairs={{0,4},{4,8},{8,12},{12,16},{16,20},{20,24},{24,28},{1,5},{5,9},{9,... | collective-permute-start | bytes 196616 | tf_op jit(solution)/shard_map/ppermute | solution.py:24
  15.8 8.7 %collective-permute-start.1 = (bf16[32,1024]{1,0:T(8,128)(2,1)S(1)}, bf16[32,1024]{1,0:T(8,128)(2,1)S(1)}, u32[]{:S(2)}, u32[]{:S(2)}) collective-permute-start(bf16[32,1024]{1,0:T(8,128)(2,1)S(1)} %get-tuple-element.36), channel_id=1, source_target_pairs={{4,0},{8,4},{12,8},{16,12},{20,16},{24,20},{28,24},{5,1},{9,5},{13... | collective-permute-start | bytes 196616 | tf_op jit(solution)/shard_map/ppermute | solution.py:26
  24.4 3.2 %copy-start.6 = (bf16[32,1024]{1,0:T(8,128)(2,1)}, bf16[32,1024]{1,0:T(8,128)(2,1)S(1)}, u32[]{:S(2)}) copy-start(bf16[32,1024]{1,0:T(8,128)(2,1)S(1)} %collective-permute-done) | copy-start | bytes 196612
  24.4 3.2 %copy-start.8 = (bf16[32,1024]{1,0:T(8,128)(2,1)}, bf16[32,1024]{1,0:T(8,128)(2,1)S(1)}, u32[]{:S(2)}) copy-start(bf16[32,1024]{1,0:T(8,128)(2,1)S(1)} %collective-permute-done.1) | copy-start | bytes 196612
  47.2 3.4 %copy-start.3 = (f32[32,16,64]{2,1,0:T(8,128)S(1)}, f32[32,16,64]{2,1,0:T(8,128)}, u32[]{:S(2)}) copy-start(f32[32,16,64]{2,1,0:T(8,128)} %convert_element_type.76) | copy-start | bytes 393220
  52.7 3.8 %copy-start.2 = (f32[32,16,64]{2,1,0:T(8,128)S(1)}, f32[32,16,64]{2,1,0:T(8,128)}, u32[]{:S(2)}) copy-start(f32[32,16,64]{2,1,0:T(8,128)} %convert_element_type.74) | copy-start | bytes 393220
  62.3 8.2 %copy-start.7 = (bf16[32,1024]{1,0:T(8,128)(2,1)S(1)}, bf16[32,1024]{1,0:T(8,128)(2,1)}, u32[]{:S(2)}) copy-start(bf16[32,1024]{1,0:T(8,128)(2,1)} %copy-done.6) | copy-start | bytes 196612
  62.3 8.2 %copy-start.9 = (bf16[32,1024]{1,0:T(8,128)(2,1)S(1)}, bf16[32,1024]{1,0:T(8,128)(2,1)}, u32[]{:S(2)}) copy-start(bf16[32,1024]{1,0:T(8,128)(2,1)} %copy-done.8) | copy-start | bytes 196612
  79.1 9.0 %copy-start.4 = (bf16[1,32,1024]{2,1,0:T(8,128)(2,1)S(1)}, bf16[1,32,1024]{2,1,0:T(8,128)(2,1)}, u32[]{:S(2)}) copy-start(bf16[1,32,1024]{2,1,0:T(8,128)(2,1)} %param.14) | copy-start | bytes 196612
  83.4 12.7 %copy-start.1 = (bf16[1,128,1024]{2,1,0:T(8,128)(2,1)S(1)}, bf16[1,128,1024]{2,1,0:T(8,128)(2,1)}, u32[]{:S(2)}) copy-start(bf16[1,128,1024]{2,1,0:T(8,128)(2,1)} %param.13) | copy-start | bytes 786436
  83.4 12.7 %copy-start.10 = (f32[1024]{0:T(1024)S(1)}, f32[1024]{0:T(1024)}, u32[]{:S(2)}) copy-start(f32[1024]{0:T(1024)} %param.18) | copy-start | bytes 12292
  83.4 6.7 %collective-permute-start.2 = (bf16[32,1024]{1,0:T(8,128)(2,1)S(1)}, bf16[32,1024]{1,0:T(8,128)(2,1)S(1)}, u32[]{:S(2)}, u32[]{:S(2)}) collective-permute-start(bf16[32,1024]{1,0:T(8,128)(2,1)S(1)} %get-tuple-element.34), channel_id=1, source_target_pairs={{0,4},{4,8},{8,12},{12,16},{16,20},{20,24},{24,28},{1,5},{5,9},{9,... | collective-permute-start | bytes 196616 | tf_op jit(solution)/shard_map/ppermute | solution.py:36
  88.8 7.2 %collective-permute-start.3 = (bf16[32,1024]{1,0:T(8,128)(2,1)S(1)}, bf16[32,1024]{1,0:T(8,128)(2,1)S(1)}, u32[]{:S(2)}, u32[]{:S(2)}) collective-permute-start(bf16[32,1024]{1,0:T(8,128)(2,1)S(1)} %get-tuple-element.33), channel_id=1, source_target_pairs={{4,0},{8,4},{12,8},{16,12},{20,16},{24,20},{28,24},{5,1},{9,5},{13... | collective-permute-start | bytes 196616 | tf_op jit(solution)/shard_map/ppermute | solution.py:36
Sparse Core Ops, SparseCore 0:
  76.6 152.4 reduce-scatter.1
where the time goes:
time: 237 us; the launch traced here: 236 us
  waiting for transfers between devices  138 us (58%)
  local copies, waits for them, and re-layouts  27.3 us (12%)
  matrix products  22.8 us (10%)
  other arithmetic  21.6 us (9%)
  between operations  14.4 us (6%)
  starting transfers between devices  12.2 us (5%)
    reduce_scatter x1, waiting for transfers between devices, per_device(): lax.psum_scatter(rows_product(partial_value, normed_window) * factor, ('b...  132 us
    scatter-add x1, other arithmetic, node_block(): partial_value = jnp.zeros((kv_window.shape[0], 2 * features), jnp.float32...  8.17 us
    gather x2, local copies, waits for them, and re-layouts, node_block(): gathered = kv_window[local_rows]  6.71 us
    ppermute x2, starting transfers between devices, passed_along(): return lax.ppermute(value, axis, pairs)  5.97 us
    dot_general x1, matrix products, rows_product(): lax.dot_general(partial_rows, normed_rows, (((0,), (0,)), ((), ())), pref...  5.92 us
    ppermute x2, waiting for transfers between devices, passed_along(): return lax.ppermute(value, axis, pairs)  5.87 us
    ppermute x1, starting transfers between devices, extended(): lax.ppermute(tail, axis, [(i, (i + 1) % count) for i in range(ends)])  4.87 us
  transfers between devices with their start and end apart: 5, of which 2 were waited for; matrix products, arithmetic and copies ran while one was open for 7% of the time, Pallas kernels for 0%

commit v1 on v0

v1 whole, which is shorter than its diff:
```python
import functools
import math

import jax
import jax.numpy as jnp
from jax import lax
from jax.experimental import pallas as pl
from jax.experimental.pallas import tpu as pltpu
from jax.sharding import PartitionSpec as P

HEADS = 16
K = 12
R = 32
EPSILON = 1e-05
F32 = jnp.float32
BF16 = jnp.bfloat16


def spec(space=pltpu.VMEM):
    return pl.BlockSpec(memory_space=space)


def estimate(flops, moved):
    return pl.CostEstimate(flops=int(flops), bytes_accessed=int(moved), transcendentals=0)


def dot(left, right):
    return jnp.dot(left, right, preferred_element_type=F32)


def dot_rows(left, right):
    return lax.dot_general(left, right, (((0,), (0,)), ((), ())), preferred_element_type=F32)


def dot_lanes(left, right):
    return lax.dot_general(left, right, (((1,), (1,)), ((), ())), preferred_element_type=F32)


def halves(wide):
    high = wide.astype(BF16)
    return high, (wide - high.astype(F32)).astype(BF16)


def normalize(values):
    values = values.astype(F32)
    average = jnp.mean(values, axis=-1, keepdims=True)
    centred = values - average
    variance = jnp.mean(centred * centred, axis=-1, keepdims=True)
    inv_std = lax.rsqrt(variance + EPSILON)
    return centred * inv_std, inv_std


def norm_kernel(grid_ref, gain_ref, normed_ref):
    standard, _ = normalize(grid_ref[...])
    normed_ref[...] = (standard * gain_ref[...]).astype(BF16)


def project_kernel(hidden_ref, gain_ref, wq_ref, normed_ref, wkv_ref, q_ref, kv_ref, hat_ref):
    @pl.when(pl.program_id(0) == 0)
    def _():
        standard, _ = normalize(hidden_ref[...])
        hat_ref[...] = (standard * gain_ref[...]).astype(BF16)

    q_ref[...] = dot(hat_ref[...], wq_ref[...]).astype(BF16)
    kv_ref[...] = dot(normed_ref[...], wkv_ref[...]).astype(BF16)


def attend_kernel(
    groups, block, where_ref, low_ref, high_ref, wkv_ref, kv_ref, q_ref, cot_ref, hidden_ref,
    index_ref, mask_ref, *refs
):
    updated_ref, partial_ref = refs[:2]
    piece_refs = refs[2:-2]
    window_ref, pieces_ref = refs[-2:]
    nodes, features = q_ref.shape
    own = kv_ref.shape[0]
    rows = own + 2 * R
    lanes = 128
    head_dim = features // HEADS
    shift = head_dim.bit_length() - 1
    scale = 1.0 / math.sqrt(head_dim)
    window_ref[:R] = dot(low_ref[...], wkv_ref[...]).astype(BF16)
    window_ref[R : R + own] = kv_ref[...]
    window_ref[R + own :] = dot(high_ref[...], wkv_ref[...]).astype(BF16)

    local = index_ref[...] - where_ref[0]
    row_id = lax.broadcasted_iota(jnp.int32, (nodes, rows), 1)
    picks = jnp.concatenate(
        [jnp.where(row_id == local[:, k : k + 1], 1.0, 0.0).astype(BF16) for k in range(K)], axis=0
    )
    valid = jnp.concatenate([mask_ref[:, k : k + 1] for k in range(K)], axis=0) > 0
    chunk = 256
    feature_id = lax.broadcasted_iota(jnp.int32, (features, lanes), 0)
    lane_id = lax.broadcasted_iota(jnp.int32, (features, lanes), 1)
    to_heads = jnp.where(jnp.right_shift(feature_id, shift) == lane_id, 1.0, 0.0).astype(BF16)
    lane_t = lax.broadcasted_iota(jnp.int32, (lanes, features), 0)
    feature_t = lax.broadcasted_iota(jnp.int32, (lanes, features), 1)
    from_heads = jnp.where(jnp.right_shift(feature_t, shift) == lane_t, 1.0, 0.0).astype(BF16)

    def repeated(ref, c):
        return jnp.broadcast_to(ref[:, c : c + chunk].astype(F32)[None], (K, nodes, chunk))

    def by_edge(ref, c, start):
        edge = dot(picks, window_ref[:, start + c : start + c + chunk])
        product = edge.reshape(K, nodes, chunk) * repeated(ref, c)
        first, second = halves(product.reshape(K * nodes, chunk))
        heads = to_heads[c : c + chunk]
        return dot(first, heads) + dot(second, heads)

    scores = by_edge(q_ref, 0, 0)
    d_probs = by_edge(cot_ref, 0, features)
    for c in range(chunk, features, chunk):
        scores = scores + by_edge(q_ref, c, 0)
        d_probs = d_probs + by_edge(cot_ref, c, features)
    scores = jnp.where(valid, scores * scale, -jnp.inf).reshape(K, nodes, lanes)
    d_probs = d_probs.reshape(K, nodes, lanes)
    terms = jnp.exp(scores - jnp.max(scores, axis=0, keepdims=True))
    probs = terms / jnp.sum(terms, axis=0, keepdims=True)
    probs_low = probs.reshape(K * nodes, lanes).astype(BF16)
    inner = jnp.sum(probs * d_probs, axis=0, keepdims=True)
    d_scores = (probs * (d_probs - inner)).reshape(K * nodes, lanes)
    d_first, d_second = halves(d_scores)

    for c in range(0, features, chunk):
        heads = from_heads[:, c : c + chunk]
        spread = dot(probs_low, heads).reshape(K, nodes, chunk)
        values = dot(picks, window_ref[:, features + c : features + c + chunk])
        attended = jnp.sum(spread * values.reshape(K, nodes, chunk), axis=0)
        updated_ref[:, c : c + chunk] = (
            hidden_ref[:, c : c + chunk].astype(F32) + attended
        ).astype(BF16)
        first, second = halves((spread * repeated(cot_ref, c)).reshape(K * nodes, chunk))
        partial_ref[:, features + c : features + c + chunk] = (
            dot_rows(picks, first) + dot_rows(picks, second)
        ).astype(BF16)
        spread = (dot(d_first, heads) + dot(d_second, heads)).reshape(K, nodes, chunk)
        keys = (spread * repeated(q_ref, c)).reshape(K * nodes, chunk) * scale
        first, second = halves(keys)
        partial_ref[:, c : c + chunk] = (
            dot_rows(picks, first) + dot_rows(picks, second)
        ).astype(BF16)

    if piece_refs:
        left = lax.broadcasted_iota(jnp.int32, (rows, lanes), 1) < block
        for g in range(groups):
            for i in range(2 * features // (groups * lanes)):
                at = (2 * i * groups + g) * block
                a = at // lanes * lanes
                b = (at + groups * block) // lanes * lanes
                one = partial_ref[:, a : a + lanes].astype(F32)
                two = partial_ref[:, b : b + lanes].astype(F32)
                if at % lanes == 0:
                    two = pltpu.roll(two, block, 1)
                else:
                    one = pltpu.roll(one, block, 1)
                pieces_ref[g, :, i * lanes : (i + 1) * lanes] = jnp.where(left, one, two).astype(BF16)
        for k, piece_ref in enumerate(piece_refs):
            piece_ref[...] = pieces_ref[where_ref[1] ^ k]


def window_kernel(partial_ref, wkv_ref, own_ref, low_ref, high_ref):
    wide = dot_lanes(partial_ref[...], wkv_ref[...])
    rows = wide.shape[0]
    low_ref[...] = wide[:R].astype(BF16)
    own_ref[...] = wide[R : rows - R]
    high_ref[...] = wide[rows - R :].astype(BF16)


def product_kernel(groups, factor, where_ref, *refs):
    left_refs, right_refs = refs[:groups], refs[groups : 2 * groups]
    out_refs, total_ref = refs[2 * groups : -1], refs[-1]
    total = dot_rows(left_refs[0][...], right_refs[0][...])
    for left_ref, right_ref in zip(left_refs[1:], right_refs[1:]):
        total = total + dot_rows(left_ref[...], right_ref[...])
    total_ref[...] = total * factor
    block = out_refs[0].shape[0]
    for k, out_ref in enumerate(out_refs):
        start = pl.multiple_of((where_ref[2] ^ k) * block, block)
        out_ref[...] = total_ref[pl.ds(start, block)].astype(out_ref.dtype)


def finish_kernel(grid_ref, gain_ref, own_ref, low_ref, high_ref, out_ref, wide_ref):
    rows = own_ref.shape[0]
    wide_ref[...] = own_ref[...]
    wide_ref[:R] = wide_ref[:R] + low_ref[...].astype(F32)
    wide_ref[rows - R :] = wide_ref[rows - R :] + high_ref[...].astype(F32)
    standard, inv_std = normalize(grid_ref[...])
    scaled = wide_ref[...] * gain_ref[...]
    out_ref[...] = (
        inv_std
        * (
            scaled
            - jnp.mean(scaled, axis=-1, keepdims=True)
            - standard * jnp.mean(scaled * standard, axis=-1, keepdims=True)
        )
    ).astype(BF16)


def total_kernel(*refs):
    total = refs[0][...]
    for ref in refs[1:-1]:
        total = total + ref[...].astype(F32)
    refs[-1][...] = total


def swapped(value, axis, by):
    count = lax.axis_size(axis)
    return lax.ppermute(value, axis, [(i, i ^ by) for i in range(count)])


def passed_along(value, axis, by):
    peers = lax.axis_size(axis)
    pairs = [(i, i + by) for i in range(peers) if 0 <= i + by < peers]
    return lax.ppermute(value, axis, pairs)


def is_power(count):
    return count & (count - 1) == 0


def per_device(grid_latent, hidden, d_updated, w_kv, w_q, src_gain, q_gain, src_index, edge_mask):
    grid_latent, hidden, d_updated = grid_latent[0], hidden[0], d_updated[0]
    rows, features = grid_latent.shape
    nodes = hidden.shape[0]
    bands, members = lax.axis_size("band"), lax.axis_size("ens")
    band, member = lax.axis_index("band"), lax.axis_index("ens")
    window = rows + 2 * R
    block = 2 * features // (bands * members)
    src_gain, q_gain = src_gain[None], q_gain[None]
    where = jnp.stack([band * rows - R, member, band]).astype(jnp.int32)
    grouped = is_power(members) and is_power(bands) and bands <= 8 and block == 64 and members % 2 == 0

    normed = pl.pallas_call(
        norm_kernel,
        out_shape=jax.ShapeDtypeStruct((rows, features), BF16),
        in_specs=[spec()] * 2,
        out_specs=spec(),
        cost_estimate=estimate(10 * rows * features, 4 * rows * features),
        name="norm",
    )(grid_latent, src_gain)
    low = passed_along(normed[rows - R :], "band", 1)
    high = passed_along(normed[:R], "band", -1)

    steps = 4
    wide_q, wide_kv = features // steps, 2 * features // steps
    queries, kv = pl.pallas_call(
        project_kernel,
        grid=(steps,),
        out_shape=(
            jax.ShapeDtypeStruct((nodes, features), BF16),
            jax.ShapeDtypeStruct((rows, 2 * features), BF16),
        ),
        in_specs=[
            pl.BlockSpec((nodes, features), lambda i: (0, 0)),
            pl.BlockSpec((1, features), lambda i: (0, 0)),
            pl.BlockSpec((features, wide_q), lambda i: (0, i)),
            pl.BlockSpec((rows, features), lambda i: (0, 0)),
            pl.BlockSpec((features, wide_kv), lambda i: (0, i)),
        ],
        out_specs=(
            pl.BlockSpec((nodes, wide_q), lambda i: (0, i)),
            pl.BlockSpec((rows, wide_kv), lambda i: (0, i)),
        ),
        scratch_shapes=[pltpu.VMEM((nodes, features), BF16)],
        cost_estimate=estimate(2 * (2 * rows + nodes) * features * features, 6 * features * features),
        name="project",
    )(hidden, q_gain, w_q, normed, w_kv)

    normed_window = jnp.concatenate([low, normed, high], axis=0)

    pieces = members if grouped else 0
    columns = 2 * features // members
    outs = pl.pallas_call(
        functools.partial(attend_kernel, members, block),
        out_shape=[
            jax.ShapeDtypeStruct((nodes, features), BF16),
            jax.ShapeDtypeStruct((window, 2 * features), BF16),
        ]
        + [jax.ShapeDtypeStruct((window, columns), BF16)] * pieces,
        in_specs=[spec(pltpu.SMEM)] + [spec()] * 9,
        out_specs=[spec()] * (2 + pieces),
        scratch_shapes=[
            pltpu.VMEM((window, 2 * features), BF16),
            pltpu.VMEM((members, window, columns), BF16),
        ],
        cost_estimate=estimate(3e9, 10 * features * features),
        name="attend",
    )(where, low, high, w_kv, kv, queries, d_updated, hidden, src_index, edge_mask)
    updated, partial_value = outs[:2]
    lefts = outs[2:]

    factor = 1.0 / math.sqrt(members * rows * bands)
    if grouped:
        lefts = [lefts[0]] + [swapped(lefts[k], "ens", k) for k in range(1, members)]
        rights = [normed_window] + [swapped(normed_window, "ens", k) for k in range(1, members)]

    d_own, d_low, d_high = pl.pallas_call(
        window_kernel,
        out_shape=(
            jax.ShapeDtypeStruct((rows, features), F32),
            jax.ShapeDtypeStruct((R, features), BF16),
            jax.ShapeDtypeStruct((R, features), BF16),
        ),
        in_specs=[spec()] * 2,
        out_specs=(spec(),) * 3,
        cost_estimate=estimate(4 * window * features * features, 6 * features * features),
        name="window",
    )(partial_value, w_kv)
    back_high = passed_along(d_low, "band", -1)
    back_low = passed_along(d_high, "band", 1)

    if grouped:
        parts = pl.pallas_call(
            functools.partial(product_kernel, members, factor),
            out_shape=[jax.ShapeDtypeStruct((block, features), F32)]
            + [jax.ShapeDtypeStruct((block, features), BF16)] * (bands - 1),
            in_specs=[spec(pltpu.SMEM)] + [spec()] * (2 * members),
            out_specs=[spec()] * bands,
            scratch_shapes=[pltpu.VMEM((columns, features), F32)],
            cost_estimate=estimate(2 * members * window * columns * features, 8 * features * features),
            name="product",
        )(where, *lefts, *rights)
        parts = [parts[0]] + [swapped(parts[k], "band", k) for k in range(1, bands)]
        d_wkv_t = pl.pallas_call(
            total_kernel,
            out_shape=jax.ShapeDtypeStruct((block, features), F32),
            in_specs=[spec()] * bands,
            out_specs=spec(),
            name="total",
        )(*parts)
    else:
        product = lax.dot_general(
            partial_value, normed_window, (((0,), (0,)), ((), ())), preferred_element_type=F32
        )
        d_wkv_t = lax.psum_scatter(
            product * factor, ("band", "ens"), scatter_dimension=0, tiled=True
        )

    d_grid = pl.pallas_call(
        finish_kernel,
        out_shape=jax.ShapeDtypeStruct((rows, features), BF16),
        in_specs=[spec()] * 5,
        out_specs=spec(),
        scratch_shapes=[pltpu.VMEM((rows, features), F32)],
        cost_estimate=estimate(20 * rows * features, 8 * rows * features),
        name="finish",
    )(grid_latent, src_gain, d_own, back_low, back_high)
    return (updated[None], d_grid[None], d_wkv_t)


def solution(mesh):
    return jax.shard_map(
        per_device,
        mesh=mesh,
        in_specs=(
            P("ens", "band", None),
            P("ens", "band", None),
            P("ens", "band", None),
            P(),
            P(),
            P(),
            P(),
            P("band", None),
            P("band", None),
        ),
        out_specs=(P("ens", "band", None), P("ens", "band", None), P(("band", "ens"), None)),
        check_vma=False,
    )
```

time: 237 us -> 106 us (0.45)
  the two profiles are of different devices: /device:TPU:0 before, /device:TPU:16 now
where the time goes in v1:
time: 106 us; the launch traced here: 105 us
  waiting for transfers between devices  41.1 us (39%)
  Pallas kernels  28.9 us (27%)
  starting transfers between devices  26.8 us (25%)
  local copies, waits for them, and re-layouts  5.94 us (6%)
  other arithmetic  1.56 us (1%)
    ppermute x13, waiting for transfers between devices, swapped(): return lax.ppermute(value, axis, [(i, i ^ by) for i in range(count)])  39.7 us
    ppermute x4, starting transfers between devices, passed_along(): return lax.ppermute(value, axis, pairs)  13.5 us
    ppermute x13, starting transfers between devices, swapped(): return lax.ppermute(value, axis, [(i, i ^ by) for i in range(count)])  13.3 us
    pallas_call x1, Pallas kernels, per_device(): pl.pallas_call(functools.partial(attend_kernel, members, block), out_shap...  8.54 us
    pallas_call x1, Pallas kernels, per_device(): pl.pallas_call(project_kernel, grid=(steps,), out_shape=(jax.ShapeDtypeSt...  5.32 us
    unnamed x50, local copies, waits for them, and re-layouts  5.06 us
    pallas_call x1, Pallas kernels, per_device(): pl.pallas_call(window_kernel, out_shape=(jax.ShapeDtypeStruct((rows, feat...  4.73 us
    pallas_call x1, Pallas kernels, per_device(): pl.pallas_call(functools.partial(product_kernel, members, factor), out_sh...  4.03 us
  transfers between devices with their start and end apart: 17, of which 7 were waited for; matrix products, arithmetic and copies ran while one was open for 4% of the time, Pallas kernels for 12%

profile of v1, /device:TPU:16, one launch (start us, length us, event | category | flops | bytes accessed | tf_op | source)
XLA Modules:
  0.0 105.1 jit_solution(18249872691216751283)
XLA Ops:
  0.6 1.9 %norm.1.normed_ref = bf16[128,1024]{1,0:T(8,128)(2,1)} custom-call(bf16[128,1024]{1,0:T(8,128)(2,1)} %bitcast.10, f32[1,1024]{1,0:T(1,128)} %bitcast.15), custom_call_target="tpu_custom_call" | custom-call | flops 1310720 | bytes 524288 | tf_op jit(solution)/shard_map/norm/pallas_call | solution.py:233
  2.5 0.9 fusion
  3.4 3.4 %collective-permute-start = (bf16[32,1024]{1,0:T(8,128)(2,1)S(1)}, bf16[32,1024]{1,0:T(8,128)(2,1)S(1)}, u32[]{:S(2)}, u32[]{:S(2)}) collective-permute-start(bf16[32,1024]{1,0:T(8,128)(2,1)S(1)} %get-tuple-element.42), channel_id=1, source_target_pairs={{0,4},{4,8},{8,12},{12,16},{16,20},{20,24},{24,28},{1,5},{5,9},{9,... | collective-permute-start | bytes 196616 | tf_op jit(solution)/shard_map/ppermute | solution.py:214
  6.8 3.3 %collective-permute-start.1 = (bf16[32,1024]{1,0:T(8,128)(2,1)S(1)}, bf16[32,1024]{1,0:T(8,128)(2,1)S(1)}, u32[]{:S(2)}, u32[]{:S(2)}) collective-permute-start(bf16[32,1024]{1,0:T(8,128)(2,1)S(1)} %get-tuple-element.41), channel_id=1, source_target_pairs={{4,0},{8,4},{12,8},{16,12},{20,16},{24,20},{28,24},{5,1},{9,5},{13... | collective-permute-start | bytes 196616 | tf_op jit(solution)/shard_map/ppermute | solution.py:214
  10.2 0.7 pad_add_fusion.where_ref
  10.8 1.4 %copy.12.index_ref = s32[32,12]{1,0:T(8,128)} copy(s32[32,12]{0,1:T(8,128)} %param.16) | data formatting | bytes 3072 | tf_op args[7]
  12.2 1.4 %copy.13.mask_ref = s32[32,12]{1,0:T(8,128)} copy(s32[32,12]{0,1:T(8,128)} %param.17) | data formatting | bytes 3072 | tf_op args[8]
  13.6 5.3 %project.1 = (bf16[32,1024]{1,0:T(8,128)(2,1)}, bf16[128,2048]{1,0:T(8,128)(2,1)}) custom-call(bf16[32,1024]{1,0:T(8,128)(2,1)} %bitcast.13, f32[1,1024]{1,0:T(1,128)} %bitcast.17, bf16[1024,1024]{1,0:T(8,128)(2,1)} %wq_ref.1, bf16[128,1024]{1,0:T(8,128)(2,1)} %norm.1.normed_ref, bf16[1024,2048]{1,0:T(8,128)(2,1)} %wkv_ref.5), custom_call_target="tpu_custom_call" | custom-call | flops 603979776 | bytes 6291456 | tf_op jit(solution)/shard_map/project/pallas_call | solution.py:246
  18.9 0.0 collective-permute-done.low_ref
  18.9 0.0 collective-permute-done.1.high_ref
  18.9 0.0 copy-start.10
  18.9 0.6 copy-done.9
  19.5 0.0 copy-done.10
  19.6 8.5 %attend.1 = (bf16[32,1024]{1,0:T(8,128)(2,1)}, bf16[192,2048]{1,0:T(8,128)(2,1)}, bf16[192,512]{1,0:T(8,128)(2,1)}, bf16[192,512]{1,0:T(8,128)(2,1)}, bf16[192,5...) custom-call(s32[3]{0:T(128)} %pad_add_fusion.where_ref, bf16[32,1024]{1,0:T(8,128)(2,1)} %copy-done.9, ...), custom_call_target="tpu_custom_call" | custom-call | flops 3000000000 | bytes 10485760 | tf_op jit(solution)/shard_map/attend/pallas_call | solution.py:273
  28.1 0.0 collective-permute-start.4
  28.1 0.0 copy-done
  28.1 0.9 pad_maximum_fusion.refs_4_
  29.0 0.0 copy-start.1
  29.0 0.6 collective-permute-start.7
  29.6 1.5 %collective-permute-start.8 = (bf16[192,1024]{1,0:T(8,128)(2,1)S(1)}, bf16[192,1024]{1,0:T(8,128)(2,1)S(1)}, u32[]{:S(2)}, u32[]{:S(2)}) collective-permute-start(bf16[192,1024]{1,0:T(8,128)(2,1)S(1)} %pad_maximum_fusion.refs_4_), channel_id=1, source_target_pairs={{0,2},{1,3},{2,0},{3,1},{4,6},{5,7},{6,4},{7,5},{8,10},{9,11},{10,... | collective-permute-start | bytes 1179656 | tf_op jit(solution)/shard_map/ppermute | solution.py:208
  31.1 0.0 collective-permute-start.9
  31.1 1.4 %collective-permute-start.5 = (bf16[192,512]{1,0:T(8,128)(2,1)}, bf16[192,512]{1,0:T(8,128)(2,1)S(1)}, u32[]{:S(2)}, u32[]{:S(2)}) collective-permute-start(bf16[192,512]{1,0:T(8,128)(2,1)} %get-tuple-element.31), channel_id=1, source_target_pairs={{0,2},{1,3},{2,0},{3,1},{4,6},{5,7},{6,4},{7,5},{8,10},{9,11},{10,... | collective-permute-start | bytes 589832 | tf_op jit(solution)/shard_map/ppermute | solution.py:208
  32.5 0.0 collective-permute-done.4.refs_1_
  32.5 0.5 collective-permute-start.6
  33.1 21.1 %collective-permute-done.5.refs_2_ = bf16[192,512]{1,0:T(8,128)(2,1)S(1)} collective-permute-done((bf16[192,512]{1,0:T(8,128)(2,1)}, bf16[192,512]{1,0:T(8,128)(2,1)S(1)}, u32[]{:S(2)}, u32[]{:S(2)}) %collective-permute-start.5) | collective-permute-done | bytes 196640 | tf_op jit(solution)/shard_map/ppermute | solution.py:208
  54.2 2.5 %collective-permute-done.6.refs_3_ = bf16[192,512]{1,0:T(8,128)(2,1)S(1)} collective-permute-done((bf16[192,512]{1,0:T(8,128)(2,1)}, bf16[192,512]{1,0:T(8,128)(2,1)S(1)}, u32[]{:S(2)}, u32[]{:S(2)}) %collective-permute-start.6) | collective-permute-done | bytes 196640 | tf_op jit(solution)/shard_map/ppermute | solution.py:208
  56.7 0.0 collective-permute-done.7.refs_5_
  56.7 0.0 collective-permute-done.8.refs_6_
  56.7 0.0 copy-start.14
  56.7 0.0 collective-permute-done.9.refs_7_
  56.7 0.0 copy-start.15
  56.7 0.0 copy-done.1
  56.7 0.0 copy-done.16
  56.7 0.0 copy-done.17
  56.8 0.6 copy-done.18
  57.4 0.2 copy-done.13
  57.5 0.1 copy-done.14
  57.6 0.2 copy-done.15
  57.8 4.0 %product.1 = (f32[64,1024]{1,0:T(8,128)}, bf16[64,1024]{1,0:T(8,128)(2,1)}, bf16[64,1024]{1,0:T(8,128)(2,1)}, bf16[64,1024]{1,0:T(8,128)(2,1)}, bf16[64,1024]{1,...) custom-call(s32[3]{0:T(128)} %pad_add_fusion.where_ref, ...), custom_call_target="tpu_custom_call" | custom-call | flops 805306368 | bytes 8388608 | tf_op jit(solution)/shard_map/product/pallas_call | solution.py:313
  61.8 0.0 copy-start.21
  61.8 0.0 copy-start.20
  61.8 0.7 collective-permute-start.10
  62.5 1.6 %collective-permute-start.11 = (bf16[64,1024]{1,0:T(8,128)(2,1)}, bf16[64,1024]{1,0:T(8,128)(2,1)S(1)}, u32[]{:S(2)}, u32[]{:S(2)}) collective-permute-start(bf16[64,1024]{1,0:T(8,128)(2,1)} %get-tuple-element.35), channel_id=1, source_target_pairs={{0,8},{4,12},{8,0},{12,4},{16,24},{20,28},{24,16},{28,20},{1,9},{5... | collective-permute-start | bytes 393224 | tf_op jit(solution)/shard_map/ppermute | solution.py:208
  64.1 4.7 %window.1 = (f32[128,1024]{1,0:T(8,128)}, bf16[32,1024]{1,0:T(8,128)(2,1)}, bf16[32,1024]{1,0:T(8,128)(2,1)}) custom-call(bf16[192,2048]{1,0:T(8,128)(2,1)} %get-tuple-element.25.partial_ref, bf16[1024,2048]{1,0:T(8,128)(2,1)} %wkv_ref.5), custom_call_target="tpu_custom_call" | custom-call | flops 805306368 | bytes 6291456 | tf_op jit(solution)/shard_map/window/pallas_call | solution.py:297
  68.8 3.3 %collective-permute-start.2 = (bf16[32,1024]{1,0:T(8,128)(2,1)}, bf16[32,1024]{1,0:T(8,128)(2,1)S(1)}, u32[]{:S(2)}, u32[]{:S(2)}) collective-permute-start(bf16[32,1024]{1,0:T(8,128)(2,1)} %get-tuple-element.27), channel_id=1, source_target_pairs={{0,4},{4,8},{8,12},{12,16},{16,20},{20,24},{24,28},{1,5},{5,9},{9,... | collective-permute-start | bytes 196616 | tf_op jit(solution)/shard_map/ppermute | solution.py:214
  72.2 3.4 %collective-permute-start.3 = (bf16[32,1024]{1,0:T(8,128)(2,1)}, bf16[32,1024]{1,0:T(8,128)(2,1)S(1)}, u32[]{:S(2)}, u32[]{:S(2)}) collective-permute-start(bf16[32,1024]{1,0:T(8,128)(2,1)} %get-tuple-element.28), channel_id=1, source_target_pairs={{4,0},{8,4},{12,8},{16,12},{20,16},{24,20},{28,24},{5,1},{9,5},{13... | collective-permute-start | bytes 196616 | tf_op jit(solution)/shard_map/ppermute | solution.py:214
  75.6 0.5 collective-permute-start.12
  76.1 0.0 collective-permute-done.2.low_ref
  76.1 1.1 %collective-permute-start.13 = (bf16[64,1024]{1,0:T(8,128)(2,1)S(1)}, bf16[64,1024]{1,0:T(8,128)(2,1)S(1)}, u32[]{:S(2)}, u32[]{:S(2)}) collective-permute-start(bf16[64,1024]{1,0:T(8,128)(2,1)S(1)} %copy-done.22), channel_id=1, source_target_pairs={{0,16},{4,20},{8,24},{12,28},{16,0},{20,4},{24,8},{28,12},{1,17},{... | collective-permute-start | bytes 393224 | tf_op jit(solution)/shard_map/ppermute | solution.py:208
  77.2 1.3 %collective-permute-done.3.high_ref = bf16[32,1024]{1,0:T(8,128)(2,1)S(1)} collective-permute-done((bf16[32,1024]{1,0:T(8,128)(2,1)}, bf16[32,1024]{1,0:T(8,128)(2,1)S(1)}, u32[]{:S(2)}, u32[]{:S(2)}) %collective-permute-start.3) | collective-permute-done | bytes 65568 | tf_op jit(solution)/shard_map/ppermute | solution.py:214
  78.5 1.8 %collective-permute-start.14 = (bf16[64,1024]{1,0:T(8,128)(2,1)S(1)}, bf16[64,1024]{1,0:T(8,128)(2,1)S(1)}, u32[]{:S(2)}, u32[]{:S(2)}) collective-permute-start(bf16[64,1024]{1,0:T(8,128)(2,1)S(1)} %copy-done.21), channel_id=1, source_target_pairs={{0,20},{4,16},{8,28},{12,24},{16,4},{20,0},{24,12},{28,8},{1,21},{... | collective-permute-start | bytes 393224 | tf_op jit(solution)/shard_map/ppermute | solution.py:208
  80.3 0.0 collective-permute-done.10.refs_1_
  80.3 1.1 %collective-permute-start.15 = (bf16[64,1024]{1,0:T(8,128)(2,1)S(1)}, bf16[64,1024]{1,0:T(8,128)(2,1)S(1)}, u32[]{:S(2)}, u32[]{:S(2)}) collective-permute-start(bf16[64,1024]{1,0:T(8,128)(2,1)S(1)} %copy-done.20), channel_id=1, source_target_pairs={{0,24},{4,28},{8,16},{12,20},{16,8},{20,12},{24,0},{28,4},{1,25},{... | collective-permute-start | bytes 393224 | tf_op jit(solution)/shard_map/ppermute | solution.py:208
  81.5 0.0 collective-permute-done.11.refs_2_
  81.5 2.5 %collective-permute-start.16 = (bf16[64,1024]{1,0:T(8,128)(2,1)S(1)}, bf16[64,1024]{1,0:T(8,128)(2,1)S(1)}, u32[]{:S(2)}, u32[]{:S(2)}) collective-permute-start(bf16[64,1024]{1,0:T(8,128)(2,1)S(1)} %copy-done.19), channel_id=1, source_target_pairs={{0,28},{4,24},{8,20},{12,16},{16,12},{20,8},{24,4},{28,0},{1,29},{... | collective-permute-start | bytes 393224 | tf_op jit(solution)/shard_map/ppermute | solution.py:208
  84.0 0.0 copy-done.12
  84.0 2.2 %finish.1 = bf16[128,1024]{1,0:T(8,128)(2,1)} custom-call(bf16[128,1024]{1,0:T(8,128)(2,1)} %bitcast.11, f32[1,1024]{1,0:T(1,128)} %bitcast.16, f32[128,1024]{1,0:T(8,128)} %get-tuple-element.26.own_ref, bf16[32,1024]{1,0:T(8,128)(2,1)} %copy-done.11, bf16[32,1024]{1,0:T(8,128)(2,1)} %copy-done.12), custom_call_target="tpu_custom_call" | custom-call | flops 2621440 | bytes 1048576 | tf_op jit(solution)/shard_map/finish/pallas_call | solution.py:339
  86.2 0.0 collective-permute-done.12.refs_3_
  86.2 6.0 %collective-permute-done.13.refs_4_ = bf16[64,1024]{1,0:T(8,128)(2,1)S(1)} collective-permute-done((bf16[64,1024]{1,0:T(8,128)(2,1)S(1)}, bf16[64,1024]{1,0:T(8,128)(2,1)S(1)}, u32[]{:S(2)}, u32[]{:S(2)}) %collective-permute-start.13) | collective-permute-done | bytes 131104 | tf_op jit(solution)/shard_map/ppermute | solution.py:208
  92.2 2.9 %collective-permute-done.14.refs_5_ = bf16[64,1024]{1,0:T(8,128)(2,1)S(1)} collective-permute-done((bf16[64,1024]{1,0:T(8,128)(2,1)S(1)}, bf16[64,1024]{1,0:T(8,128)(2,1)S(1)}, u32[]{:S(2)}, u32[]{:S(2)}) %collective-permute-start.14) | collective-permute-done | bytes 131104 | tf_op jit(solution)/shard_map/ppermute | solution.py:208
  95.2 4.8 %collective-permute-done.15.refs_6_ = bf16[64,1024]{1,0:T(8,128)(2,1)S(1)} collective-permute-done((bf16[64,1024]{1,0:T(8,128)(2,1)S(1)}, bf16[64,1024]{1,0:T(8,128)(2,1)S(1)}, u32[]{:S(2)}, u32[]{:S(2)}) %collective-permute-start.15) | collective-permute-done | bytes 131104 | tf_op jit(solution)/shard_map/ppermute | solution.py:208
  99.9 2.4 %collective-permute-done.16.refs_7_ = bf16[64,1024]{1,0:T(8,128)(2,1)S(1)} collective-permute-done((bf16[64,1024]{1,0:T(8,128)(2,1)S(1)}, bf16[64,1024]{1,0:T(8,128)(2,1)S(1)}, u32[]{:S(2)}, u32[]{:S(2)}) %collective-permute-start.16) | collective-permute-done | bytes 131104 | tf_op jit(solution)/shard_map/ppermute | solution.py:208
  102.4 0.6 copy-done.8
  103.0 2.1 %total.1 = f32[64,1024]{1,0:T(8,128)} custom-call(f32[64,1024]{1,0:T(8,128)} %get-tuple-element.33.refs_0_, bf16[64,1024]{1,0:T(8,128)(2,1)} %copy-done.2, bf16[64,1024]{1,0:T(8,128)(2,1)} %copy-done.3, bf16[64,1024]{1,0:T(8,128)(2,1)} %copy-done.4, bf16[64,1024]{1,0:T(8,128)(2,1)} %copy-done.5, bf16[64,1024]{1,0:T(8,128)(2,1)} %copy-done.6, ...), custom_call_target="tpu_custom_call" | custom-call | tf_op jit(solution)/shard_map/total/pallas_call | solution.py:324
  (30 shorter events, 0.1 us)
Async XLA Ops:
  3.4 15.5 %collective-permute-start = (bf16[32,1024]{1,0:T(8,128)(2,1)S(1)}, bf16[32,1024]{1,0:T(8,128)(2,1)S(1)}, u32[]{:S(2)}, u32[]{:S(2)}) collective-permute-start(bf16[32,1024]{1,0:T(8,128)(2,1)S(1)} %get-tuple-element.42), channel_id=1, source_target_pairs={{0,4},{4,8},{8,12},{12,16},{16,20},{20,24},{24,28},{1,5},{5,9},{9,... | collective-permute-start | bytes 196616 | tf_op jit(solution)/shard_map/ppermute | solution.py:214
  6.8 12.1 %collective-permute-start.1 = (bf16[32,1024]{1,0:T(8,128)(2,1)S(1)}, bf16[32,1024]{1,0:T(8,128)(2,1)S(1)}, u32[]{:S(2)}, u32[]{:S(2)}) collective-permute-start(bf16[32,1024]{1,0:T(8,128)(2,1)S(1)} %get-tuple-element.41), channel_id=1, source_target_pairs={{4,0},{8,4},{12,8},{16,12},{20,16},{24,20},{28,24},{5,1},{9,5},{13... | collective-permute-start | bytes 196616 | tf_op jit(solution)/shard_map/ppermute | solution.py:214
  18.9 0.6 copy-start.9
  18.9 0.6 copy-start.10
  19.6 8.6 %copy-start = (bf16[128,1024]{1,0:T(8,128)(2,1)S(1)}, bf16[128,1024]{1,0:T(8,128)(2,1)}, u32[]{:S(2)}) copy-start(bf16[128,1024]{1,0:T(8,128)(2,1)} %norm.1.normed_ref) | copy-start | bytes 786436
  28.1 4.4 %collective-permute-start.4 = (bf16[192,512]{1,0:T(8,128)(2,1)}, bf16[192,512]{1,0:T(8,128)(2,1)S(1)}, u32[]{:S(2)}, u32[]{:S(2)}) collective-permute-start(bf16[192,512]{1,0:T(8,128)(2,1)} %get-tuple-element.30), channel_id=1, source_target_pairs={{0,1},{1,0},{2,3},{3,2},{4,5},{5,4},{6,7},{7,6},{8,9},{9,8},{10,11... | collective-permute-start | bytes 589832 | tf_op jit(solution)/shard_map/ppermute | solution.py:208
  29.0 27.7 %copy-start.1 = (bf16[192,1024]{1,0:T(8,128)(2,1)}, bf16[192,1024]{1,0:T(8,128)(2,1)S(1)}, u32[]{:S(2)}) copy-start(bf16[192,1024]{1,0:T(8,128)(2,1)S(1)} %pad_maximum_fusion.refs_4_) | copy-start | bytes 1179652
  29.0 27.7 %collective-permute-start.7 = (bf16[192,1024]{1,0:T(8,128)(2,1)S(1)}, bf16[192,1024]{1,0:T(8,128)(2,1)S(1)}, u32[]{:S(2)}, u32[]{:S(2)}) collective-permute-start(bf16[192,1024]{1,0:T(8,128)(2,1)S(1)} %pad_maximum_fusion.refs_4_), channel_id=1, source_target_pairs={{0,1},{1,0},{2,3},{3,2},{4,5},{5,4},{6,7},{7,6},{8,9},{9,8},{10,11... | collective-permute-start | bytes 1179656 | tf_op jit(solution)/shard_map/ppermute | solution.py:208
  29.6 27.1 %collective-permute-start.8 = (bf16[192,1024]{1,0:T(8,128)(2,1)S(1)}, bf16[192,1024]{1,0:T(8,128)(2,1)S(1)}, u32[]{:S(2)}, u32[]{:S(2)}) collective-permute-start(bf16[192,1024]{1,0:T(8,128)(2,1)S(1)} %pad_maximum_fusion.refs_4_), channel_id=1, source_target_pairs={{0,2},{1,3},{2,0},{3,1},{4,6},{5,7},{6,4},{7,5},{8,10},{9,11},{10,... | collective-permute-start | bytes 1179656 | tf_op jit(solution)/shard_map/ppermute | solution.py:208
  31.1 25.6 %collective-permute-start.9 = (bf16[192,1024]{1,0:T(8,128)(2,1)S(1)}, bf16[192,1024]{1,0:T(8,128)(2,1)S(1)}, u32[]{:S(2)}, u32[]{:S(2)}) collective-permute-start(bf16[192,1024]{1,0:T(8,128)(2,1)S(1)} %pad_maximum_fusion.refs_4_), channel_id=1, source_target_pairs={{0,3},{1,2},{2,1},{3,0},{4,7},{5,6},{6,5},{7,4},{8,11},{9,10},{10,... | collective-permute-start | bytes 1179656 | tf_op jit(solution)/shard_map/ppermute | solution.py:208
  31.1 23.1 %collective-permute-start.5 = (bf16[192,512]{1,0:T(8,128)(2,1)}, bf16[192,512]{1,0:T(8,128)(2,1)S(1)}, u32[]{:S(2)}, u32[]{:S(2)}) collective-permute-start(bf16[192,512]{1,0:T(8,128)(2,1)} %get-tuple-element.31), channel_id=1, source_target_pairs={{0,2},{1,3},{2,0},{3,1},{4,6},{5,7},{6,4},{7,5},{8,10},{9,11},{10,... | collective-permute-start | bytes 589832 | tf_op jit(solution)/shard_map/ppermute | solution.py:208
  32.5 24.2 %copy-start.16 = (bf16[192,512]{1,0:T(8,128)(2,1)}, bf16[192,512]{1,0:T(8,128)(2,1)S(1)}, u32[]{:S(2)}) copy-start(bf16[192,512]{1,0:T(8,128)(2,1)S(1)} %collective-permute-done.4.refs_1_) | copy-start | bytes 589828
  32.5 24.1 %collective-permute-start.6 = (bf16[192,512]{1,0:T(8,128)(2,1)}, bf16[192,512]{1,0:T(8,128)(2,1)S(1)}, u32[]{:S(2)}, u32[]{:S(2)}) collective-permute-start(bf16[192,512]{1,0:T(8,128)(2,1)} %get-tuple-element.32), channel_id=1, source_target_pairs={{0,3},{1,2},{2,1},{3,0},{4,7},{5,6},{6,5},{7,4},{8,11},{9,10},{10,... | collective-permute-start | bytes 589832 | tf_op jit(solution)/shard_map/ppermute | solution.py:208
  54.2 2.5 %copy-start.17 = (bf16[192,512]{1,0:T(8,128)(2,1)}, bf16[192,512]{1,0:T(8,128)(2,1)S(1)}, u32[]{:S(2)}) copy-start(bf16[192,512]{1,0:T(8,128)(2,1)S(1)} %collective-permute-done.5.refs_2_) | copy-start | bytes 589828
  56.7 0.7 copy-start.18
  56.7 0.8 copy-start.13
  56.7 0.9 copy-start.14
  56.7 1.1 %copy-start.15 = (bf16[192,1024]{1,0:T(8,128)(2,1)}, bf16[192,1024]{1,0:T(8,128)(2,1)S(1)}, u32[]{:S(2)}) copy-start(bf16[192,1024]{1,0:T(8,128)(2,1)S(1)} %collective-permute-done.9.refs_7_) | copy-start | bytes 1179652
  61.8 13.8 %copy-start.23 = (bf16[64,1024]{1,0:T(8,128)(2,1)S(1)}, bf16[64,1024]{1,0:T(8,128)(2,1)}, u32[]{:S(2)}) copy-start(bf16[64,1024]{1,0:T(8,128)(2,1)} %get-tuple-element.36) | copy-start | bytes 393220
  61.8 14.3 %copy-start.22 = (bf16[64,1024]{1,0:T(8,128)(2,1)S(1)}, bf16[64,1024]{1,0:T(8,128)(2,1)}, u32[]{:S(2)}) copy-start(bf16[64,1024]{1,0:T(8,128)(2,1)} %get-tuple-element.37) | copy-start | bytes 393220
  61.8 16.7 %copy-start.21 = (bf16[64,1024]{1,0:T(8,128)(2,1)S(1)}, bf16[64,1024]{1,0:T(8,128)(2,1)}, u32[]{:S(2)}) copy-start(bf16[64,1024]{1,0:T(8,128)(2,1)} %get-tuple-element.38) | copy-start | bytes 393220
  61.8 18.5 %copy-start.20 = (bf16[64,1024]{1,0:T(8,128)(2,1)S(1)}, bf16[64,1024]{1,0:T(8,128)(2,1)}, u32[]{:S(2)}) copy-start(bf16[64,1024]{1,0:T(8,128)(2,1)} %get-tuple-element.39) | copy-start | bytes 393220
  61.8 19.6 %copy-start.19 = (bf16[64,1024]{1,0:T(8,128)(2,1)S(1)}, bf16[64,1024]{1,0:T(8,128)(2,1)}, u32[]{:S(2)}) copy-start(bf16[64,1024]{1,0:T(8,128)(2,1)} %get-tuple-element.40) | copy-start | bytes 393220
  61.8 18.5 %collective-permute-start.10 = (bf16[64,1024]{1,0:T(8,128)(2,1)}, bf16[64,1024]{1,0:T(8,128)(2,1)S(1)}, u32[]{:S(2)}, u32[]{:S(2)}) collective-permute-start(bf16[64,1024]{1,0:T(8,128)(2,1)} %get-tuple-element.34), channel_id=1, source_target_pairs={{0,4},{4,0},{8,12},{12,8},{16,20},{20,16},{24,28},{28,24},{1,5},{5... | collective-permute-start | bytes 393224 | tf_op jit(solution)/shard_map/ppermute | solution.py:208
  62.5 19.0 %collective-permute-start.11 = (bf16[64,1024]{1,0:T(8,128)(2,1)}, bf16[64,1024]{1,0:T(8,128)(2,1)S(1)}, u32[]{:S(2)}, u32[]{:S(2)}) collective-permute-start(bf16[64,1024]{1,0:T(8,128)(2,1)} %get-tuple-element.35), channel_id=1, source_target_pairs={{0,8},{4,12},{8,0},{12,4},{16,24},{20,28},{24,16},{28,20},{1,9},{5... | collective-permute-start | bytes 393224 | tf_op jit(solution)/shard_map/ppermute | solution.py:208
  68.8 7.3 %collective-permute-start.2 = (bf16[32,1024]{1,0:T(8,128)(2,1)}, bf16[32,1024]{1,0:T(8,128)(2,1)S(1)}, u32[]{:S(2)}, u32[]{:S(2)}) collective-permute-start(bf16[32,1024]{1,0:T(8,128)(2,1)} %get-tuple-element.27), channel_id=1, source_target_pairs={{0,4},{4,8},{8,12},{12,16},{16,20},{20,24},{24,28},{1,5},{5,9},{9,... | collective-permute-start | bytes 196616 | tf_op jit(solution)/shard_map/ppermute | solution.py:214
  72.2 6.4 %collective-permute-start.3 = (bf16[32,1024]{1,0:T(8,128)(2,1)}, bf16[32,1024]{1,0:T(8,128)(2,1)S(1)}, u32[]{:S(2)}, u32[]{:S(2)}) collective-permute-start(bf16[32,1024]{1,0:T(8,128)(2,1)} %get-tuple-element.28), channel_id=1, source_target_pairs={{4,0},{8,4},{12,8},{16,12},{20,16},{24,20},{28,24},{5,1},{9,5},{13... | collective-permute-start | bytes 196616 | tf_op jit(solution)/shard_map/ppermute | solution.py:214
  75.6 10.7 %collective-permute-start.12 = (bf16[64,1024]{1,0:T(8,128)(2,1)S(1)}, bf16[64,1024]{1,0:T(8,128)(2,1)S(1)}, u32[]{:S(2)}, u32[]{:S(2)}) collective-permute-start(bf16[64,1024]{1,0:T(8,128)(2,1)S(1)} %copy-done.23), channel_id=1, source_target_pairs={{0,12},{4,8},{8,4},{12,0},{16,28},{20,24},{24,20},{28,16},{1,13},{... | collective-permute-start | bytes 393224 | tf_op jit(solution)/shard_map/ppermute | solution.py:208
  76.1 7.9 %copy-start.11 = (bf16[32,1024]{1,0:T(8,128)(2,1)}, bf16[32,1024]{1,0:T(8,128)(2,1)S(1)}, u32[]{:S(2)}) copy-start(bf16[32,1024]{1,0:T(8,128)(2,1)S(1)} %collective-permute-done.2.low_ref) | copy-start | bytes 196612
  76.1 16.1 %collective-permute-start.13 = (bf16[64,1024]{1,0:T(8,128)(2,1)S(1)}, bf16[64,1024]{1,0:T(8,128)(2,1)S(1)}, u32[]{:S(2)}, u32[]{:S(2)}) collective-permute-start(bf16[64,1024]{1,0:T(8,128)(2,1)S(1)} %copy-done.22), channel_id=1, source_target_pairs={{0,16},{4,20},{8,24},{12,28},{16,0},{20,4},{24,8},{28,12},{1,17},{... | collective-permute-start | bytes 393224 | tf_op jit(solution)/shard_map/ppermute | solution.py:208
  78.5 5.5 %copy-start.12 = (bf16[32,1024]{1,0:T(8,128)(2,1)}, bf16[32,1024]{1,0:T(8,128)(2,1)S(1)}, u32[]{:S(2)}) copy-start(bf16[32,1024]{1,0:T(8,128)(2,1)S(1)} %collective-permute-done.3.high_ref) | copy-start | bytes 196612
  78.5 16.6 %collective-permute-start.14 = (bf16[64,1024]{1,0:T(8,128)(2,1)S(1)}, bf16[64,1024]{1,0:T(8,128)(2,1)S(1)}, u32[]{:S(2)}, u32[]{:S(2)}) collective-permute-start(bf16[64,1024]{1,0:T(8,128)(2,1)S(1)} %copy-done.21), channel_id=1, source_target_pairs={{0,20},{4,16},{8,28},{12,24},{16,4},{20,0},{24,12},{28,8},{1,21},{... | collective-permute-start | bytes 393224 | tf_op jit(solution)/shard_map/ppermute | solution.py:208
  80.3 22.0 %copy-start.2 = (bf16[64,1024]{1,0:T(8,128)(2,1)}, bf16[64,1024]{1,0:T(8,128)(2,1)S(1)}, u32[]{:S(2)}) copy-start(bf16[64,1024]{1,0:T(8,128)(2,1)S(1)} %collective-permute-done.10.refs_1_) | copy-start | bytes 393220
  80.3 19.6 %collective-permute-start.15 = (bf16[64,1024]{1,0:T(8,128)(2,1)S(1)}, bf16[64,1024]{1,0:T(8,128)(2,1)S(1)}, u32[]{:S(2)}, u32[]{:S(2)}) collective-permute-start(bf16[64,1024]{1,0:T(8,128)(2,1)S(1)} %copy-done.20), channel_id=1, source_target_pairs={{0,24},{4,28},{8,16},{12,20},{16,8},{20,12},{24,0},{28,4},{1,25},{... | collective-permute-start | bytes 393224 | tf_op jit(solution)/shard_map/ppermute | solution.py:208
  81.5 20.9 %copy-start.3 = (bf16[64,1024]{1,0:T(8,128)(2,1)}, bf16[64,1024]{1,0:T(8,128)(2,1)S(1)}, u32[]{:S(2)}) copy-start(bf16[64,1024]{1,0:T(8,128)(2,1)S(1)} %collective-permute-done.11.refs_2_) | copy-start | bytes 393220
  81.5 20.9 %collective-permute-start.16 = (bf16[64,1024]{1,0:T(8,128)(2,1)S(1)}, bf16[64,1024]{1,0:T(8,128)(2,1)S(1)}, u32[]{:S(2)}, u32[]{:S(2)}) collective-permute-start(bf16[64,1024]{1,0:T(8,128)(2,1)S(1)} %copy-done.19), channel_id=1, source_target_pairs={{0,28},{4,24},{8,20},{12,16},{16,12},{20,8},{24,4},{28,0},{1,29},{... | collective-permute-start | bytes 393224 | tf_op jit(solution)/shard_map/ppermute | solution.py:208
  86.2 16.1 %copy-start.4 = (bf16[64,1024]{1,0:T(8,128)(2,1)}, bf16[64,1024]{1,0:T(8,128)(2,1)S(1)}, u32[]{:S(2)}) copy-start(bf16[64,1024]{1,0:T(8,128)(2,1)S(1)} %collective-permute-done.12.refs_3_) | copy-start | bytes 393220
  92.2 10.2 %copy-start.5 = (bf16[64,1024]{1,0:T(8,128)(2,1)}, bf16[64,1024]{1,0:T(8,128)(2,1)S(1)}, u32[]{:S(2)}) copy-start(bf16[64,1024]{1,0:T(8,128)(2,1)S(1)} %collective-permute-done.13.refs_4_) | copy-start | bytes 393220
  95.1 7.2 %copy-start.6 = (bf16[64,1024]{1,0:T(8,128)(2,1)}, bf16[64,1024]{1,0:T(8,128)(2,1)S(1)}, u32[]{:S(2)}) copy-start(bf16[64,1024]{1,0:T(8,128)(2,1)S(1)} %collective-permute-done.14.refs_5_) | copy-start | bytes 393220
  99.9 2.5 %copy-start.7 = (bf16[64,1024]{1,0:T(8,128)(2,1)}, bf16[64,1024]{1,0:T(8,128)(2,1)S(1)}, u32[]{:S(2)}) copy-start(bf16[64,1024]{1,0:T(8,128)(2,1)S(1)} %collective-permute-done.15.refs_6_) | copy-start | bytes 393220
  102.4 0.6 copy-start.8

commit v2 on v1

v2 whole, which is shorter than its diff:
```python
import functools
import math

import jax
import jax.numpy as jnp
from jax import lax
from jax.experimental import pallas as pl
from jax.experimental.pallas import tpu as pltpu
from jax.sharding import PartitionSpec as P

HEADS = 16
K = 12
R = 32
EPSILON = 1e-05
F32 = jnp.float32
BF16 = jnp.bfloat16


def spec(space=pltpu.VMEM):
    return pl.BlockSpec(memory_space=space)


def estimate(flops, moved):
    return pl.CostEstimate(flops=int(flops), bytes_accessed=int(moved), transcendentals=0)


def dot(left, right):
    return jnp.dot(left, right, preferred_element_type=F32)


def dot_rows(left, right):
    return lax.dot_general(left, right, (((0,), (0,)), ((), ())), preferred_element_type=F32)


def dot_lanes(left, right):
    return lax.dot_general(left, right, (((1,), (1,)), ((), ())), preferred_element_type=F32)


def halves(wide):
    high = wide.astype(BF16)
    return high, (wide - high.astype(F32)).astype(BF16)


def normalize(values):
    values = values.astype(F32)
    average = jnp.mean(values, axis=-1, keepdims=True)
    centred = values - average
    variance = jnp.mean(centred * centred, axis=-1, keepdims=True)
    inv_std = lax.rsqrt(variance + EPSILON)
    return centred * inv_std, inv_std


def parity():
    return lax.rem(lax.axis_index("band"), 2)


def pick(flag, one, zero):
    return flag * one + (1 - flag) * zero


def norm_kernel(grid_ref, gain_ref, normed_ref, edge_ref):
    standard, _ = normalize(grid_ref[...])
    normed_ref[...] = (standard * gain_ref[...]).astype(BF16)
    start = pl.multiple_of(pick(parity(), normed_ref.shape[0] - R, 0), R)
    edge_ref[...] = normed_ref[pl.ds(start, R)]


def query_kernel(hidden_ref, gain_ref, wq_ref, q_ref, hat_ref):
    @pl.when(pl.program_id(0) == 0)
    def _():
        standard, _ = normalize(hidden_ref[...])
        hat_ref[...] = (standard * gain_ref[...]).astype(BF16)

    q_ref[...] = dot(hat_ref[...], wq_ref[...]).astype(BF16)


def own_kernel(normed_ref, wkv_ref, kv_ref):
    kv_ref[...] = dot(normed_ref[...], wkv_ref[...]).astype(BF16)


def halo_kernel(outer_ref, pair_ref, far_ref, wkv_ref, kv_ref, shared_ref, both_ref):
    rows = pair_ref.shape[0]

    @pl.when(pl.program_id(0) == 0)
    def _():
        odd = parity()
        outer_at = pl.multiple_of(pick(odd, R, 0), R)
        inner_at = pl.multiple_of(pick(odd, 0, R), R)
        from_at = pl.multiple_of(pick(odd, rows - R, 0), R)
        both_ref[pl.ds(outer_at, R)] = outer_ref[...]
        both_ref[pl.ds(inner_at, R)] = pair_ref[pl.ds(from_at, R)]
        shared_ref[:rows] = pair_ref[...]
        shared_ref[rows : rows + R] = outer_ref[...]
        shared_ref[rows + R :] = far_ref[...]

    kv_ref[...] = dot(both_ref[...], wkv_ref[...]).astype(BF16)


def attend_kernel(
    halo_ref, kv_ref, q_ref, cot_ref, hidden_ref, index_ref, mask_ref, updated_ref, partial_ref,
    *refs
):
    piece_refs, window_ref = refs[:-1], refs[-1]
    nodes, features = q_ref.shape
    own = kv_ref.shape[0]
    rows = own + 2 * R
    lanes = 128
    head_dim = features // HEADS
    shift = head_dim.bit_length() - 1
    scale = 1.0 / math.sqrt(head_dim)
    window_ref[:R] = halo_ref[:R]
    window_ref[R : R + own] = kv_ref[...]
    window_ref[R + own :] = halo_ref[R:]

    eye_a = lax.broadcasted_iota(jnp.int32, (K, lanes), 0)
    eye_b = lax.broadcasted_iota(jnp.int32, (K, lanes), 1)
    eye = jnp.where(eye_a == eye_b, 1.0, 0.0).astype(BF16)
    first_row = lax.axis_index("band") * own - R
    local = dot_rows((index_ref[...] - first_row).astype(F32).astype(BF16), eye).astype(jnp.int32)
    mask = dot_rows(mask_ref[...].astype(F32).astype(BF16), eye)
    row_id = lax.broadcasted_iota(jnp.int32, (nodes, rows), 1)
    picks = jnp.concatenate(
        [jnp.where(row_id == local[:, k : k + 1], 1.0, 0.0).astype(BF16) for k in range(K)], axis=0
    )
    valid = jnp.concatenate([mask[:, k : k + 1] for k in range(K)], axis=0) > 0.5
    chunk = 256
    feature_id = lax.broadcasted_iota(jnp.int32, (features, lanes), 0)
    lane_id = lax.broadcasted_iota(jnp.int32, (features, lanes), 1)
    to_heads = jnp.where(jnp.right_shift(feature_id, shift) == lane_id, 1.0, 0.0).astype(BF16)
    lane_t = lax.broadcasted_iota(jnp.int32, (lanes, features), 0)
    feature_t = lax.broadcasted_iota(jnp.int32, (lanes, features), 1)
    from_heads = jnp.where(jnp.right_shift(feature_t, shift) == lane_t, 1.0, 0.0).astype(BF16)

    def repeated(ref, c):
        return jnp.broadcast_to(ref[:, c : c + chunk].astype(F32)[None], (K, nodes, chunk))

    def by_edge(ref, c, start):
        edge = dot(picks, window_ref[:, start + c : start + c + chunk])
        product = edge.reshape(K, nodes, chunk) * repeated(ref, c)
        first, second = halves(product.reshape(K * nodes, chunk))
        heads = to_heads[c : c + chunk]
        return dot(first, heads) + dot(second, heads)

    scores = by_edge(q_ref, 0, 0)
    d_probs = by_edge(cot_ref, 0, features)
    for c in range(chunk, features, chunk):
        scores = scores + by_edge(q_ref, c, 0)
        d_probs = d_probs + by_edge(cot_ref, c, features)
    scores = jnp.where(valid, scores * scale, -jnp.inf).reshape(K, nodes, lanes)
    d_probs = d_probs.reshape(K, nodes, lanes)
    terms = jnp.exp(scores - jnp.max(scores, axis=0, keepdims=True))
    probs = terms / jnp.sum(terms, axis=0, keepdims=True)
    probs_low = probs.reshape(K * nodes, lanes).astype(BF16)
    inner = jnp.sum(probs * d_probs, axis=0, keepdims=True)
    d_scores = (probs * (d_probs - inner)).reshape(K * nodes, lanes)
    d_first, d_second = halves(d_scores)

    for c in range(0, features, chunk):
        heads = from_heads[:, c : c + chunk]
        spread = dot(probs_low, heads).reshape(K, nodes, chunk)
        values = dot(picks, window_ref[:, features + c : features + c + chunk])
        attended = jnp.sum(spread * values.reshape(K, nodes, chunk), axis=0)
        updated_ref[:, c : c + chunk] = (
            hidden_ref[:, c : c + chunk].astype(F32) + attended
        ).astype(BF16)
        first, second = halves((spread * repeated(cot_ref, c)).reshape(K * nodes, chunk))
        partial_ref[:, features + c : features + c + chunk] = (
            dot_rows(picks, first) + dot_rows(picks, second)
        ).astype(BF16)
        spread = (dot(d_first, heads) + dot(d_second, heads)).reshape(K, nodes, chunk)
        keys = (spread * repeated(q_ref, c)).reshape(K * nodes, chunk) * scale
        first, second = halves(keys)
        partial_ref[:, c : c + chunk] = (
            dot_rows(picks, first) + dot_rows(picks, second)
        ).astype(BF16)

    mine = 2 * parity() + lax.axis_index("ens") // 2
    for k, piece_ref in enumerate(piece_refs):
        for i in range(piece_ref.shape[1] // lanes):
            start = pl.multiple_of((4 * i + (mine ^ k)) * lanes, lanes)
            piece_ref[:, i * lanes : (i + 1) * lanes] = partial_ref[:, pl.ds(start, lanes)]


def window_kernel(partial_ref, wkv_ref, own_ref, inner_ref, outer_ref, wide_ref):
    wide_ref[...] = dot_lanes(partial_ref[...], wkv_ref[...])
    rows = wide_ref.shape[0]
    odd = parity()
    inner_at = pl.multiple_of(pick(odd, 0, rows - R), R)
    outer_at = pl.multiple_of(pick(odd, rows - R, 0), R)
    own_ref[...] = wide_ref[R : rows - R]
    inner_ref[...] = wide_ref[pl.ds(inner_at, R)].astype(BF16)
    outer_ref[...] = wide_ref[pl.ds(outer_at, R)].astype(BF16)


def product_kernel(factor, *refs):
    lefts, (own, outer, pair, far, side, side_pair) = refs[:4], refs[4:10]
    keep_ref, send_ref, left_ref, right_ref, total_ref = refs[10:]
    window = lefts[0].shape[0]
    rows = own.shape[0]
    odd = parity()
    pieces = (
        ((own, 0), (outer, 0), (pair, 0)),
        ((side, 0), (side_pair, rows), (side_pair, 0)),
        ((pair, 0), (far, 0), (own, 0)),
        ((side_pair, 0), (side_pair, rows + R), (side, 0)),
    )
    for k, ((middle, m_at), (edge, e_at), (other, o_at)) in enumerate(pieces):
        base = k * window
        left_ref[base : base + window] = lefts[k][...]
        right_ref[base + R : base + R + rows] = middle[m_at : m_at + rows]
        flag = odd if k < 2 else 1 - odd
        edge_at = pl.multiple_of(base + pick(flag, R + rows, 0), R)
        other_at = pl.multiple_of(base + pick(flag, 0, R + rows), R)
        from_at = pl.multiple_of(o_at + pick(flag, rows - R, 0), R)
        right_ref[pl.ds(edge_at, R)] = edge[e_at : e_at + R]
        right_ref[pl.ds(other_at, R)] = other[pl.ds(from_at, R)]
    total_ref[...] = dot_rows(left_ref[...], right_ref[...]) * factor
    core = lax.rem(lax.axis_index("ens"), 2)
    block = keep_ref.shape[1]
    for i in range(keep_ref.shape[0]):
        keep_at = pl.multiple_of((2 * i + core) * block, block)
        send_at = pl.multiple_of((2 * i + 1 - core) * block, block)
        keep_ref[i] = total_ref[pl.ds(keep_at, block)]
        send_ref[i] = total_ref[pl.ds(send_at, block)].astype(BF16)


def pair_kernel(keep_ref, got_ref, *out_refs):
    group = lax.axis_index("band") // 2
    for k, out_ref in enumerate(out_refs):
        at = group ^ k
        out_ref[...] = (keep_ref[at] + got_ref[at].astype(F32)).astype(out_ref.dtype)


def finish_kernel(grid_ref, gain_ref, own_ref, inner_ref, outer_ref, out_ref, wide_ref):
    rows = own_ref.shape[0]
    odd = parity()
    wide_ref[...] = own_ref[...]
    inner_at = pl.multiple_of(pick(odd, 0, rows - R), R)
    outer_at = pl.multiple_of(pick(odd, rows - R, 0), R)
    wide_ref[pl.ds(inner_at, R)] = wide_ref[pl.ds(inner_at, R)] + inner_ref[...].astype(F32)
    wide_ref[pl.ds(outer_at, R)] = wide_ref[pl.ds(outer_at, R)] + outer_ref[...].astype(F32)
    standard, inv_std = normalize(grid_ref[...])
    scaled = wide_ref[...] * gain_ref[...]
    out_ref[...] = (
        inv_std
        * (
            scaled
            - jnp.mean(scaled, axis=-1, keepdims=True)
            - standard * jnp.mean(scaled * standard, axis=-1, keepdims=True)
        )
    ).astype(BF16)


def total_kernel(*refs):
    total = refs[0][...]
    for ref in refs[1:-1]:
        total = total + ref[...].astype(F32)
    refs[-1][...] = total


def swapped(value, band_bits, ens_bits):
    bands, members = lax.axis_size("band"), lax.axis_size("ens")
    flip = band_bits * members + ens_bits
    pairs = [(i, i ^ flip) for i in range(bands * members)]
    return lax.ppermute(value, ("band", "ens"), pairs)


def outward(value):
    bands = lax.axis_size("band")
    pairs = [(i, i + 1) for i in range(1, bands - 1, 2)]
    return lax.ppermute(value, "band", pairs + [(j, i) for i, j in pairs])


def call(kernel, name, shapes, operands, scratch=(), flops=0, moved=0, **options):
    if "in_specs" not in options:
        options["in_specs"] = [spec()] * len(operands)
        options["out_specs"] = [spec()] * len(shapes)
    return pl.pallas_call(
        kernel,
        out_shape=[jax.ShapeDtypeStruct(*shape) for shape in shapes],
        scratch_shapes=[pltpu.VMEM(*shape) for shape in scratch],
        cost_estimate=estimate(flops, moved),
        name=name,
        **options,
    )(*operands)


def streamed(kernel, name, steps, fixed, weight, shapes, scratch, flops):
    features, columns = weight.shape
    wide = columns // steps
    whole = [pl.BlockSpec(value.shape, lambda i: (0, 0)) for value in fixed]
    out = [pl.BlockSpec((shapes[0][0][0], wide), lambda i: (0, i))]
    out += [pl.BlockSpec(shape[0], lambda i: (0, 0)) for shape in shapes[1:]]
    return call(
        kernel, name, shapes, [*fixed, weight], scratch, flops, 2 * features * columns,
        grid=(steps,), in_specs=whole + [pl.BlockSpec((features, wide), lambda i: (0, i))],
        out_specs=out,
    )


def per_device(grid_latent, hidden, d_updated, w_kv, w_q, src_gain, q_gain, src_index, edge_mask):
    grid_latent, hidden, d_updated = grid_latent[0], hidden[0], d_updated[0]
    rows, features = grid_latent.shape
    nodes = hidden.shape[0]
    bands, members = lax.axis_size("band"), lax.axis_size("ens")
    window = rows + 2 * R
    block = 2 * features // (bands * members)
    groups = bands // 2
    src_gain, q_gain = src_gain[None], q_gain[None]
    grouped = members == 4 and groups & (groups - 1) == 0 and block == 64
    square = features * features

    normed, edge = call(
        norm_kernel, "norm", [((rows, features), BF16), ((R, features), BF16)],
        [grid_latent, src_gain], flops=10 * rows * features, moved=4 * rows * features,
    )
    outer = outward(edge)
    pair = swapped(normed, 1, 0)
    if grouped:
        side = swapped(normed, 0, 2)
    far = swapped(outer, 1, 0)

    (queries,) = streamed(
        query_kernel, "query", 2, [hidden, q_gain], w_q, [((nodes, features), BF16)],
        [((nodes, features), BF16)], 2 * nodes * square,
    )
    (kv,) = streamed(
        own_kernel, "own", 4, [normed], w_kv, [((rows, 2 * features), BF16)], [],
        4 * rows * square,
    )
    kv_halo, shared = streamed(
        halo_kernel, "halo", 4, [outer, pair, far], w_kv,
        [((2 * R, 2 * features), BF16), ((window, features), BF16)],
        [((2 * R, features), BF16)], 8 * R * square,
    )
    if grouped:
        side_pair = swapped(shared, 0, 2)

    pieces = 4 if grouped else 0
    updated, partial_value, *lefts = call(
        attend_kernel, "attend",
        [((nodes, features), BF16), ((window, 2 * features), BF16)]
        + [((window, features // 2), BF16)] * pieces,
        [kv_halo, kv, queries, d_updated, hidden, src_index.T, edge_mask.T],
        [((window, 2 * features), BF16)], flops=3e9, moved=4 * square,
    )
    if grouped:
        lefts = [lefts[0], swapped(lefts[1], 0, 2), swapped(lefts[2], 1, 0), swapped(lefts[3], 1, 2)]

    d_own, d_inner, d_outer = call(
        window_kernel, "window",
        [((rows, features), F32), ((R, features), BF16), ((R, features), BF16)],
        [partial_value, w_kv], [((window, features), F32)],
        flops=4 * window * square, moved=4 * square,
    )
    d_inner = swapped(d_inner, 1, 0)
    d_outer = outward(d_outer)

    factor = 1.0 / math.sqrt(members * rows * bands)
    if grouped:
        keep, send = call(
            functools.partial(product_kernel, factor), "product",
            [((groups, block, features), F32), ((groups, block, features), BF16)],
            [*lefts, normed, outer, pair, far, side, side_pair],
            [
                ((4 * window, features // 2), BF16),
                ((4 * window, features), BF16),
                ((features // 2, features), F32),
            ],
            flops=4 * window * square, moved=4 * square,
        )
        got = swapped(send, 0, 1)
        parts = call(
            pair_kernel, "pair",
            [((block, features), F32)] + [((block, features), BF16)] * (groups - 1),
            [keep, got], flops=square, moved=4 * square,
        )
        parts = [parts[0]] + [swapped(parts[k], 2 * k, 0) for k in range(1, groups)]
        (d_wkv_t,) = call(total_kernel, "total", [((block, features), F32)], parts)
    else:
        odd = lax.rem(lax.axis_index("band"), 2) == 1
        low = jnp.where(odd, pair[rows - R :], outer)
        high = jnp.where(odd, outer, pair[:R])
        normed_window = jnp.concatenate([low, normed, high], axis=0)
        d_wkv_t = lax.psum_scatter(
            dot_rows(partial_value, normed_window) * factor,
            ("band", "ens"), scatter_dimension=0, tiled=True,
        )

    (d_grid,) = call(
        finish_kernel, "finish", [((rows, features), BF16)],
        [grid_latent, src_gain, d_own, d_inner, d_outer], [((rows, features), F32)],
        flops=20 * rows * features, moved=8 * rows * features,
    )
    return (updated[None], d_grid[None], d_wkv_t)


def solution(mesh):
    return jax.shard_map(
        per_device,
        mesh=mesh,
        in_specs=(
            P("ens", "band", None),
            P("ens", "band", None),
            P("ens", "band", None),
            P(),
            P(),
            P(),
            P(),
            P("band", None),
            P("band", None),
        ),
        out_specs=(P("ens", "band", None), P("ens", "band", None), P(("band", "ens"), None)),
        check_vma=False,
    )
```

time: 106 us -> 78.2 us (0.74)
  waiting for transfers between devices: 41.1 us -> 20.3 us
  starting transfers between devices: 26.8 us -> 17.2 us
  Pallas kernels: 28.9 us -> 35 us
  local copies, waits for them, and re-layouts: 5.94 us -> 4.37 us
  other arithmetic: 1.56 us -> 0 us
    ppermute x17 -> x14, waiting for transfers between devices: 41.1 us -> 20.3 us  [the longest x12 10.3 us: swapped(): return lax.ppermute(value, ('band', 'ens'), pairs)]
    ppermute x17 -> x14, starting transfers between devices: 26.8 us -> 17.2 us  [the longest x12 12.5 us: swapped(): return lax.ppermute(value, ('band', 'ens'), pairs)]
    pallas_call x7 -> x10, Pallas kernels: 28.9 us -> 35 us  [call(): pl.pallas_call(kernel, out_shape=[jax.ShapeDtypeStruct(*shape) for shape...]
    unnamed x50 -> x28, local copies, waits for them, and re-layouts: 5.06 us -> 4.37 us
  transfers between devices with their start and end apart: 17 -> 14, of which waited for: 7 -> 5; matrix products, arithmetic and copies ran while one was open for 4% -> 0% of each run, Pallas kernels for 12% -> 32%
where the time goes in v2:
time: 78.2 us; the launch traced here: 77.5 us
  Pallas kernels  35 us (45%)
  waiting for transfers between devices  20.3 us (26%)
  starting transfers between devices  17.2 us (22%)
  local copies, waits for them, and re-layouts  4.37 us (6%)
    pallas_call x10, Pallas kernels, call(): pl.pallas_call(kernel, out_shape=[jax.ShapeDtypeStruct(*shape) for shape...  35 us
    ppermute x12, starting transfers between devices, swapped(): return lax.ppermute(value, ('band', 'ens'), pairs)  12.5 us
    ppermute x12, waiting for transfers between devices, swapped(): return lax.ppermute(value, ('band', 'ens'), pairs)  10.3 us
    ppermute x2, waiting for transfers between devices, outward(): return lax.ppermute(value, 'band', pairs + [(j, i) for i, j in pairs])  10 us
    ppermute x2, starting transfers between devices, outward(): return lax.ppermute(value, 'band', pairs + [(j, i) for i, j in pairs])  4.63 us
    unnamed x28, local copies, waits for them, and re-layouts  4.37 us
  transfers between devices with their start and end apart: 14, of which 5 were waited for; matrix products, arithmetic and copies ran while one was open for 0% of the time, Pallas kernels for 32%

profile of v2, /device:TPU:16, one launch (start us, length us, event | category | flops | bytes accessed | tf_op | source)
XLA Modules:
  0.0 77.5 jit_solution(9158512418605634168)
XLA Ops:
  0.6 1.9 %norm.1 = (bf16[128,1024]{1,0:T(8,128)(2,1)}, bf16[32,1024]{1,0:T(8,128)(2,1)}) custom-call(bf16[128,1024]{1,0:T(8,128)(2,1)} %bitcast.9, f32[1,1024]{1,0:T(1,128)} %bitcast.14), custom_call_target="tpu_custom_call" | custom-call | flops 1310720 | bytes 524288 | tf_op jit(solution)/shard_map/norm/pallas_call | solution.py:278
  2.5 1.5 %collective-permute-start.1 = (bf16[128,1024]{1,0:T(8,128)(2,1)}, bf16[128,1024]{1,0:T(8,128)(2,1)S(1)}, u32[]{:S(2)}, u32[]{:S(2)}) collective-permute-start(bf16[128,1024]{1,0:T(8,128)(2,1)} %get-tuple-element.23.normed_ref.refs_4_), channel_id=1, source_target_pairs={{0,4},{1,5},{2,6},{3,7},{4,0},{5,1},{6,2},{7,3},{8,12},{9,13},{10,... | collective-permute-start | bytes 786440 | tf_op jit(solution)/shard_map/ppermute | solution.py:265
  4.0 2.3 %collective-permute-start = (bf16[32,1024]{1,0:T(8,128)(2,1)}, bf16[32,1024]{1,0:T(8,128)(2,1)S(1)}, u32[]{:S(2)}, u32[]{:S(2)}) collective-permute-start(bf16[32,1024]{1,0:T(8,128)(2,1)} %get-tuple-element.22), channel_id=1, source_target_pairs={{4,8},{12,16},{20,24},{8,4},{16,12},{24,20},{5,9},{13,17},{21,25},... | collective-permute-start | bytes 196616 | tf_op jit(solution)/shard_map/ppermute | solution.py:271
  6.4 5.0 %collective-permute-done.outer_ref.refs_5_ = bf16[32,1024]{1,0:T(8,128)(2,1)S(1)} collective-permute-done((bf16[32,1024]{1,0:T(8,128)(2,1)}, bf16[32,1024]{1,0:T(8,128)(2,1)S(1)}, u32[]{:S(2)}, u32[]{:S(2)}) %collective-permute-start) | collective-permute-done | bytes 65568 | tf_op jit(solution)/shard_map/ppermute | solution.py:271
  11.4 0.0 copy-start.5
  11.4 0.5 collective-permute-start.2
  11.9 1.5 %collective-permute-start.8 = (bf16[128,1024]{1,0:T(8,128)(2,1)}, bf16[128,1024]{1,0:T(8,128)(2,1)S(1)}, u32[]{:S(2)}, u32[]{:S(2)}) collective-permute-start(bf16[128,1024]{1,0:T(8,128)(2,1)} %get-tuple-element.23.normed_ref.refs_4_), channel_id=1, source_target_pairs={{0,2},{1,3},{2,0},{3,1},{4,6},{5,7},{6,4},{7,5},{8,10},{9,11},{10,... | collective-permute-start | bytes 786440 | tf_op jit(solution)/shard_map/ppermute | solution.py:265
  13.4 2.6 %query.1.q_ref = bf16[32,1024]{1,0:T(8,128)(2,1)} custom-call(bf16[32,1024]{1,0:T(8,128)(2,1)} %bitcast.12, f32[1,1024]{1,0:T(1,128)} %bitcast.16, bf16[1024,1024]{1,0:T(8,128)(2,1)} %wq_ref.1), custom_call_target="tpu_custom_call" | custom-call | flops 67108864 | bytes 2097152 | tf_op jit(solution)/shard_map/query/pallas_call | solution.py:278
  16.1 4.5 %own.1.kv_ref = bf16[128,2048]{1,0:T(8,128)(2,1)} custom-call(bf16[128,1024]{1,0:T(8,128)(2,1)} %get-tuple-element.23.normed_ref.refs_4_, bf16[1024,2048]{1,0:T(8,128)(2,1)} %wkv_ref.5), custom_call_target="tpu_custom_call" | custom-call | flops 536870912 | bytes 4194304 | tf_op jit(solution)/shard_map/own/pallas_call | solution.py:278
  20.6 0.0 collective-permute-done.2.far_ref.refs_7_
  20.6 0.0 copy-start.6
  20.6 0.0 collective-permute-done.1.pair_ref.refs_6_
  20.6 0.0 copy-done.5
  20.6 0.6 copy-done.6
  21.2 0.0 copy-start.1
  21.2 0.7 copy-done.1
  21.9 4.5 %halo.1 = (bf16[64,2048]{1,0:T(8,128)(2,1)}, bf16[192,1024]{1,0:T(8,128)(2,1)}) custom-call(bf16[32,1024]{1,0:T(8,128)(2,1)} %copy-done.5, bf16[128,1024]{1,0:T(8,128)(2,1)} %copy-done.1, bf16[32,1024]{1,0:T(8,128)(2,1)} %copy-done.6, bf16[1024,2048]{1,0:T(8,128)(2,1)} %wkv_ref.5), custom_call_target="tpu_custom_call" | custom-call | flops 268435456 | bytes 4194304 | tf_op jit(solution)/shard_map/halo/pallas_call | solution.py:278
  26.4 0.5 collective-permute-start.9
  26.9 6.0 %attend.1 = (bf16[32,1024]{1,0:T(8,128)(2,1)}, bf16[192,2048]{1,0:T(8,128)(2,1)}, bf16[192,512]{1,0:T(8,128)(2,1)}, bf16[192,512]{1,0:T(8,128)(2,1)}, bf16[192,5...) custom-call(bf16[64,2048]{1,0:T(8,128)(2,1)} %get-tuple-element.24.halo_ref, bf16[128,2048]{1,0:T(8,128)(2,1)} %own.1.kv_ref, ...), custom_call_target="tpu_custom_call" | custom-call | flops 3000000000 | bytes 4194304 | tf_op jit(solution)/shard_map/attend/pallas_call | solution.py:278
  33.0 1.5 %collective-permute-start.5 = (bf16[192,512]{1,0:T(8,128)(2,1)}, bf16[192,512]{1,0:T(8,128)(2,1)S(1)}, u32[]{:S(2)}, u32[]{:S(2)}) collective-permute-start(bf16[192,512]{1,0:T(8,128)(2,1)} %get-tuple-element.31), channel_id=1, source_target_pairs={{0,2},{1,3},{2,0},{3,1},{4,6},{5,7},{6,4},{7,5},{8,10},{9,11},{10,... | collective-permute-start | bytes 589832 | tf_op jit(solution)/shard_map/ppermute | solution.py:265
  34.5 1.5 %collective-permute-start.6 = (bf16[192,512]{1,0:T(8,128)(2,1)}, bf16[192,512]{1,0:T(8,128)(2,1)S(1)}, u32[]{:S(2)}, u32[]{:S(2)}) collective-permute-start(bf16[192,512]{1,0:T(8,128)(2,1)} %get-tuple-element.32), channel_id=1, source_target_pairs={{0,4},{1,5},{2,6},{3,7},{4,0},{5,1},{6,2},{7,3},{8,12},{9,13},{10,... | collective-permute-start | bytes 589832 | tf_op jit(solution)/shard_map/ppermute | solution.py:265
  36.0 0.5 collective-permute-start.7
  36.5 0.0 collective-permute-done.8.refs_8_
  36.5 0.0 copy-start.10
  36.5 7.5 %collective-permute-done.5.refs_1_ = bf16[192,512]{1,0:T(8,128)(2,1)S(1)} collective-permute-done((bf16[192,512]{1,0:T(8,128)(2,1)}, bf16[192,512]{1,0:T(8,128)(2,1)S(1)}, u32[]{:S(2)}, u32[]{:S(2)}) %collective-permute-start.5) | collective-permute-done | bytes 196640 | tf_op jit(solution)/shard_map/ppermute | solution.py:265
  43.9 0.0 copy-start.11
  43.9 0.0 collective-permute-done.6.refs_2_
  43.9 0.0 copy-start.12
  43.9 0.0 collective-permute-done.7.refs_3_
  43.9 0.0 copy-start.13
  43.9 0.0 collective-permute-done.9.refs_9_
  44.0 0.0 copy-start.9
  44.0 0.0 copy-done.10
  44.0 0.6 copy-done.11
  44.6 0.1 copy-done.12
  44.7 0.1 copy-done.13
  44.7 0.1 copy-done.9
  44.9 4.2 %product.1 = (f32[4,64,1024]{2,1,0:T(8,128)}, bf16[4,64,1024]{2,1,0:T(8,128)(2,1)}) custom-call(bf16[192,512]{1,0:T(8,128)(2,1)} %get-tuple-element.30.refs_0_, bf16[192,512]{1,0:T(8,128)(2,1)} %copy-done.11, bf16[192,512]{1,0:T(8,128)(2,1)} %copy-done.12, bf16[192,512]{1,0:T(8,128)(2,1)} %copy-done.13, ...), custom_call_target="tpu_custom_call" | custom-call | flops 805306368 | bytes 4194304 | tf_op jit(solution)/shard_map/product/pallas_call | solution.py:278
  49.1 0.0 collective-permute-start.10
  49.1 2.1 %collective-permute-done.10.got_ref = bf16[4,64,1024]{2,1,0:T(8,128)(2,1)S(1)} collective-permute-done((bf16[4,64,1024]{2,1,0:T(8,128)(2,1)}, bf16[4,64,1024]{2,1,0:T(8,128)(2,1)S(1)}, u32[]{:S(2)}, u32[]{:S(2)}) %collective-permute-start.10) | collective-permute-done | bytes 524320 | tf_op jit(solution)/shard_map/ppermute | solution.py:265
  51.2 0.0 copy-start
  51.2 0.8 %copy-done = bf16[4,64,1024]{2,1,0:T(8,128)(2,1)} copy-done((bf16[4,64,1024]{2,1,0:T(8,128)(2,1)}, bf16[4,64,1024]{2,1,0:T(8,128)(2,1)S(1)}, u32[]{:S(2)}) %copy-start) | copy-done | bytes 524312
  52.0 2.2 %pair.1 = (f32[64,1024]{1,0:T(8,128)}, bf16[64,1024]{1,0:T(8,128)(2,1)}, bf16[64,1024]{1,0:T(8,128)(2,1)}, bf16[64,1024]{1,0:T(8,128)(2,1)}) custom-call(f32[4,64,1024]{2,1,0:T(8,128)} %get-tuple-element.35.keep_ref, bf16[4,64,1024]{2,1,0:T(8,128)(2,1)} %copy-done), custom_call_target="tpu_custom_call" | custom-call | flops 1048576 | bytes 4194304 | tf_op jit(solution)/shard_map/pair/pallas_call | solution.py:278
  54.3 1.3 %collective-permute-start.11 = (bf16[64,1024]{1,0:T(8,128)(2,1)}, bf16[64,1024]{1,0:T(8,128)(2,1)S(1)}, u32[]{:S(2)}, u32[]{:S(2)}) collective-permute-start(bf16[64,1024]{1,0:T(8,128)(2,1)} %get-tuple-element.38), channel_id=1, source_target_pairs={{0,8},{1,9},{2,10},{3,11},{4,12},{5,13},{6,14},{7,15},{8,0},{9,1},... | collective-permute-start | bytes 393224 | tf_op jit(solution)/shard_map/ppermute | solution.py:265
  55.6 0.6 collective-permute-start.12
  56.2 1.6 %collective-permute-start.13 = (bf16[64,1024]{1,0:T(8,128)(2,1)}, bf16[64,1024]{1,0:T(8,128)(2,1)S(1)}, u32[]{:S(2)}, u32[]{:S(2)}) collective-permute-start(bf16[64,1024]{1,0:T(8,128)(2,1)} %get-tuple-element.40), channel_id=1, source_target_pairs={{0,24},{1,25},{2,26},{3,27},{4,28},{5,29},{6,30},{7,31},{8,16},{9,... | collective-permute-start | bytes 393224 | tf_op jit(solution)/shard_map/ppermute | solution.py:265
  57.7 4.8 %window.1 = (f32[128,1024]{1,0:T(8,128)}, bf16[32,1024]{1,0:T(8,128)(2,1)}, bf16[32,1024]{1,0:T(8,128)(2,1)}) custom-call(bf16[192,2048]{1,0:T(8,128)(2,1)} %get-tuple-element.26.partial_ref, bf16[1024,2048]{1,0:T(8,128)(2,1)} %wkv_ref.5), custom_call_target="tpu_custom_call" | custom-call | flops 805306368 | bytes 4194304 | tf_op jit(solution)/shard_map/window/pallas_call | solution.py:278
  62.5 1.5 %collective-permute-start.3 = (bf16[32,1024]{1,0:T(8,128)(2,1)}, bf16[32,1024]{1,0:T(8,128)(2,1)S(1)}, u32[]{:S(2)}, u32[]{:S(2)}) collective-permute-start(bf16[32,1024]{1,0:T(8,128)(2,1)} %get-tuple-element.28), channel_id=1, source_target_pairs={{0,4},{1,5},{2,6},{3,7},{4,0},{5,1},{6,2},{7,3},{8,12},{9,13},{10,... | collective-permute-start | bytes 196616 | tf_op jit(solution)/shard_map/ppermute | solution.py:265
  64.0 2.3 %collective-permute-start.4 = (bf16[32,1024]{1,0:T(8,128)(2,1)}, bf16[32,1024]{1,0:T(8,128)(2,1)S(1)}, u32[]{:S(2)}, u32[]{:S(2)}) collective-permute-start(bf16[32,1024]{1,0:T(8,128)(2,1)} %get-tuple-element.29), channel_id=1, source_target_pairs={{4,8},{12,16},{20,24},{8,4},{16,12},{24,20},{5,9},{13,17},{21,25},... | collective-permute-start | bytes 196616 | tf_op jit(solution)/shard_map/ppermute | solution.py:271
  66.3 0.7 collective-permute-done.3.inner_ref
  67.0 0.0 copy-start.7
  67.0 5.0 %collective-permute-done.4.outer_ref = bf16[32,1024]{1,0:T(8,128)(2,1)S(1)} collective-permute-done((bf16[32,1024]{1,0:T(8,128)(2,1)}, bf16[32,1024]{1,0:T(8,128)(2,1)S(1)}, u32[]{:S(2)}, u32[]{:S(2)}) %collective-permute-start.4) | collective-permute-done | bytes 65568 | tf_op jit(solution)/shard_map/ppermute | solution.py:271
  72.0 0.0 copy-done.7
  72.0 0.6 copy-done.8
  72.6 2.3 %finish.1 = bf16[128,1024]{1,0:T(8,128)(2,1)} custom-call(bf16[128,1024]{1,0:T(8,128)(2,1)} %bitcast.10, f32[1,1024]{1,0:T(1,128)} %bitcast.15, f32[128,1024]{1,0:T(8,128)} %get-tuple-element.27.own_ref, bf16[32,1024]{1,0:T(8,128)(2,1)} %copy-done.7, bf16[32,1024]{1,0:T(8,128)(2,1)} %copy-done.8), custom_call_target="tpu_custom_call" | custom-call | flops 2621440 | bytes 1048576 | tf_op jit(solution)/shard_map/finish/pallas_call | solution.py:278
  74.9 0.0 collective-permute-done.11.refs_1_
  74.9 0.0 collective-permute-done.12.refs_2_
  74.9 0.0 copy-start.3
  74.9 0.0 collective-permute-done.13.refs_3_
  75.0 0.0 copy-start.4
  75.0 0.6 copy-done.2
  75.6 0.0 copy-done.3
  75.6 0.1 copy-done.4
  75.7 1.9 %total.1 = f32[64,1024]{1,0:T(8,128)} custom-call(f32[64,1024]{1,0:T(8,128)} %get-tuple-element.37.refs_0_, bf16[64,1024]{1,0:T(8,128)(2,1)} %copy-done.2, bf16[64,1024]{1,0:T(8,128)(2,1)} %copy-done.3, bf16[64,1024]{1,0:T(8,128)(2,1)} %copy-done.4), custom_call_target="tpu_custom_call" | custom-call | tf_op jit(solution)/shard_map/total/pallas_call | solution.py:278
  (2 shorter events, 0.0 us)
Async XLA Ops:
  2.5 18.1 %collective-permute-start.1 = (bf16[128,1024]{1,0:T(8,128)(2,1)}, bf16[128,1024]{1,0:T(8,128)(2,1)S(1)}, u32[]{:S(2)}, u32[]{:S(2)}) collective-permute-start(bf16[128,1024]{1,0:T(8,128)(2,1)} %get-tuple-element.23.normed_ref.refs_4_), channel_id=1, source_target_pairs={{0,4},{1,5},{2,6},{3,7},{4,0},{5,1},{6,2},{7,3},{8,12},{9,13},{10,... | collective-permute-start | bytes 786440 | tf_op jit(solution)/shard_map/ppermute | solution.py:265
  4.0 7.4 %collective-permute-start = (bf16[32,1024]{1,0:T(8,128)(2,1)}, bf16[32,1024]{1,0:T(8,128)(2,1)S(1)}, u32[]{:S(2)}, u32[]{:S(2)}) collective-permute-start(bf16[32,1024]{1,0:T(8,128)(2,1)} %get-tuple-element.22), channel_id=1, source_target_pairs={{4,8},{12,16},{20,24},{8,4},{16,12},{24,20},{5,9},{13,17},{21,25},... | collective-permute-start | bytes 196616 | tf_op jit(solution)/shard_map/ppermute | solution.py:271
  11.4 9.2 %copy-start.5 = (bf16[32,1024]{1,0:T(8,128)(2,1)}, bf16[32,1024]{1,0:T(8,128)(2,1)S(1)}, u32[]{:S(2)}) copy-start(bf16[32,1024]{1,0:T(8,128)(2,1)S(1)} %collective-permute-done.outer_ref.refs_5_) | copy-start | bytes 196612
  11.4 9.2 %collective-permute-start.2 = (bf16[32,1024]{1,0:T(8,128)(2,1)S(1)}, bf16[32,1024]{1,0:T(8,128)(2,1)S(1)}, u32[]{:S(2)}, u32[]{:S(2)}) collective-permute-start(bf16[32,1024]{1,0:T(8,128)(2,1)S(1)} %collective-permute-done.outer_ref.refs_5_), channel_id=1, source_target_pairs={{0,4},{1,5},{2,6},{3,7},{4,0},{5,1},{6,2},{7,3},{8,12},{9,13},{10,... | collective-permute-start | bytes 196616 | tf_op jit(solution)/shard_map/ppermute | solution.py:265
  11.9 24.5 %collective-permute-start.8 = (bf16[128,1024]{1,0:T(8,128)(2,1)}, bf16[128,1024]{1,0:T(8,128)(2,1)S(1)}, u32[]{:S(2)}, u32[]{:S(2)}) collective-permute-start(bf16[128,1024]{1,0:T(8,128)(2,1)} %get-tuple-element.23.normed_ref.refs_4_), channel_id=1, source_target_pairs={{0,2},{1,3},{2,0},{3,1},{4,6},{5,7},{6,4},{7,5},{8,10},{9,11},{10,... | collective-permute-start | bytes 786440 | tf_op jit(solution)/shard_map/ppermute | solution.py:265
  20.6 0.6 copy-start.6
  21.2 0.7 copy-start.1
  26.4 17.5 %collective-permute-start.9 = (bf16[192,1024]{1,0:T(8,128)(2,1)}, bf16[192,1024]{1,0:T(8,128)(2,1)S(1)}, u32[]{:S(2)}, u32[]{:S(2)}) collective-permute-start(bf16[192,1024]{1,0:T(8,128)(2,1)} %get-tuple-element.34), channel_id=1, source_target_pairs={{0,2},{1,3},{2,0},{3,1},{4,6},{5,7},{6,4},{7,5},{8,10},{9,11},{10,... | collective-permute-start | bytes 1179656 | tf_op jit(solution)/shard_map/ppermute | solution.py:265
  33.0 11.0 %collective-permute-start.5 = (bf16[192,512]{1,0:T(8,128)(2,1)}, bf16[192,512]{1,0:T(8,128)(2,1)S(1)}, u32[]{:S(2)}, u32[]{:S(2)}) collective-permute-start(bf16[192,512]{1,0:T(8,128)(2,1)} %get-tuple-element.31), channel_id=1, source_target_pairs={{0,2},{1,3},{2,0},{3,1},{4,6},{5,7},{6,4},{7,5},{8,10},{9,11},{10,... | collective-permute-start | bytes 589832 | tf_op jit(solution)/shard_map/ppermute | solution.py:265
  34.5 9.4 %collective-permute-start.6 = (bf16[192,512]{1,0:T(8,128)(2,1)}, bf16[192,512]{1,0:T(8,128)(2,1)S(1)}, u32[]{:S(2)}, u32[]{:S(2)}) collective-permute-start(bf16[192,512]{1,0:T(8,128)(2,1)} %get-tuple-element.32), channel_id=1, source_target_pairs={{0,4},{1,5},{2,6},{3,7},{4,0},{5,1},{6,2},{7,3},{8,12},{9,13},{10,... | collective-permute-start | bytes 589832 | tf_op jit(solution)/shard_map/ppermute | solution.py:265
  36.0 7.9 %collective-permute-start.7 = (bf16[192,512]{1,0:T(8,128)(2,1)}, bf16[192,512]{1,0:T(8,128)(2,1)S(1)}, u32[]{:S(2)}, u32[]{:S(2)}) collective-permute-start(bf16[192,512]{1,0:T(8,128)(2,1)} %get-tuple-element.33), channel_id=1, source_target_pairs={{0,6},{1,7},{2,4},{3,5},{4,2},{5,3},{6,0},{7,1},{8,14},{9,15},{10,... | collective-permute-start | bytes 589832 | tf_op jit(solution)/shard_map/ppermute | solution.py:265
  36.5 7.5 %copy-start.10 = (bf16[128,1024]{1,0:T(8,128)(2,1)}, bf16[128,1024]{1,0:T(8,128)(2,1)S(1)}, u32[]{:S(2)}) copy-start(bf16[128,1024]{1,0:T(8,128)(2,1)S(1)} %collective-permute-done.8.refs_8_) | copy-start | bytes 786436
  43.9 0.7 copy-start.11
  43.9 0.8 copy-start.12
  43.9 0.8 %copy-start.13 = (bf16[192,512]{1,0:T(8,128)(2,1)}, bf16[192,512]{1,0:T(8,128)(2,1)S(1)}, u32[]{:S(2)}) copy-start(bf16[192,512]{1,0:T(8,128)(2,1)S(1)} %collective-permute-done.7.refs_3_) | copy-start | bytes 589828
  44.0 0.9 %copy-start.9 = (bf16[192,1024]{1,0:T(8,128)(2,1)}, bf16[192,1024]{1,0:T(8,128)(2,1)S(1)}, u32[]{:S(2)}) copy-start(bf16[192,1024]{1,0:T(8,128)(2,1)S(1)} %collective-permute-done.9.refs_9_) | copy-start | bytes 1179652
  49.1 2.1 %collective-permute-start.10 = (bf16[4,64,1024]{2,1,0:T(8,128)(2,1)}, bf16[4,64,1024]{2,1,0:T(8,128)(2,1)S(1)}, u32[]{:S(2)}, u32[]{:S(2)}) collective-permute-start(bf16[4,64,1024]{2,1,0:T(8,128)(2,1)} %get-tuple-element.36), channel_id=1, source_target_pairs={{0,1},{1,0},{2,3},{3,2},{4,5},{5,4},{6,7},{7,6},{8,9},{9,8},{10,11... | collective-permute-start | bytes 1572872 | tf_op jit(solution)/shard_map/ppermute | solution.py:265
  51.2 0.8 %copy-start = (bf16[4,64,1024]{2,1,0:T(8,128)(2,1)}, bf16[4,64,1024]{2,1,0:T(8,128)(2,1)S(1)}, u32[]{:S(2)}) copy-start(bf16[4,64,1024]{2,1,0:T(8,128)(2,1)S(1)} %collective-permute-done.10.got_ref) | copy-start | bytes 1572868
  54.3 20.7 %collective-permute-start.11 = (bf16[64,1024]{1,0:T(8,128)(2,1)}, bf16[64,1024]{1,0:T(8,128)(2,1)S(1)}, u32[]{:S(2)}, u32[]{:S(2)}) collective-permute-start(bf16[64,1024]{1,0:T(8,128)(2,1)} %get-tuple-element.38), channel_id=1, source_target_pairs={{0,8},{1,9},{2,10},{3,11},{4,12},{5,13},{6,14},{7,15},{8,0},{9,1},... | collective-permute-start | bytes 393224 | tf_op jit(solution)/shard_map/ppermute | solution.py:265
  55.6 19.3 %collective-permute-start.12 = (bf16[64,1024]{1,0:T(8,128)(2,1)}, bf16[64,1024]{1,0:T(8,128)(2,1)S(1)}, u32[]{:S(2)}, u32[]{:S(2)}) collective-permute-start(bf16[64,1024]{1,0:T(8,128)(2,1)} %get-tuple-element.39), channel_id=1, source_target_pairs={{0,16},{1,17},{2,18},{3,19},{4,20},{5,21},{6,22},{7,23},{8,24},{9,... | collective-permute-start | bytes 393224 | tf_op jit(solution)/shard_map/ppermute | solution.py:265
  56.2 18.8 %collective-permute-start.13 = (bf16[64,1024]{1,0:T(8,128)(2,1)}, bf16[64,1024]{1,0:T(8,128)(2,1)S(1)}, u32[]{:S(2)}, u32[]{:S(2)}) collective-permute-start(bf16[64,1024]{1,0:T(8,128)(2,1)} %get-tuple-element.40), channel_id=1, source_target_pairs={{0,24},{1,25},{2,26},{3,27},{4,28},{5,29},{6,30},{7,31},{8,16},{9,... | collective-permute-start | bytes 393224 | tf_op jit(solution)/shard_map/ppermute | solution.py:265
  62.5 4.5 %collective-permute-start.3 = (bf16[32,1024]{1,0:T(8,128)(2,1)}, bf16[32,1024]{1,0:T(8,128)(2,1)S(1)}, u32[]{:S(2)}, u32[]{:S(2)}) collective-permute-start(bf16[32,1024]{1,0:T(8,128)(2,1)} %get-tuple-element.28), channel_id=1, source_target_pairs={{0,4},{1,5},{2,6},{3,7},{4,0},{5,1},{6,2},{7,3},{8,12},{9,13},{10,... | collective-permute-start | bytes 196616 | tf_op jit(solution)/shard_map/ppermute | solution.py:265
  64.0 8.0 %collective-permute-start.4 = (bf16[32,1024]{1,0:T(8,128)(2,1)}, bf16[32,1024]{1,0:T(8,128)(2,1)S(1)}, u32[]{:S(2)}, u32[]{:S(2)}) collective-permute-start(bf16[32,1024]{1,0:T(8,128)(2,1)} %get-tuple-element.29), channel_id=1, source_target_pairs={{4,8},{12,16},{20,24},{8,4},{16,12},{24,20},{5,9},{13,17},{21,25},... | collective-permute-start | bytes 196616 | tf_op jit(solution)/shard_map/ppermute | solution.py:271
  67.0 5.0 %copy-start.7 = (bf16[32,1024]{1,0:T(8,128)(2,1)}, bf16[32,1024]{1,0:T(8,128)(2,1)S(1)}, u32[]{:S(2)}) copy-start(bf16[32,1024]{1,0:T(8,128)(2,1)S(1)} %collective-permute-done.3.inner_ref) | copy-start | bytes 196612
  72.0 0.6 copy-start.8
  74.9 0.7 copy-start.2
  74.9 0.7 copy-start.3
  75.0 0.7 copy-start.4

commit v3 on v2

--- a/solution.py
+++ b/solution.py
@@ -12,6 +12,7 @@
 K = 12
 R = 32
 EPSILON = 1e-05
+LIMIT = 24 << 20
 F32 = jnp.float32
 BF16 = jnp.bfloat16
 
@@ -65,42 +66,18 @@
     edge_ref[...] = normed_ref[pl.ds(start, R)]
 
 
-def query_kernel(hidden_ref, gain_ref, wq_ref, q_ref, hat_ref):
-    @pl.when(pl.program_id(0) == 0)
-    def _():
-        standard, _ = normalize(hidden_ref[...])
-        hat_ref[...] = (standard * gain_ref[...]).astype(BF16)
-
-    q_ref[...] = dot(hat_ref[...], wq_ref[...]).astype(BF16)
-
-
-def own_kernel(normed_ref, wkv_ref, kv_ref):
+def project_kernel(hidden_ref, gain_ref, wq_ref, normed_ref, wkv_ref, q_ref, kv_ref):
+    standard, _ = normalize(hidden_ref[...])
+    hat = (standard * gain_ref[...]).astype(BF16)
+    q_ref[...] = dot(hat, wq_ref[...]).astype(BF16)
     kv_ref[...] = dot(normed_ref[...], wkv_ref[...]).astype(BF16)
 
 
-def halo_kernel(outer_ref, pair_ref, far_ref, wkv_ref, kv_ref, shared_ref, both_ref):
-    rows = pair_ref.shape[0]
-
-    @pl.when(pl.program_id(0) == 0)
-    def _():
-        odd = parity()
-        outer_at = pl.multiple_of(pick(odd, R, 0), R)
-        inner_at = pl.multiple_of(pick(odd, 0, R), R)
-        from_at = pl.multiple_of(pick(odd, rows - R, 0), R)
-        both_ref[pl.ds(outer_at, R)] = outer_ref[...]
-        both_ref[pl.ds(inner_at, R)] = pair_ref[pl.ds(from_at, R)]
-        shared_ref[:rows] = pair_ref[...]
-        shared_ref[rows : rows + R] = outer_ref[...]
-        shared_ref[rows + R :] = far_ref[...]
-
-    kv_ref[...] = dot(both_ref[...], wkv_ref[...]).astype(BF16)
-
-
 def attend_kernel(
-    halo_ref, kv_ref, q_ref, cot_ref, hidden_ref, index_ref, mask_ref, updated_ref, partial_ref,
-    *refs
+    outer_ref, pair_ref, wkv_ref, kv_ref, q_ref, cot_ref, hidden_ref, index_ref, mask_ref,
+    updated_ref, partial_ref, *refs
 ):
-    piece_refs, window_ref = refs[:-1], refs[-1]
+    piece_refs, (both_ref, halo_ref, window_ref) = refs[:-3], refs[-3:]
     nodes, features = q_ref.shape
     own = kv_ref.shape[0]
     rows = own + 2 * R
@@ -108,6 +85,13 @@
     head_dim = features // HEADS
     shift = head_dim.bit_length() - 1
     scale = 1.0 / math.sqrt(head_dim)
+    odd = parity()
+    outer_at = pl.multiple_of(pick(odd, R, 0), R)
+    inner_at = pl.multiple_of(pick(odd, 0, R), R)
+    from_at = pl.multiple_of(pick(odd, own - R, 0), R)
+    both_ref[pl.ds(outer_at, R)] = outer_ref[...]
+    both_ref[pl.ds(inner_at, R)] = pair_ref[pl.ds(from_at, R)]
+    halo_ref[...] = dot(both_ref[...], wkv_ref[...]).astype(BF16)
     window_ref[:R] = halo_ref[:R]
     window_ref[R : R + own] = kv_ref[...]
     window_ref[R + own :] = halo_ref[R:]
@@ -174,11 +158,24 @@
             dot_rows(picks, first) + dot_rows(picks, second)
         ).astype(BF16)
 
-    mine = 2 * parity() + lax.axis_index("ens") // 2
+    mine = 2 * odd + lax.axis_index("ens") // 2
+    core = lax.rem(lax.axis_index("ens"), 2)
+    half = lanes // 2
+    left = lax.broadcasted_iota(jnp.int32, (rows, lanes), 1) < half
     for k, piece_ref in enumerate(piece_refs):
-        for i in range(piece_ref.shape[1] // lanes):
-            start = pl.multiple_of((4 * i + (mine ^ k)) * lanes, lanes)
-            piece_ref[:, i * lanes : (i + 1) * lanes] = partial_ref[:, pl.ds(start, lanes)]
+        count = piece_ref.shape[1] // lanes
+        for i in range(count // 2):
+            tiles = []
+            for t in (2 * i, 2 * i + 1):
+                start = pl.multiple_of((4 * t + (mine ^ k)) * lanes, lanes)
+                tiles.append(partial_ref[:, pl.ds(start, lanes)].astype(F32))
+            one, two = tiles
+            firsts = jnp.where(left, one, pltpu.roll(two, half, 1)).astype(BF16)
+            seconds = jnp.where(left, pltpu.roll(one, half, 1), two).astype(BF16)
+            first_at = pl.multiple_of((pick(core, 0, count // 2) + i) * lanes, lanes)
+            second_at = pl.multiple_of((pick(core, count // 2, 0) + i) * lanes, lanes)
+            piece_ref[:, pl.ds(first_at, lanes)] = firsts
+            piece_ref[:, pl.ds(second_at, lanes)] = seconds
 
 
 def window_kernel(partial_ref, wkv_ref, own_ref, inner_ref, outer_ref, wide_ref):
@@ -192,9 +189,10 @@
     outer_ref[...] = wide_ref[pl.ds(outer_at, R)].astype(BF16)
 
 
-def product_kernel(factor, *refs):
+def product_kernel(factor, start, *refs):
     lefts, (own, outer, pair, far, side, side_pair) = refs[:4], refs[4:10]
-    keep_ref, send_ref, left_ref, right_ref, total_ref = refs[10:]
+    out_ref, left_ref, right_ref = refs[10:]
+    columns = left_ref.shape[1]
     window = lefts[0].shape[0]
     rows = own.shape[0]
     odd = parity()
@@ -206,7 +204,7 @@
     )
     for k, ((middle, m_at), (edge, e_at), (other, o_at)) in enumerate(pieces):
         base = k * window
-        left_ref[base : base + window] = lefts[k][...]
+        left_ref[base : base + window] = lefts[k][:, start : start + columns]
         right_ref[base + R : base + R + rows] = middle[m_at : m_at + rows]
         flag = odd if k < 2 else 1 - odd
         edge_at = pl.multiple_of(base + pick(flag, R + rows, 0), R)
@@ -214,20 +212,15 @@
         from_at = pl.multiple_of(o_at + pick(flag, rows - R, 0), R)
         right_ref[pl.ds(edge_at, R)] = edge[e_at : e_at + R]
         right_ref[pl.ds(other_at, R)] = other[pl.ds(from_at, R)]
-    total_ref[...] = dot_rows(left_ref[...], right_ref[...]) * factor
-    core = lax.rem(lax.axis_index("ens"), 2)
-    block = keep_ref.shape[1]
-    for i in range(keep_ref.shape[0]):
-        keep_at = pl.multiple_of((2 * i + core) * block, block)
-        send_at = pl.multiple_of((2 * i + 1 - core) * block, block)
-        keep_ref[i] = total_ref[pl.ds(keep_at, block)]
-        send_ref[i] = total_ref[pl.ds(send_at, block)].astype(BF16)
+    total = dot_rows(left_ref[...], right_ref[...]) * factor
+    out_ref[...] = total.astype(out_ref.dtype)
 
 
 def pair_kernel(keep_ref, got_ref, *out_refs):
     group = lax.axis_index("band") // 2
+    block = out_refs[0].shape[0]
     for k, out_ref in enumerate(out_refs):
-        at = group ^ k
+        at = pl.ds(pl.multiple_of((group ^ k) * block, block), block)
         out_ref[...] = (keep_ref[at] + got_ref[at].astype(F32)).astype(out_ref.dtype)
 
 
@@ -271,6 +264,12 @@
     return lax.ppermute(value, "band", pairs + [(j, i) for i, j in pairs])
 
 
+def beyond(value):
+    bands = lax.axis_size("band")
+    pairs = [(i, i + 2) for i in range(1, bands - 2, 2)]
+    return lax.ppermute(value, "band", pairs + [(i + 2, i) for i in range(0, bands - 2, 2)])
+
+
 def call(kernel, name, shapes, operands, scratch=(), flops=0, moved=0, **options):
     if "in_specs" not in options:
         options["in_specs"] = [spec()] * len(operands)
@@ -280,22 +279,10 @@
         out_shape=[jax.ShapeDtypeStruct(*shape) for shape in shapes],
         scratch_shapes=[pltpu.VMEM(*shape) for shape in scratch],
         cost_estimate=estimate(flops, moved),
+        compiler_params=pltpu.CompilerParams(vmem_limit_bytes=LIMIT),
         name=name,
         **options,
     )(*operands)
-
-
-def streamed(kernel, name, steps, fixed, weight, shapes, scratch, flops):
-    features, columns = weight.shape
-    wide = columns // steps
-    whole = [pl.BlockSpec(value.shape, lambda i: (0, 0)) for value in fixed]
-    out = [pl.BlockSpec((shapes[0][0][0], wide), lambda i: (0, i))]
-    out += [pl.BlockSpec(shape[0], lambda i: (0, 0)) for shape in shapes[1:]]
-    return call(
-        kernel, name, shapes, [*fixed, weight], scratch, flops, 2 * features * columns,
-        grid=(steps,), in_specs=whole + [pl.BlockSpec((features, wide), lambda i: (0, i))],
-        out_specs=out,
-    )
 
 
 def per_device(grid_latent, hidden, d_updated, w_kv, w_q, src_gain, q_gain, src_index, edge_mask):
@@ -318,31 +305,26 @@
     pair = swapped(normed, 1, 0)
     if grouped:
         side = swapped(normed, 0, 2)
-    far = swapped(outer, 1, 0)
-
-    (queries,) = streamed(
-        query_kernel, "query", 2, [hidden, q_gain], w_q, [((nodes, features), BF16)],
-        [((nodes, features), BF16)], 2 * nodes * square,
-    )
-    (kv,) = streamed(
-        own_kernel, "own", 4, [normed], w_kv, [((rows, 2 * features), BF16)], [],
-        4 * rows * square,
-    )
-    kv_halo, shared = streamed(
-        halo_kernel, "halo", 4, [outer, pair, far], w_kv,
-        [((2 * R, 2 * features), BF16), ((window, features), BF16)],
-        [((2 * R, features), BF16)], 8 * R * square,
+    far = beyond(edge)
+
+    queries, kv = call(
+        project_kernel, "project", [((nodes, features), BF16), ((rows, 2 * features), BF16)],
+        [hidden, q_gain, w_q, normed, w_kv], flops=2 * (2 * rows + nodes) * square, moved=6 * square,
     )
     if grouped:
-        side_pair = swapped(shared, 0, 2)
+        side_pair = swapped(jnp.concatenate([pair, outer, far], axis=0), 0, 2)
 
     pieces = 4 if grouped else 0
     updated, partial_value, *lefts = call(
         attend_kernel, "attend",
         [((nodes, features), BF16), ((window, 2 * features), BF16)]
         + [((window, features // 2), BF16)] * pieces,
-        [kv_halo, kv, queries, d_updated, hidden, src_index.T, edge_mask.T],
-        [((window, 2 * features), BF16)], flops=3e9, moved=4 * square,
+        [outer, pair, w_kv, kv, queries, d_updated, hidden, src_index.T, edge_mask.T],
+        [
+            ((2 * R, features), BF16), ((2 * R, 2 * features), BF16),
+            ((window, 2 * features), BF16),
+        ],
+        flops=3e9, moved=4 * square,
     )
     if grouped:
         lefts = [lefts[0], swapped(lefts[1], 0, 2), swapped(lefts[2], 1, 0), swapped(lefts[3], 1, 2)]
@@ -358,18 +340,20 @@
 
     factor = 1.0 / math.sqrt(members * rows * bands)
     if grouped:
-        keep, send = call(
-            functools.partial(product_kernel, factor), "product",
-            [((groups, block, features), F32), ((groups, block, features), BF16)],
-            [*lefts, normed, outer, pair, far, side, side_pair],
-            [
-                ((4 * window, features // 2), BF16),
-                ((4 * window, features), BF16),
-                ((features // 2, features), F32),
-            ],
-            flops=4 * window * square, moved=4 * square,
+        operands = [*lefts, normed, outer, pair, far, side, side_pair]
+        columns = features // 4
+        buffers = [((4 * window, columns), BF16), ((4 * window, features), BF16)]
+        (send,) = call(
+            functools.partial(product_kernel, factor, 0), "product_send",
+            [((columns, features), BF16)], operands, buffers,
+            flops=2 * window * square, moved=4 * square,
         )
         got = swapped(send, 0, 1)
+        (keep,) = call(
+            functools.partial(product_kernel, factor, columns), "product_keep",
+            [((columns, features), F32)], operands, buffers,
+            flops=2 * window * square, moved=4 * square,
+        )
         parts = call(
             pair_kernel, "pair",
             [((block, features), F32)] + [((block, features), BF16)] * (groups - 1),

time: 78.2 us -> 58.9 us (0.75)
  Pallas kernels: 35 us -> 11.7 us
  starting transfers between devices: 17.2 us -> 20.9 us
  local copies, waits for them, and re-layouts: 4.37 us -> 7.66 us
  waiting for transfers between devices: 20.3 us -> 17.5 us
    pallas_call x10 -> x9, Pallas kernels: 35 us -> 11.7 us  [call(): pl.pallas_call(kernel, out_shape=[jax.ShapeDtypeStruct(*shape) for shape...]
    unnamed x28 -> x22, local copies, waits for them, and re-layouts: 4.37 us -> 7.66 us
    ppermute x2, waiting for transfers between devices: 10 us -> 7.86 us  [outward(): return lax.ppermute(value, 'band', pairs + [(j, i) for i, j in pairs])]
    ppermute x0 -> x1, starting transfers between devices: none -> 1.95 us  [beyond(): lax.ppermute(value, 'band', pairs + [(i + 2, i) for i in range(0, bands -...]
    ppermute x12 -> x11, starting transfers between devices: 12.5 us -> 13.5 us  [swapped(): return lax.ppermute(value, ('band', 'ens'), pairs)]
    ppermute x2, starting transfers between devices: 4.63 us -> 5.42 us  [outward(): return lax.ppermute(value, 'band', pairs + [(j, i) for i, j in pairs])]
    ppermute x12 -> x11, waiting for transfers between devices: 10.3 us -> 9.62 us  [swapped(): return lax.ppermute(value, ('band', 'ens'), pairs)]
  transfers between devices with their start and end apart: 14 -> 14, of which waited for: 5 -> 3; matrix products, arithmetic and copies ran while one was open for 0% -> 0% of each run, Pallas kernels for 32% -> 17%
where the time goes in v3:
time: 58.9 us; the launch traced here: 58.5 us
  starting transfers between devices  20.9 us (35%)
  waiting for transfers between devices  17.5 us (30%)
  Pallas kernels  11.7 us (20%)
  local copies, waits for them, and re-layouts  7.66 us (13%)
  between operations  0.78 us (1%)
    ppermute x11, starting transfers between devices, swapped(): return lax.ppermute(value, ('band', 'ens'), pairs)  13.5 us
    pallas_call x9, Pallas kernels, call(): pl.pallas_call(kernel, out_shape=[jax.ShapeDtypeStruct(*shape) for shape...  11.7 us
    ppermute x11, waiting for transfers between devices, swapped(): return lax.ppermute(value, ('band', 'ens'), pairs)  9.62 us
    ppermute x2, waiting for transfers between devices, outward(): return lax.ppermute(value, 'band', pairs + [(j, i) for i, j in pairs])  7.86 us
    unnamed x22, local copies, waits for them, and re-layouts  7.66 us
    ppermute x2, starting transfers between devices, outward(): return lax.ppermute(value, 'band', pairs + [(j, i) for i, j in pairs])  5.42 us
    ppermute x1, starting transfers between devices, beyond(): lax.ppermute(value, 'band', pairs + [(i + 2, i) for i in range(0, bands -...  1.95 us
  transfers between devices with their start and end apart: 14, of which 3 were waited for; matrix products, arithmetic and copies ran while one was open for 0% of the time, Pallas kernels for 17%

profile of v3, /device:TPU:16, one launch (start us, length us, event | category | flops | bytes accessed | tf_op | source)
XLA Modules:
  0.0 58.5 jit_solution(4636950924592630819)
XLA Ops:
  0.6 0.0 copy-start.3
  0.6 0.9 %copy-done.3 = bf16[1,128,1024]{2,1,0:T(8,128)(2,1)S(1)} copy-done((bf16[1,128,1024]{2,1,0:T(8,128)(2,1)S(1)}, bf16[1,128,1024]{2,1,0:T(8,128)(2,1)}, u32[]{:S(2)}) %copy-start.3) | copy-done | bytes 262168
  1.6 0.0 copy-start.6
  1.6 0.7 %copy-done.6 = f32[1024]{0:T(1024)S(1)} copy-done((f32[1024]{0:T(1024)S(1)}, f32[1024]{0:T(1024)}, u32[]{:S(2)}) %copy-start.6) | copy-done | bytes 4120
  2.3 0.0 copy-start.8
  2.3 0.0 copy-start.9
  2.3 0.0 copy-start.10
  2.3 0.3 norm.1
  2.5 1.6 %collective-permute-start.1 = (bf16[128,1024]{1,0:T(8,128)(2,1)S(1)}, bf16[128,1024]{1,0:T(8,128)(2,1)S(1)}, u32[]{:S(2)}, u32[]{:S(2)}) collective-permute-start(bf16[128,1024]{1,0:T(8,128)(2,1)S(1)} %get-tuple-element.21.normed_ref.refs_4_), channel_id=1, source_target_pairs={{0,4},{1,5},{2,6},{3,7},{4,0},{5,1},{6,2},{7,3},{8,12},{9,13},{10,... | collective-permute-start | bytes 786440 | tf_op jit(solution)/shard_map/ppermute | solution.py:258
  4.1 2.3 %collective-permute-start = (bf16[32,1024]{1,0:T(8,128)(2,1)S(1)}, bf16[32,1024]{1,0:T(8,128)(2,1)S(1)}, u32[]{:S(2)}, u32[]{:S(2)}) collective-permute-start(bf16[32,1024]{1,0:T(8,128)(2,1)S(1)} %get-tuple-element.20), channel_id=1, source_target_pairs={{4,8},{12,16},{20,24},{8,4},{16,12},{24,20},{5,9},{13,17},{21,25},... | collective-permute-start | bytes 196616 | tf_op jit(solution)/shard_map/ppermute | solution.py:264
  6.4 2.0 %collective-permute-start.7 = (bf16[32,1024]{1,0:T(8,128)(2,1)S(1)}, bf16[32,1024]{1,0:T(8,128)(2,1)S(1)}, u32[]{:S(2)}, u32[]{:S(2)}) collective-permute-start(bf16[32,1024]{1,0:T(8,128)(2,1)S(1)} %get-tuple-element.20), channel_id=1, source_target_pairs={{4,12},{12,20},{20,28},{8,0},{16,8},{24,16},{5,13},{13,21},{21,29}... | collective-permute-start | bytes 196616 | tf_op jit(solution)/shard_map/ppermute | solution.py:270
  8.4 2.0 %collective-permute-start.8 = (bf16[128,1024]{1,0:T(8,128)(2,1)S(1)}, bf16[128,1024]{1,0:T(8,128)(2,1)S(1)}, u32[]{:S(2)}, u32[]{:S(2)}) collective-permute-start(bf16[128,1024]{1,0:T(8,128)(2,1)S(1)} %get-tuple-element.21.normed_ref.refs_4_), channel_id=1, source_target_pairs={{0,2},{1,3},{2,0},{3,1},{4,6},{5,7},{6,4},{7,5},{8,10},{9,11},{10,... | collective-permute-start | bytes 786440 | tf_op jit(solution)/shard_map/ppermute | solution.py:258
  10.4 0.0 copy-start
  10.4 2.2 %copy-done = bf16[1024,2048]{1,0:T(8,128)(2,1)S(1)} copy-done((bf16[1024,2048]{1,0:T(8,128)(2,1)S(1)}, bf16[1024,2048]{1,0:T(8,128)(2,1)}, u32[]{:S(2)}) %copy-start) | copy-done | bytes 4194328
  12.6 0.0 copy-start.2
  12.6 1.6 %copy-done.2 = bf16[1024,1024]{1,0:T(8,128)(2,1)S(1)} copy-done((bf16[1024,1024]{1,0:T(8,128)(2,1)S(1)}, bf16[1024,1024]{1,0:T(8,128)(2,1)}, u32[]{:S(2)}) %copy-start.2) | copy-done | bytes 2097176
  14.1 0.0 copy-start.5
  14.2 0.8 %copy-done.5 = bf16[1,32,1024]{2,1,0:T(8,128)(2,1)S(1)} copy-done((bf16[1,32,1024]{2,1,0:T(8,128)(2,1)S(1)}, bf16[1,32,1024]{2,1,0:T(8,128)(2,1)}, u32[]{:S(2)}) %copy-start.5) | copy-done | bytes 65560
  15.0 0.0 copy-start.7
  15.0 0.7 %copy-done.7 = f32[1024]{0:T(1024)S(1)} copy-done((f32[1024]{0:T(1024)S(1)}, f32[1024]{0:T(1024)}, u32[]{:S(2)}) %copy-start.7) | copy-done | bytes 4120
  15.7 0.0 copy-start.1
  15.7 1.2 %project.1 = (bf16[32,1024]{1,0:T(8,128)(2,1)S(1)}, bf16[128,2048]{1,0:T(8,128)(2,1)S(1)}) custom-call(bf16[32,1024]{1,0:T(8,128)(2,1)S(1)} %bitcast.11, f32[1,1024]{1,0:T(1,128)S(1)} %bitcast.15, bf16[1024,1024]{1,0:T(8,128)(2,1)S(1)} %copy-done.2, bf16[128,1024]{1,0:T(8,128)(2,1)S(1)} %get-tuple-element.21.normed_ref.refs_4_, bf16[1024,2048]{1,0:T(8,128)(2,1)S(1)} %copy-done), custom_call_target="tpu_custom_call" | custom-call | flops 603979776 | bytes 6291456 | tf_op jit(solution)/shard_map/project/pallas_call | solution.py:277
  16.9 0.0 collective-permute-done.outer_ref.refs_5_
  16.9 0.0 collective-permute-done.7.refs_7_
  16.9 0.0 collective-permute-done.1.pair_ref.refs_6_
  17.0 0.2 collective-permute-start.9
  17.2 0.0 copy-done.8
  17.2 0.0 copy-done.9
  17.2 0.0 copy-done.10
  17.2 0.7 %copy-done.1 = bf16[1024,2048]{1,0:T(8,128)(2,1)S(1)} copy-done((bf16[1024,2048]{1,0:T(8,128)(2,1)S(1)}, bf16[1024,2048]{1,0:T(8,128)(2,1)}, u32[]{:S(2)}) %copy-start.1) | copy-done | bytes 4194328
  17.9 5.3 %attend.1 = (bf16[32,1024]{1,0:T(8,128)(2,1)}, bf16[192,2048]{1,0:T(8,128)(2,1)S(1)}, bf16[192,512]{1,0:T(8,128)(2,1)S(1)}, bf16[192,512]{1,0:T(8,128)(2,1)S(1)}...) custom-call(bf16[32,1024]{1,0:T(8,128)(2,1)S(1)} %collective-permute-done.outer_ref.refs_5_, ...), custom_call_target="tpu_custom_call" | custom-call | flops 3000000000 | bytes 4194304 | tf_op jit(solution)/shard_map/attend/pallas_call | solution.py:277
  23.2 1.2 %collective-permute-start.4 = (bf16[192,512]{1,0:T(8,128)(2,1)S(1)}, bf16[192,512]{1,0:T(8,128)(2,1)S(1)}, u32[]{:S(2)}, u32[]{:S(2)}) collective-permute-start(bf16[192,512]{1,0:T(8,128)(2,1)S(1)} %get-tuple-element.30), channel_id=1, source_target_pairs={{0,2},{1,3},{2,0},{3,1},{4,6},{5,7},{6,4},{7,5},{8,10},{9,11},{10,... | collective-permute-start | bytes 589832 | tf_op jit(solution)/shard_map/ppermute | solution.py:258
  24.5 2.2 %collective-permute-start.5 = (bf16[192,512]{1,0:T(8,128)(2,1)S(1)}, bf16[192,512]{1,0:T(8,128)(2,1)S(1)}, u32[]{:S(2)}, u32[]{:S(2)}) collective-permute-start(bf16[192,512]{1,0:T(8,128)(2,1)S(1)} %get-tuple-element.31), channel_id=1, source_target_pairs={{0,4},{1,5},{2,6},{3,7},{4,0},{5,1},{6,2},{7,3},{8,12},{9,13},{10,... | collective-permute-start | bytes 589832 | tf_op jit(solution)/shard_map/ppermute | solution.py:258
  26.6 0.2 collective-permute-start.6
  26.9 0.0 collective-permute-done.8.refs_8_
  26.9 8.3 %collective-permute-done.4.refs_1_ = bf16[192,512]{1,0:T(8,128)(2,1)S(1)} collective-permute-done((bf16[192,512]{1,0:T(8,128)(2,1)S(1)}, bf16[192,512]{1,0:T(8,128)(2,1)S(1)}, u32[]{:S(2)}, u32[]{:S(2)}) %collective-permute-start.4) | collective-permute-done | bytes 196640 | tf_op jit(solution)/shard_map/ppermute | solution.py:258
  35.2 0.0 collective-permute-done.5.refs_2_
  35.2 0.0 collective-permute-done.6.refs_3_
  35.2 0.0 collective-permute-done.9.refs_9_
  35.2 0.7 %product_send.1 = bf16[256,1024]{1,0:T(8,128)(2,1)S(1)} custom-call(bf16[192,512]{1,0:T(8,128)(2,1)S(1)} %get-tuple-element.29.refs_0_, bf16[192,512]{1,0:T(8,128)(2,1)S(1)} %collective-permute-done.4.refs_1_, bf16[192,512]{1,0:T(8,128)(2,1)S(1)} %collective-permute-done.5.refs_2_, bf16[192,512]{1,0:T(8,128)(2,1)S(1)} %collective-permute-done.6.refs_3_, ...), custom_call_target="tpu_custom_call" | custom-call | flops 402653184 | bytes 4194304 | tf_op jit(solution)/shard_map/product_send/pallas_call | solution.py:277
  35.9 0.0 copy-start.4
  35.9 0.1 collective-permute-start.10
  36.0 0.6 %product_keep.1.keep_ref = f32[256,1024]{1,0:T(8,128)S(1)} custom-call(bf16[192,512]{1,0:T(8,128)(2,1)S(1)} %get-tuple-element.29.refs_0_, bf16[192,512]{1,0:T(8,128)(2,1)S(1)} %collective-permute-done.4.refs_1_, bf16[192,512]{1,0:T(8,128)(2,1)S(1)} %collective-permute-done.5.refs_2_, bf16[192,512]{1,0:T(8,128)(2,1)S(1)} %collective-permute-done.6.refs_3_, ...), custom_call_target="tpu_custom_call" | custom-call | flops 402653184 | bytes 4194304 | tf_op jit(solution)/shard_map/product_keep/pallas_call | solution.py:277
  36.6 1.3 %collective-permute-done.10.got_ref = bf16[256,1024]{1,0:T(8,128)(2,1)S(1)} collective-permute-done((bf16[256,1024]{1,0:T(8,128)(2,1)S(1)}, bf16[256,1024]{1,0:T(8,128)(2,1)S(1)}, u32[]{:S(2)}, u32[]{:S(2)}) %collective-permute-start.10) | collective-permute-done | bytes 524320 | tf_op jit(solution)/shard_map/ppermute | solution.py:258
  37.9 0.1 pair.1
  38.0 1.6 %collective-permute-start.11 = (bf16[64,1024]{1,0:T(8,128)(2,1)S(1)}, bf16[64,1024]{1,0:T(8,128)(2,1)S(1)}, u32[]{:S(2)}, u32[]{:S(2)}) collective-permute-start(bf16[64,1024]{1,0:T(8,128)(2,1)S(1)} %get-tuple-element.34), channel_id=1, source_target_pairs={{0,8},{1,9},{2,10},{3,11},{4,12},{5,13},{6,14},{7,15},{8,0},{9,1},... | collective-permute-start | bytes 393224 | tf_op jit(solution)/shard_map/ppermute | solution.py:258
  39.6 1.2 %collective-permute-start.12 = (bf16[64,1024]{1,0:T(8,128)(2,1)S(1)}, bf16[64,1024]{1,0:T(8,128)(2,1)S(1)}, u32[]{:S(2)}, u32[]{:S(2)}) collective-permute-start(bf16[64,1024]{1,0:T(8,128)(2,1)S(1)} %get-tuple-element.35), channel_id=1, source_target_pairs={{0,16},{1,17},{2,18},{3,19},{4,20},{5,21},{6,22},{7,23},{8,24},{9,... | collective-permute-start | bytes 393224 | tf_op jit(solution)/shard_map/ppermute | solution.py:258
  40.9 0.7 %collective-permute-start.13 = (bf16[64,1024]{1,0:T(8,128)(2,1)S(1)}, bf16[64,1024]{1,0:T(8,128)(2,1)S(1)}, u32[]{:S(2)}, u32[]{:S(2)}) collective-permute-start(bf16[64,1024]{1,0:T(8,128)(2,1)S(1)} %get-tuple-element.36), channel_id=1, source_target_pairs={{0,24},{1,25},{2,26},{3,27},{4,28},{5,29},{6,30},{7,31},{8,16},{9,... | collective-permute-start | bytes 393224 | tf_op jit(solution)/shard_map/ppermute | solution.py:258
  41.5 1.5 %window.1 = (f32[128,1024]{1,0:T(8,128)S(1)}, bf16[32,1024]{1,0:T(8,128)(2,1)S(1)}, bf16[32,1024]{1,0:T(8,128)(2,1)S(1)}) custom-call(bf16[192,2048]{1,0:T(8,128)(2,1)S(1)} %get-tuple-element.25.partial_ref, bf16[1024,2048]{1,0:T(8,128)(2,1)S(1)} %copy-done.1), custom_call_target="tpu_custom_call" | custom-call | flops 805306368 | bytes 4194304 | tf_op jit(solution)/shard_map/window/pallas_call | solution.py:277
  43.1 2.5 %collective-permute-start.2 = (bf16[32,1024]{1,0:T(8,128)(2,1)S(1)}, bf16[32,1024]{1,0:T(8,128)(2,1)S(1)}, u32[]{:S(2)}, u32[]{:S(2)}) collective-permute-start(bf16[32,1024]{1,0:T(8,128)(2,1)S(1)} %get-tuple-element.27), channel_id=1, source_target_pairs={{0,4},{1,5},{2,6},{3,7},{4,0},{5,1},{6,2},{7,3},{8,12},{9,13},{10,... | collective-permute-start | bytes 196616 | tf_op jit(solution)/shard_map/ppermute | solution.py:258
  45.6 3.1 %collective-permute-start.3 = (bf16[32,1024]{1,0:T(8,128)(2,1)S(1)}, bf16[32,1024]{1,0:T(8,128)(2,1)S(1)}, u32[]{:S(2)}, u32[]{:S(2)}) collective-permute-start(bf16[32,1024]{1,0:T(8,128)(2,1)S(1)} %get-tuple-element.28), channel_id=1, source_target_pairs={{4,8},{12,16},{20,24},{8,4},{16,12},{24,20},{5,9},{13,17},{21,25},... | collective-permute-start | bytes 196616 | tf_op jit(solution)/shard_map/ppermute | solution.py:264
  48.7 0.0 collective-permute-done.2.inner_ref
  48.7 7.9 %collective-permute-done.3.outer_ref = bf16[32,1024]{1,0:T(8,128)(2,1)S(1)} collective-permute-done((bf16[32,1024]{1,0:T(8,128)(2,1)S(1)}, bf16[32,1024]{1,0:T(8,128)(2,1)S(1)}, u32[]{:S(2)}, u32[]{:S(2)}) %collective-permute-start.3) | collective-permute-done | bytes 65568 | tf_op jit(solution)/shard_map/ppermute | solution.py:264
  56.6 0.0 copy-done.4
  56.6 1.1 %finish.1 = bf16[128,1024]{1,0:T(8,128)(2,1)} custom-call(bf16[128,1024]{1,0:T(8,128)(2,1)S(1)} %bitcast.10, f32[1,1024]{1,0:T(1,128)S(1)} %bitcast.14, f32[128,1024]{1,0:T(8,128)S(1)} %get-tuple-element.26.own_ref, bf16[32,1024]{1,0:T(8,128)(2,1)S(1)} %collective-permute-done.2.inner_ref, bf16[32,1024]{1,0:T(8,128)(2,1)S(1)} %collective-permute-done.3.outer_ref), custom_call_target="tpu_custom_call" | custom-call | flops 2621440 | bytes 1048576 | tf_op jit(solution)/shard_map/finish/pallas_call | solution.py:277
  57.7 0.0 collective-permute-done.11.refs_1_
  57.7 0.0 collective-permute-done.12.refs_2_
  57.7 0.0 collective-permute-done.13.refs_3_
  57.7 0.8 %total.1 = f32[64,1024]{1,0:T(8,128)} custom-call(f32[64,1024]{1,0:T(8,128)S(1)} %get-tuple-element.33.refs_0_, bf16[64,1024]{1,0:T(8,128)(2,1)S(1)} %collective-permute-done.11.refs_1_, bf16[64,1024]{1,0:T(8,128)(2,1)S(1)} %collective-permute-done.12.refs_2_, bf16[64,1024]{1,0:T(8,128)(2,1)S(1)} %collective-permute-done.13.refs_3_), custom_call_target="tpu_custom_call" | custom-call | tf_op jit(solution)/shard_map/total/pallas_call | solution.py:277
  (1 shorter events, 0.0 us)
Async XLA Ops:
  0.6 1.0 %copy-start.3 = (bf16[1,128,1024]{2,1,0:T(8,128)(2,1)S(1)}, bf16[1,128,1024]{2,1,0:T(8,128)(2,1)}, u32[]{:S(2)}) copy-start(bf16[1,128,1024]{2,1,0:T(8,128)(2,1)} %param.9) | copy-start | bytes 786436
  1.6 0.7 %copy-start.6 = (f32[1024]{0:T(1024)S(1)}, f32[1024]{0:T(1024)}, u32[]{:S(2)}) copy-start(f32[1024]{0:T(1024)} %param.14) | copy-start | bytes 12292
  2.3 14.9 %copy-start.8 = (bf16[1,32,1024]{2,1,0:T(8,128)(2,1)S(1)}, bf16[1,32,1024]{2,1,0:T(8,128)(2,1)}, u32[]{:S(2)}) copy-start(bf16[1,32,1024]{2,1,0:T(8,128)(2,1)} %param.11) | copy-start | bytes 196612
  2.3 14.9 %copy-start.9 = (s32[32,12]{0,1:T(8,128)S(1)}, s32[32,12]{0,1:T(8,128)}, u32[]{:S(2)}) copy-start(s32[32,12]{0,1:T(8,128)} %param.16) | copy-start | bytes 4612
  2.3 14.9 %copy-start.10 = (s32[32,12]{0,1:T(8,128)S(1)}, s32[32,12]{0,1:T(8,128)}, u32[]{:S(2)}) copy-start(s32[32,12]{0,1:T(8,128)} %param.17) | copy-start | bytes 4612
  2.5 14.4 %collective-permute-start.1 = (bf16[128,1024]{1,0:T(8,128)(2,1)S(1)}, bf16[128,1024]{1,0:T(8,128)(2,1)S(1)}, u32[]{:S(2)}, u32[]{:S(2)}) collective-permute-start(bf16[128,1024]{1,0:T(8,128)(2,1)S(1)} %get-tuple-element.21.normed_ref.refs_4_), channel_id=1, source_target_pairs={{0,4},{1,5},{2,6},{3,7},{4,0},{5,1},{6,2},{7,3},{8,12},{9,13},{10,... | collective-permute-start | bytes 786440 | tf_op jit(solution)/shard_map/ppermute | solution.py:258
  4.1 12.8 %collective-permute-start = (bf16[32,1024]{1,0:T(8,128)(2,1)S(1)}, bf16[32,1024]{1,0:T(8,128)(2,1)S(1)}, u32[]{:S(2)}, u32[]{:S(2)}) collective-permute-start(bf16[32,1024]{1,0:T(8,128)(2,1)S(1)} %get-tuple-element.20), channel_id=1, source_target_pairs={{4,8},{12,16},{20,24},{8,4},{16,12},{24,20},{5,9},{13,17},{21,25},... | collective-permute-start | bytes 196616 | tf_op jit(solution)/shard_map/ppermute | solution.py:264
  6.4 10.5 %collective-permute-start.7 = (bf16[32,1024]{1,0:T(8,128)(2,1)S(1)}, bf16[32,1024]{1,0:T(8,128)(2,1)S(1)}, u32[]{:S(2)}, u32[]{:S(2)}) collective-permute-start(bf16[32,1024]{1,0:T(8,128)(2,1)S(1)} %get-tuple-element.20), channel_id=1, source_target_pairs={{4,12},{12,20},{20,28},{8,0},{16,8},{24,16},{5,13},{13,21},{21,29}... | collective-permute-start | bytes 196616 | tf_op jit(solution)/shard_map/ppermute | solution.py:270
  8.4 18.5 %collective-permute-start.8 = (bf16[128,1024]{1,0:T(8,128)(2,1)S(1)}, bf16[128,1024]{1,0:T(8,128)(2,1)S(1)}, u32[]{:S(2)}, u32[]{:S(2)}) collective-permute-start(bf16[128,1024]{1,0:T(8,128)(2,1)S(1)} %get-tuple-element.21.normed_ref.refs_4_), channel_id=1, source_target_pairs={{0,2},{1,3},{2,0},{3,1},{4,6},{5,7},{6,4},{7,5},{8,10},{9,11},{10,... | collective-permute-start | bytes 786440 | tf_op jit(solution)/shard_map/ppermute | solution.py:258
  10.4 2.2 %copy-start = (bf16[1024,2048]{1,0:T(8,128)(2,1)S(1)}, bf16[1024,2048]{1,0:T(8,128)(2,1)}, u32[]{:S(2)}) copy-start(bf16[1024,2048]{1,0:T(8,128)(2,1)} %wkv_ref.5) | copy-start | bytes 12582916
  12.6 1.6 %copy-start.2 = (bf16[1024,1024]{1,0:T(8,128)(2,1)S(1)}, bf16[1024,1024]{1,0:T(8,128)(2,1)}, u32[]{:S(2)}) copy-start(bf16[1024,1024]{1,0:T(8,128)(2,1)} %wq_ref.1) | copy-start | bytes 6291460
  14.1 0.8 %copy-start.5 = (bf16[1,32,1024]{2,1,0:T(8,128)(2,1)S(1)}, bf16[1,32,1024]{2,1,0:T(8,128)(2,1)}, u32[]{:S(2)}) copy-start(bf16[1,32,1024]{2,1,0:T(8,128)(2,1)} %param.10) | copy-start | bytes 196612
  15.0 0.7 %copy-start.7 = (f32[1024]{0:T(1024)S(1)}, f32[1024]{0:T(1024)}, u32[]{:S(2)}) copy-start(f32[1024]{0:T(1024)} %param.15) | copy-start | bytes 12292
  15.7 2.2 %copy-start.1 = (bf16[1024,2048]{1,0:T(8,128)(2,1)S(1)}, bf16[1024,2048]{1,0:T(8,128)(2,1)}, u32[]{:S(2)}) copy-start(bf16[1024,2048]{1,0:T(8,128)(2,1)} %wkv_ref.5) | copy-start | bytes 12582916
  17.0 18.2 %collective-permute-start.9 = (bf16[192,1024]{1,0:T(8,128)(2,1)S(1)}, bf16[192,1024]{1,0:T(8,128)(2,1)S(1)}, u32[]{:S(2)}, u32[]{:S(2)}) collective-permute-start(bf16[192,1024]{1,0:T(8,128)(2,1)S(1)} %pad_maximum_fusion), channel_id=1, source_target_pairs={{0,2},{1,3},{2,0},{3,1},{4,6},{5,7},{6,4},{7,5},{8,10},{9,11},{10,... | collective-permute-start | bytes 1179656 | tf_op jit(solution)/shard_map/ppermute | solution.py:258
  23.2 12.0 %collective-permute-start.4 = (bf16[192,512]{1,0:T(8,128)(2,1)S(1)}, bf16[192,512]{1,0:T(8,128)(2,1)S(1)}, u32[]{:S(2)}, u32[]{:S(2)}) collective-permute-start(bf16[192,512]{1,0:T(8,128)(2,1)S(1)} %get-tuple-element.30), channel_id=1, source_target_pairs={{0,2},{1,3},{2,0},{3,1},{4,6},{5,7},{6,4},{7,5},{8,10},{9,11},{10,... | collective-permute-start | bytes 589832 | tf_op jit(solution)/shard_map/ppermute | solution.py:258
  24.5 10.8 %collective-permute-start.5 = (bf16[192,512]{1,0:T(8,128)(2,1)S(1)}, bf16[192,512]{1,0:T(8,128)(2,1)S(1)}, u32[]{:S(2)}, u32[]{:S(2)}) collective-permute-start(bf16[192,512]{1,0:T(8,128)(2,1)S(1)} %get-tuple-element.31), channel_id=1, source_target_pairs={{0,4},{1,5},{2,6},{3,7},{4,0},{5,1},{6,2},{7,3},{8,12},{9,13},{10,... | collective-permute-start | bytes 589832 | tf_op jit(solution)/shard_map/ppermute | solution.py:258
  26.6 8.6 %collective-permute-start.6 = (bf16[192,512]{1,0:T(8,128)(2,1)S(1)}, bf16[192,512]{1,0:T(8,128)(2,1)S(1)}, u32[]{:S(2)}, u32[]{:S(2)}) collective-permute-start(bf16[192,512]{1,0:T(8,128)(2,1)S(1)} %get-tuple-element.32), channel_id=1, source_target_pairs={{0,6},{1,7},{2,4},{3,5},{4,2},{5,3},{6,0},{7,1},{8,14},{9,15},{10,... | collective-permute-start | bytes 589832 | tf_op jit(solution)/shard_map/ppermute | solution.py:258
  35.9 20.7 %copy-start.4 = (bf16[1,128,1024]{2,1,0:T(8,128)(2,1)S(1)}, bf16[1,128,1024]{2,1,0:T(8,128)(2,1)}, u32[]{:S(2)}) copy-start(bf16[1,128,1024]{2,1,0:T(8,128)(2,1)} %param.9) | copy-start | bytes 786436
  35.9 2.0 %collective-permute-start.10 = (bf16[256,1024]{1,0:T(8,128)(2,1)S(1)}, bf16[256,1024]{1,0:T(8,128)(2,1)S(1)}, u32[]{:S(2)}, u32[]{:S(2)}) collective-permute-start(bf16[256,1024]{1,0:T(8,128)(2,1)S(1)} %product_send.1), channel_id=1, source_target_pairs={{0,1},{1,0},{2,3},{3,2},{4,5},{5,4},{6,7},{7,6},{8,9},{9,8},{10,11... | collective-permute-start | bytes 1572872 | tf_op jit(solution)/shard_map/ppermute | solution.py:258
  38.0 19.7 %collective-permute-start.11 = (bf16[64,1024]{1,0:T(8,128)(2,1)S(1)}, bf16[64,1024]{1,0:T(8,128)(2,1)S(1)}, u32[]{:S(2)}, u32[]{:S(2)}) collective-permute-start(bf16[64,1024]{1,0:T(8,128)(2,1)S(1)} %get-tuple-element.34), channel_id=1, source_target_pairs={{0,8},{1,9},{2,10},{3,11},{4,12},{5,13},{6,14},{7,15},{8,0},{9,1},... | collective-permute-start | bytes 393224 | tf_op jit(solution)/shard_map/ppermute | solution.py:258
  39.6 18.1 %collective-permute-start.12 = (bf16[64,1024]{1,0:T(8,128)(2,1)S(1)}, bf16[64,1024]{1,0:T(8,128)(2,1)S(1)}, u32[]{:S(2)}, u32[]{:S(2)}) collective-permute-start(bf16[64,1024]{1,0:T(8,128)(2,1)S(1)} %get-tuple-element.35), channel_id=1, source_target_pairs={{0,16},{1,17},{2,18},{3,19},{4,20},{5,21},{6,22},{7,23},{8,24},{9,... | collective-permute-start | bytes 393224 | tf_op jit(solution)/shard_map/ppermute | solution.py:258
  40.9 16.8 %collective-permute-start.13 = (bf16[64,1024]{1,0:T(8,128)(2,1)S(1)}, bf16[64,1024]{1,0:T(8,128)(2,1)S(1)}, u32[]{:S(2)}, u32[]{:S(2)}) collective-permute-start(bf16[64,1024]{1,0:T(8,128)(2,1)S(1)} %get-tuple-element.36), channel_id=1, source_target_pairs={{0,24},{1,25},{2,26},{3,27},{4,28},{5,29},{6,30},{7,31},{8,16},{9,... | collective-permute-start | bytes 393224 | tf_op jit(solution)/shard_map/ppermute | solution.py:258
  43.1 5.6 %collective-permute-start.2 = (bf16[32,1024]{1,0:T(8,128)(2,1)S(1)}, bf16[32,1024]{1,0:T(8,128)(2,1)S(1)}, u32[]{:S(2)}, u32[]{:S(2)}) collective-permute-start(bf16[32,1024]{1,0:T(8,128)(2,1)S(1)} %get-tuple-element.27), channel_id=1, source_target_pairs={{0,4},{1,5},{2,6},{3,7},{4,0},{5,1},{6,2},{7,3},{8,12},{9,13},{10,... | collective-permute-start | bytes 196616 | tf_op jit(solution)/shard_map/ppermute | solution.py:258
  45.6 11.0 %collective-permute-start.3 = (bf16[32,1024]{1,0:T(8,128)(2,1)S(1)}, bf16[32,1024]{1,0:T(8,128)(2,1)S(1)}, u32[]{:S(2)}, u32[]{:S(2)}) collective-permute-start(bf16[32,1024]{1,0:T(8,128)(2,1)S(1)} %get-tuple-element.28), channel_id=1, source_target_pairs={{4,8},{12,16},{20,24},{8,4},{16,12},{24,20},{5,9},{13,17},{21,25},... | collective-permute-start | bytes 196616 | tf_op jit(solution)/shard_map/ppermute | solution.py:264

commit v4 on v3

--- a/solution.py
+++ b/solution.py
@@ -12,6 +12,7 @@
 K = 12
 R = 32
 EPSILON = 1e-05
+SLOTS = 16
 LIMIT = 24 << 20
 F32 = jnp.float32
 BF16 = jnp.bfloat16
@@ -73,11 +74,19 @@
     kv_ref[...] = dot(normed_ref[...], wkv_ref[...]).astype(BF16)
 
 
+def picked(local, rows):
+    row_id = lax.broadcasted_iota(jnp.int32, (local.shape[0], rows), 1)
+    return jnp.concatenate(
+        [jnp.where(row_id == local[:, k : k + 1], 1.0, 0.0).astype(BF16) for k in range(K)], axis=0
+    )
+
+
 def attend_kernel(
     outer_ref, pair_ref, wkv_ref, kv_ref, q_ref, cot_ref, hidden_ref, index_ref, mask_ref,
     updated_ref, partial_ref, *refs
 ):
     piece_refs, (both_ref, halo_ref, window_ref) = refs[:-3], refs[-3:]
+    piece_ref, packet_refs = piece_refs[:1], piece_refs[1:]
     nodes, features = q_ref.shape
     own = kv_ref.shape[0]
     rows = own + 2 * R
@@ -100,12 +109,10 @@
     eye_b = lax.broadcasted_iota(jnp.int32, (K, lanes), 1)
     eye = jnp.where(eye_a == eye_b, 1.0, 0.0).astype(BF16)
     first_row = lax.axis_index("band") * own - R
-    local = dot_rows((index_ref[...] - first_row).astype(F32).astype(BF16), eye).astype(jnp.int32)
+    rows_low = (index_ref[...] - first_row).astype(F32).astype(BF16)
+    local = dot_rows(rows_low, eye).astype(jnp.int32)
     mask = dot_rows(mask_ref[...].astype(F32).astype(BF16), eye)
-    row_id = lax.broadcasted_iota(jnp.int32, (nodes, rows), 1)
-    picks = jnp.concatenate(
-        [jnp.where(row_id == local[:, k : k + 1], 1.0, 0.0).astype(BF16) for k in range(K)], axis=0
-    )
+    picks = picked(local, rows)
     valid = jnp.concatenate([mask[:, k : k + 1] for k in range(K)], axis=0) > 0.5
     chunk = 256
     feature_id = lax.broadcasted_iota(jnp.int32, (features, lanes), 0)
@@ -136,7 +143,7 @@
     probs = terms / jnp.sum(terms, axis=0, keepdims=True)
     probs_low = probs.reshape(K * nodes, lanes).astype(BF16)
     inner = jnp.sum(probs * d_probs, axis=0, keepdims=True)
-    d_scores = (probs * (d_probs - inner)).reshape(K * nodes, lanes)
+    d_scores = (probs * (d_probs - inner)).reshape(K * nodes, lanes) * scale
     d_first, d_second = halves(d_scores)
 
     for c in range(0, features, chunk):
@@ -152,30 +159,48 @@
             dot_rows(picks, first) + dot_rows(picks, second)
         ).astype(BF16)
         spread = (dot(d_first, heads) + dot(d_second, heads)).reshape(K, nodes, chunk)
-        keys = (spread * repeated(q_ref, c)).reshape(K * nodes, chunk) * scale
-        first, second = halves(keys)
+        first, second = halves((spread * repeated(q_ref, c)).reshape(K * nodes, chunk))
         partial_ref[:, c : c + chunk] = (
             dot_rows(picks, first) + dot_rows(picks, second)
         ).astype(BF16)
 
     mine = 2 * odd + lax.axis_index("ens") // 2
     core = lax.rem(lax.axis_index("ens"), 2)
-    half = lanes // 2
-    left = lax.broadcasted_iota(jnp.int32, (rows, lanes), 1) < half
-    for k, piece_ref in enumerate(piece_refs):
-        count = piece_ref.shape[1] // lanes
-        for i in range(count // 2):
+    def arranged(sources, out_ref, row, group):
+        count = sources[0].shape[0]
+        left = lax.broadcasted_iota(jnp.int32, (count, lanes), 1) < head_dim
+        for i in range(2):
+            source = sources[i % len(sources)]
+            shift_by = i * features if len(sources) == 1 else 0
             tiles = []
-            for t in (2 * i, 2 * i + 1):
-                start = pl.multiple_of((4 * t + (mine ^ k)) * lanes, lanes)
-                tiles.append(partial_ref[:, pl.ds(start, lanes)].astype(F32))
+            for t in range(2):
+                start = pl.multiple_of(shift_by + (4 * t + group) * lanes, lanes)
+                tiles.append(source[:, pl.ds(start, lanes)].astype(F32))
             one, two = tiles
-            firsts = jnp.where(left, one, pltpu.roll(two, half, 1)).astype(BF16)
-            seconds = jnp.where(left, pltpu.roll(one, half, 1), two).astype(BF16)
-            first_at = pl.multiple_of((pick(core, 0, count // 2) + i) * lanes, lanes)
-            second_at = pl.multiple_of((pick(core, count // 2, 0) + i) * lanes, lanes)
-            piece_ref[:, pl.ds(first_at, lanes)] = firsts
-            piece_ref[:, pl.ds(second_at, lanes)] = seconds
+            firsts = jnp.where(left, one, pltpu.roll(two, head_dim, 1)).astype(BF16)
+            seconds = jnp.where(left, pltpu.roll(one, head_dim, 1), two).astype(BF16)
+            first_at = pl.multiple_of((pick(core, 0, 2) + i) * lanes, lanes)
+            second_at = pl.multiple_of((pick(core, 2, 0) + i) * lanes, lanes)
+            out_ref[row : row + count, pl.ds(first_at, lanes)] = firsts
+            out_ref[row : row + count, pl.ds(second_at, lanes)] = seconds
+
+    if piece_ref:
+        arranged([partial_ref], piece_ref[0], 0, mine)
+    row_r = lax.broadcasted_iota(jnp.int32, (SLOTS, lanes), 0)
+    lane_r = lax.broadcasted_iota(jnp.int32, (SLOTS, lanes), 1)
+    keep = jnp.bitwise_and(jnp.right_shift(row_r, 1), 1)
+    head_r = jnp.where(keep == 1, core, 1 - core) + (HEADS // 2) * jnp.bitwise_and(row_r, 1)
+    for k, packet_ref in enumerate(packet_refs):
+        group = mine ^ (k + 1)
+        chosen = lane_r == head_r + 2 * group
+        factors = jnp.zeros((SLOTS, K * nodes), F32)
+        for kind, values in enumerate((probs_low, d_first, d_second)):
+            select = jnp.where(jnp.right_shift(row_r, 2) == kind, jnp.where(chosen, 1.0, 0.0), 0.0)
+            factors = factors + dot_lanes(select.astype(BF16), values)
+        packet_ref[:SLOTS, : K * nodes] = factors.astype(BF16)
+        packet_ref[:SLOTS, K * nodes :] = jnp.zeros((SLOTS, 4 * lanes - K * nodes), BF16)
+        packet_ref[:K, K * nodes : K * nodes + nodes] = rows_low
+        arranged([q_ref, cot_ref], packet_ref, SLOTS, group)
 
 
 def window_kernel(partial_ref, wkv_ref, own_ref, inner_ref, outer_ref, wide_ref):
@@ -192,8 +217,31 @@
 def product_kernel(factor, start, *refs):
     lefts, (own, outer, pair, far, side, side_pair) = refs[:4], refs[4:10]
     out_ref, left_ref, right_ref = refs[10:]
-    columns = left_ref.shape[1]
-    window = lefts[0].shape[0]
+    window, columns = lefts[0].shape[0], left_ref.shape[1]
+    nodes = lefts[1].shape[0] - SLOTS
+    edges, lanes, shift = K * nodes, 128, (columns // 4).bit_length() - 1
+    row_r = lax.broadcasted_iota(jnp.int32, (SLOTS, columns), 0)
+    part = jnp.right_shift(lax.broadcasted_iota(jnp.int32, (SLOTS, columns), 1), shift)
+    kind = jnp.minimum(jnp.right_shift(row_r, 2), 1)
+    wanted = 2 * (start // columns) + jnp.bitwise_and(part, 1)
+    expand = jnp.where(jnp.bitwise_and(row_r, 3) == wanted, 1.0, 0.0)
+    expand = jnp.where(kind == 1 - jnp.right_shift(part, 1), expand, 0.0)
+    expand = jnp.where(row_r < 12, expand, 0.0).astype(BF16)
+    eye_a = lax.broadcasted_iota(jnp.int32, (SLOTS, lanes), 0)
+    eye_b = lax.broadcasted_iota(jnp.int32, (SLOTS, lanes), 1)
+    eye = jnp.where(eye_a == eye_b, 1.0, 0.0).astype(BF16)
+    left_ref[:window] = lefts[0][:, start : start + columns]
+    for k in range(1, 4):
+        packet = lefts[k]
+        if k < 3:
+            local = dot_rows(packet[:SLOTS, edges:], eye)[:nodes].astype(jnp.int32)
+            picks = picked(local, window)
+        spread = dot_rows(packet[:SLOTS, :edges], expand).reshape(K, nodes, columns)
+        given = packet[SLOTS:, start : start + columns].astype(F32)
+        first, second = halves((spread * given[None]).reshape(edges, columns))
+        left_ref[k * window : (k + 1) * window] = (
+            dot_rows(picks, first) + dot_rows(picks, second)
+        ).astype(BF16)
     rows = own.shape[0]
     odd = parity()
     pieces = (
@@ -204,7 +252,6 @@
     )
     for k, ((middle, m_at), (edge, e_at), (other, o_at)) in enumerate(pieces):
         base = k * window
-        left_ref[base : base + window] = lefts[k][:, start : start + columns]
         right_ref[base + R : base + R + rows] = middle[m_at : m_at + rows]
         flag = odd if k < 2 else 1 - odd
         edge_at = pl.multiple_of(base + pick(flag, R + rows, 0), R)
@@ -294,12 +341,13 @@
     block = 2 * features // (bands * members)
     groups = bands // 2
     src_gain, q_gain = src_gain[None], q_gain[None]
-    grouped = members == 4 and groups & (groups - 1) == 0 and block == 64
+    grouped = members == 4 and groups & (groups - 1) == 0 and block == features // HEADS == 64
+    grouped = grouped and features == 8 * 128 and K * nodes + nodes <= features // 2
     square = features * features
 
     normed, edge = call(
         norm_kernel, "norm", [((rows, features), BF16), ((R, features), BF16)],
-        [grid_latent, src_gain], flops=10 * rows * features, moved=4 * rows * features,
+        [grid_latent, src_gain], flops=1e10, moved=4 * rows * features,
     )
     outer = outward(edge)
     pair = swapped(normed, 1, 0)
@@ -314,11 +362,12 @@
     if grouped:
         side_pair = swapped(jnp.concatenate([pair, outer, far], axis=0), 0, 2)
 
-    pieces = 4 if grouped else 0
+    pieces = 1 if grouped else 0
     updated, partial_value, *lefts = call(
         attend_kernel, "attend",
         [((nodes, features), BF16), ((window, 2 * features), BF16)]
-        + [((window, features // 2), BF16)] * pieces,
+        + [((window, features // 2), BF16)] * pieces
+        + [((SLOTS + nodes, features // 2), BF16)] * (3 * pieces),
         [outer, pair, w_kv, kv, queries, d_updated, hidden, src_index.T, edge_mask.T],
         [
             ((2 * R, features), BF16), ((2 * R, 2 * features), BF16),
@@ -340,6 +389,7 @@
 
     factor = 1.0 / math.sqrt(members * rows * bands)
     if grouped:
+        *lefts, _ = lax.optimization_barrier((*lefts, d_own))
         operands = [*lefts, normed, outer, pair, far, side, side_pair]
         columns = features // 4
         buffers = [((4 * window, columns), BF16), ((4 * window, features), BF16)]

time: 58.9 us -> 51.7 us (0.88)
  local copies, waits for them, and re-layouts: 7.66 us -> 1.68 us
  waiting for transfers between devices: 17.5 us -> 13.8 us
  Pallas kernels: 11.7 us -> 13.5 us
  starting transfers between devices: 20.9 us -> 21.7 us
    ppermute x11, waiting for transfers between devices: 9.62 us -> 2.91 us  [swapped(): return lax.ppermute(value, ('band', 'ens'), pairs)]
    unnamed x22, local copies, waits for them, and re-layouts: 7.66 us -> 1.68 us
    ppermute x2, waiting for transfers between devices: 7.86 us -> 10.9 us  [outward(): return lax.ppermute(value, 'band', pairs + [(j, i) for i, j in pairs])]
    pallas_call x9, Pallas kernels: 11.7 us -> 13.5 us  [call(): pl.pallas_call(kernel, out_shape=[jax.ShapeDtypeStruct(*shape) for shape...]
    ppermute x2, starting transfers between devices: 5.42 us -> 6.81 us  [outward(): return lax.ppermute(value, 'band', pairs + [(j, i) for i, j in pairs])]
    ppermute x11, starting transfers between devices: 13.5 us -> 12.4 us  [swapped(): return lax.ppermute(value, ('band', 'ens'), pairs)]
  transfers between devices with their start and end apart: 14 -> 14, of which waited for: 3 -> 6; matrix products, arithmetic and copies ran while one was open for 0% -> 0% of each run, Pallas kernels for 17% -> 21%
where the time goes in v4:
time: 51.7 us; the launch traced here: 51.5 us
  starting transfers between devices  21.7 us (42%)
  waiting for transfers between devices  13.8 us (27%)
  Pallas kernels  13.5 us (26%)
  local copies, waits for them, and re-layouts  1.68 us (3%)
  between operations  0.81 us (2%)
    pallas_call x9, Pallas kernels, call(): pl.pallas_call(kernel, out_shape=[jax.ShapeDtypeStruct(*shape) for shape...  13.5 us
    ppermute x11, starting transfers between devices, swapped(): return lax.ppermute(value, ('band', 'ens'), pairs)  12.4 us
    ppermute x2, waiting for transfers between devices, outward(): return lax.ppermute(value, 'band', pairs + [(j, i) for i, j in pairs])  10.9 us
    ppermute x2, starting transfers between devices, outward(): return lax.ppermute(value, 'band', pairs + [(j, i) for i, j in pairs])  6.81 us
    ppermute x11, waiting for transfers between devices, swapped(): return lax.ppermute(value, ('band', 'ens'), pairs)  2.91 us
    ppermute x1, starting transfers between devices, beyond(): lax.ppermute(value, 'band', pairs + [(i + 2, i) for i in range(0, bands -...  2.48 us
    unnamed x22, local copies, waits for them, and re-layouts  1.68 us
  transfers between devices with their start and end apart: 14, of which 6 were waited for; matrix products, arithmetic and copies ran while one was open for 0% of the time, Pallas kernels for 21%

profile of v4, /device:TPU:16, one launch (start us, length us, event | category | flops | bytes accessed | tf_op | source)
XLA Modules:
  0.0 51.5 jit_solution(11514510124669476080)
XLA Ops:
  0.6 0.0 copy-start.2
  0.6 0.9 %copy-done.2 = bf16[1,128,1024]{2,1,0:T(8,128)(2,1)S(1)} copy-done((bf16[1,128,1024]{2,1,0:T(8,128)(2,1)S(1)}, bf16[1,128,1024]{2,1,0:T(8,128)(2,1)}, u32[]{:S(2)}) %copy-start.2) | copy-done | bytes 262168
  1.6 0.0 copy-start.5
  1.6 0.7 %copy-done.5 = f32[1024]{0:T(1024)S(1)} copy-done((f32[1024]{0:T(1024)S(1)}, f32[1024]{0:T(1024)}, u32[]{:S(2)}) %copy-start.5) | copy-done | bytes 4120
  2.3 0.0 copy-start
  2.3 0.0 copy-start.1
  2.3 0.0 copy-start.4
  2.3 0.0 copy-start.7
  2.3 0.3 norm.1
  2.5 0.0 copy-start.8
  2.6 0.0 copy-start.9
  2.6 0.0 copy-start.10
  2.6 1.6 %collective-permute-start.1 = (bf16[128,1024]{1,0:T(8,128)(2,1)S(1)}, bf16[128,1024]{1,0:T(8,128)(2,1)S(1)}, u32[]{:S(2)}, u32[]{:S(2)}) collective-permute-start(bf16[128,1024]{1,0:T(8,128)(2,1)S(1)} %get-tuple-element.25.normed_ref.refs_4_), channel_id=1, source_target_pairs={{0,4},{1,5},{2,6},{3,7},{4,0},{5,1},{6,2},{7,3},{8,12},{9,13},{10,... | collective-permute-start | bytes 786440 | tf_op jit(solution)/shard_map/ppermute | solution.py:305
  4.1 2.5 %collective-permute-start.7 = (bf16[32,1024]{1,0:T(8,128)(2,1)S(1)}, bf16[32,1024]{1,0:T(8,128)(2,1)S(1)}, u32[]{:S(2)}, u32[]{:S(2)}) collective-permute-start(bf16[32,1024]{1,0:T(8,128)(2,1)S(1)} %get-tuple-element.24), channel_id=1, source_target_pairs={{4,12},{12,20},{20,28},{8,0},{16,8},{24,16},{5,13},{13,21},{21,29}... | collective-permute-start | bytes 196616 | tf_op jit(solution)/shard_map/ppermute | solution.py:317
  6.6 3.6 %collective-permute-start = (bf16[32,1024]{1,0:T(8,128)(2,1)S(1)}, bf16[32,1024]{1,0:T(8,128)(2,1)S(1)}, u32[]{:S(2)}, u32[]{:S(2)}) collective-permute-start(bf16[32,1024]{1,0:T(8,128)(2,1)S(1)} %get-tuple-element.24), channel_id=1, source_target_pairs={{4,8},{12,16},{20,24},{8,4},{16,12},{24,20},{5,9},{13,17},{21,25},... | collective-permute-start | bytes 196616 | tf_op jit(solution)/shard_map/ppermute | solution.py:311
  10.2 1.6 %collective-permute-start.8 = (bf16[128,1024]{1,0:T(8,128)(2,1)S(1)}, bf16[128,1024]{1,0:T(8,128)(2,1)S(1)}, u32[]{:S(2)}, u32[]{:S(2)}) collective-permute-start(bf16[128,1024]{1,0:T(8,128)(2,1)S(1)} %get-tuple-element.25.normed_ref.refs_4_), channel_id=1, source_target_pairs={{0,2},{1,3},{2,0},{3,1},{4,6},{5,7},{6,4},{7,5},{8,10},{9,11},{10,... | collective-permute-start | bytes 786440 | tf_op jit(solution)/shard_map/ppermute | solution.py:305
  11.8 0.0 collective-permute-done.7.refs_7_
  11.8 1.9 %collective-permute-done.outer_ref.refs_5_ = bf16[32,1024]{1,0:T(8,128)(2,1)S(1)} collective-permute-done((bf16[32,1024]{1,0:T(8,128)(2,1)S(1)}, bf16[32,1024]{1,0:T(8,128)(2,1)S(1)}, u32[]{:S(2)}, u32[]{:S(2)}) %collective-permute-start) | collective-permute-done | bytes 65568 | tf_op jit(solution)/shard_map/ppermute | solution.py:311
  13.7 0.0 collective-permute-done.1.pair_ref.refs_6_
  13.7 1.6 %collective-permute-start.9 = (bf16[192,1024]{1,0:T(8,128)(2,1)S(1)}, bf16[192,1024]{1,0:T(8,128)(2,1)S(1)}, u32[]{:S(2)}, u32[]{:S(2)}) collective-permute-start(bf16[192,1024]{1,0:T(8,128)(2,1)S(1)} %pad_maximum_fusion), channel_id=1, source_target_pairs={{0,2},{1,3},{2,0},{3,1},{4,6},{5,7},{6,4},{7,5},{8,10},{9,11},{10,... | collective-permute-start | bytes 1179656 | tf_op jit(solution)/shard_map/ppermute | solution.py:305
  15.3 0.0 copy-done
  15.3 0.0 copy-done.1
  15.3 0.0 copy-done.4
  15.3 0.0 copy-done.7
  15.3 1.3 %project.1 = (bf16[32,1024]{1,0:T(8,128)(2,1)S(1)}, bf16[128,2048]{1,0:T(8,128)(2,1)S(1)}) custom-call(bf16[32,1024]{1,0:T(8,128)(2,1)S(1)} %bitcast.11, f32[1,1024]{1,0:T(1,128)S(1)} %bitcast.15, bf16[1024,1024]{1,0:T(8,128)(2,1)S(1)} %copy-done.1, bf16[128,1024]{1,0:T(8,128)(2,1)S(1)} %get-tuple-element.25.normed_ref.refs_4_, bf16[1024,2048]{1,0:T(8,128)(2,1)S(1)} %copy-done), custom_call_target="tpu_custom_call" | custom-call | flops 603979776 | bytes 6291456 | tf_op jit(solution)/shard_map/project/pallas_call | solution.py:324
  16.6 0.0 copy-done.8
  16.6 0.0 copy-done.9
  16.6 0.0 copy-done.10
  16.6 5.1 %attend.1 = (bf16[32,1024]{1,0:T(8,128)(2,1)}, bf16[192,2048]{1,0:T(8,128)(2,1)S(1)}, bf16[192,512]{1,0:T(8,128)(2,1)S(1)}, bf16[48,512]{1,0:T(8,128)(2,1)S(1)},...) custom-call(bf16[32,1024]{1,0:T(8,128)(2,1)S(1)} %collective-permute-done.outer_ref.refs_5_, ...), custom_call_target="tpu_custom_call" | custom-call | flops 3000000000 | bytes 4194304 | tf_op jit(solution)/shard_map/attend/pallas_call | solution.py:324
  21.7 0.5 collective-permute-start.4
  22.2 1.8 %collective-permute-start.5 = (bf16[48,512]{1,0:T(8,128)(2,1)S(1)}, bf16[48,512]{1,0:T(8,128)(2,1)S(1)}, u32[]{:S(2)}, u32[]{:S(2)}) collective-permute-start(bf16[48,512]{1,0:T(8,128)(2,1)S(1)} %get-tuple-element.35), channel_id=1, source_target_pairs={{0,4},{1,5},{2,6},{3,7},{4,0},{5,1},{6,2},{7,3},{8,12},{9,13},{10,... | collective-permute-start | bytes 147464 | tf_op jit(solution)/shard_map/ppermute | solution.py:305
  24.0 1.2 %collective-permute-start.6 = (bf16[48,512]{1,0:T(8,128)(2,1)S(1)}, bf16[48,512]{1,0:T(8,128)(2,1)S(1)}, u32[]{:S(2)}, u32[]{:S(2)}) collective-permute-start(bf16[48,512]{1,0:T(8,128)(2,1)S(1)} %get-tuple-element.36), channel_id=1, source_target_pairs={{0,6},{1,7},{2,4},{3,5},{4,2},{5,3},{6,0},{7,1},{8,14},{9,15},{10,... | collective-permute-start | bytes 147464 | tf_op jit(solution)/shard_map/ppermute | solution.py:305
  25.2 1.5 %window.1 = (f32[128,1024]{1,0:T(8,128)S(1)}, bf16[32,1024]{1,0:T(8,128)(2,1)S(1)}, bf16[32,1024]{1,0:T(8,128)(2,1)S(1)}) custom-call(bf16[192,2048]{1,0:T(8,128)(2,1)S(1)} %get-tuple-element.29.partial_ref, bf16[1024,2048]{1,0:T(8,128)(2,1)S(1)} %copy-done), custom_call_target="tpu_custom_call" | custom-call | flops 805306368 | bytes 4194304 | tf_op jit(solution)/shard_map/window/pallas_call | solution.py:324
  26.7 0.0 copy-start.3
  26.7 0.0 copy-start.6
  26.8 0.7 %collective-permute-done.4.refs_1_ = bf16[48,512]{1,0:T(8,128)(2,1)S(1)} collective-permute-done((bf16[48,512]{1,0:T(8,128)(2,1)S(1)}, bf16[48,512]{1,0:T(8,128)(2,1)S(1)}, u32[]{:S(2)}, u32[]{:S(2)}) %collective-permute-start.4) | collective-permute-done | bytes 49184 | tf_op jit(solution)/shard_map/ppermute | solution.py:305
  27.5 0.0 collective-permute-done.5.refs_2_
  27.5 1.5 %collective-permute-done.6.refs_3_ = bf16[48,512]{1,0:T(8,128)(2,1)S(1)} collective-permute-done((bf16[48,512]{1,0:T(8,128)(2,1)S(1)}, bf16[48,512]{1,0:T(8,128)(2,1)S(1)}, u32[]{:S(2)}, u32[]{:S(2)}) %collective-permute-start.6) | collective-permute-done | bytes 49184 | tf_op jit(solution)/shard_map/ppermute | solution.py:305
  29.0 0.0 collective-permute-done.8.refs_8_
  29.0 0.0 collective-permute-done.9.refs_9_
  29.0 1.7 %product_send.1 = bf16[256,1024]{1,0:T(8,128)(2,1)S(1)} custom-call(bf16[192,512]{1,0:T(8,128)(2,1)S(1)} %get-tuple-element.37.refs_0_, bf16[48,512]{1,0:T(8,128)(2,1)S(1)} %collective-permute-done.4.refs_1_, bf16[48,512]{1,0:T(8,128)(2,1)S(1)} %collective-permute-done.5.refs_2_, bf16[48,512]{1,0:T(8,128)(2,1)S(1)} %collective-permute-done.6.refs_3_, ...), custom_call_target="tpu_custom_call" | custom-call | flops 402653184 | bytes 4194304 | tf_op jit(solution)/shard_map/product_send/pallas_call | solution.py:324
  30.7 0.1 collective-permute-start.10
  30.7 1.7 %product_keep.1.keep_ref = f32[256,1024]{1,0:T(8,128)S(1)} custom-call(bf16[192,512]{1,0:T(8,128)(2,1)S(1)} %get-tuple-element.37.refs_0_, bf16[48,512]{1,0:T(8,128)(2,1)S(1)} %collective-permute-done.4.refs_1_, bf16[48,512]{1,0:T(8,128)(2,1)S(1)} %collective-permute-done.5.refs_2_, bf16[48,512]{1,0:T(8,128)(2,1)S(1)} %collective-permute-done.6.refs_3_, ...), custom_call_target="tpu_custom_call" | custom-call | flops 402653184 | bytes 4194304 | tf_op jit(solution)/shard_map/product_keep/pallas_call | solution.py:324
  32.4 0.2 collective-permute-done.10.got_ref
  32.6 0.1 pair.1
  32.7 0.7 %collective-permute-start.11 = (bf16[64,1024]{1,0:T(8,128)(2,1)S(1)}, bf16[64,1024]{1,0:T(8,128)(2,1)S(1)}, u32[]{:S(2)}, u32[]{:S(2)}) collective-permute-start(bf16[64,1024]{1,0:T(8,128)(2,1)S(1)} %get-tuple-element.42), channel_id=1, source_target_pairs={{0,8},{1,9},{2,10},{3,11},{4,12},{5,13},{6,14},{7,15},{8,0},{9,1},... | collective-permute-start | bytes 393224 | tf_op jit(solution)/shard_map/ppermute | solution.py:305
  33.4 1.3 %collective-permute-start.12 = (bf16[64,1024]{1,0:T(8,128)(2,1)S(1)}, bf16[64,1024]{1,0:T(8,128)(2,1)S(1)}, u32[]{:S(2)}, u32[]{:S(2)}) collective-permute-start(bf16[64,1024]{1,0:T(8,128)(2,1)S(1)} %get-tuple-element.43), channel_id=1, source_target_pairs={{0,16},{1,17},{2,18},{3,19},{4,20},{5,21},{6,22},{7,23},{8,24},{9,... | collective-permute-start | bytes 393224 | tf_op jit(solution)/shard_map/ppermute | solution.py:305
  34.7 1.6 %collective-permute-start.13 = (bf16[64,1024]{1,0:T(8,128)(2,1)S(1)}, bf16[64,1024]{1,0:T(8,128)(2,1)S(1)}, u32[]{:S(2)}, u32[]{:S(2)}) collective-permute-start(bf16[64,1024]{1,0:T(8,128)(2,1)S(1)} %get-tuple-element.44), channel_id=1, source_target_pairs={{0,24},{1,25},{2,26},{3,27},{4,28},{5,29},{6,30},{7,31},{8,16},{9,... | collective-permute-start | bytes 393224 | tf_op jit(solution)/shard_map/ppermute | solution.py:305
  36.3 0.6 %collective-permute-start.2 = (bf16[32,1024]{1,0:T(8,128)(2,1)S(1)}, bf16[32,1024]{1,0:T(8,128)(2,1)S(1)}, u32[]{:S(2)}, u32[]{:S(2)}) collective-permute-start(bf16[32,1024]{1,0:T(8,128)(2,1)S(1)} %get-tuple-element.31), channel_id=1, source_target_pairs={{0,4},{1,5},{2,6},{3,7},{4,0},{5,1},{6,2},{7,3},{8,12},{9,13},{10,... | collective-permute-start | bytes 196616 | tf_op jit(solution)/shard_map/ppermute | solution.py:305
  36.9 3.2 %collective-permute-start.3 = (bf16[32,1024]{1,0:T(8,128)(2,1)S(1)}, bf16[32,1024]{1,0:T(8,128)(2,1)S(1)}, u32[]{:S(2)}, u32[]{:S(2)}) collective-permute-start(bf16[32,1024]{1,0:T(8,128)(2,1)S(1)} %get-tuple-element.32), channel_id=1, source_target_pairs={{4,8},{12,16},{20,24},{8,4},{16,12},{24,20},{5,9},{13,17},{21,25},... | collective-permute-start | bytes 196616 | tf_op jit(solution)/shard_map/ppermute | solution.py:311
  40.1 0.5 collective-permute-done.2.inner_ref
  40.5 9.0 %collective-permute-done.3.outer_ref = bf16[32,1024]{1,0:T(8,128)(2,1)S(1)} collective-permute-done((bf16[32,1024]{1,0:T(8,128)(2,1)S(1)}, bf16[32,1024]{1,0:T(8,128)(2,1)S(1)}, u32[]{:S(2)}, u32[]{:S(2)}) %collective-permute-start.3) | collective-permute-done | bytes 65568 | tf_op jit(solution)/shard_map/ppermute | solution.py:311
  49.6 0.0 copy-done.3
  49.6 0.0 copy-done.6
  49.6 1.1 %finish.1 = bf16[128,1024]{1,0:T(8,128)(2,1)} custom-call(bf16[128,1024]{1,0:T(8,128)(2,1)S(1)} %bitcast.10, f32[1,1024]{1,0:T(1,128)S(1)} %bitcast.14, f32[128,1024]{1,0:T(8,128)S(1)} %get-tuple-element.30.own_ref, bf16[32,1024]{1,0:T(8,128)(2,1)S(1)} %collective-permute-done.2.inner_ref, bf16[32,1024]{1,0:T(8,128)(2,1)S(1)} %collective-permute-done.3.outer_ref), custom_call_target="tpu_custom_call" | custom-call | flops 2621440 | bytes 1048576 | tf_op jit(solution)/shard_map/finish/pallas_call | solution.py:324
  50.7 0.0 collective-permute-done.11.refs_1_
  50.7 0.0 collective-permute-done.12.refs_2_
  50.7 0.0 collective-permute-done.13.refs_3_
  50.7 0.8 %total.1 = f32[64,1024]{1,0:T(8,128)} custom-call(f32[64,1024]{1,0:T(8,128)S(1)} %get-tuple-element.41.refs_0_, bf16[64,1024]{1,0:T(8,128)(2,1)S(1)} %collective-permute-done.11.refs_1_, bf16[64,1024]{1,0:T(8,128)(2,1)S(1)} %collective-permute-done.12.refs_2_, bf16[64,1024]{1,0:T(8,128)(2,1)S(1)} %collective-permute-done.13.refs_3_), custom_call_target="tpu_custom_call" | custom-call | tf_op jit(solution)/shard_map/total/pallas_call | solution.py:324
  (1 shorter events, 0.0 us)
Async XLA Ops:
  0.6 1.0 %copy-start.2 = (bf16[1,128,1024]{2,1,0:T(8,128)(2,1)S(1)}, bf16[1,128,1024]{2,1,0:T(8,128)(2,1)}, u32[]{:S(2)}) copy-start(bf16[1,128,1024]{2,1,0:T(8,128)(2,1)} %param.9) | copy-start | bytes 786436
  1.6 0.7 %copy-start.5 = (f32[1024]{0:T(1024)S(1)}, f32[1024]{0:T(1024)}, u32[]{:S(2)}) copy-start(f32[1024]{0:T(1024)} %param.14) | copy-start | bytes 12292
  2.3 13.0 %copy-start = (bf16[1024,2048]{1,0:T(8,128)(2,1)S(1)}, bf16[1024,2048]{1,0:T(8,128)(2,1)}, u32[]{:S(2)}) copy-start(bf16[1024,2048]{1,0:T(8,128)(2,1)} %wkv_ref.5) | copy-start | bytes 12582916
  2.3 13.0 %copy-start.1 = (bf16[1024,1024]{1,0:T(8,128)(2,1)S(1)}, bf16[1024,1024]{1,0:T(8,128)(2,1)}, u32[]{:S(2)}) copy-start(bf16[1024,1024]{1,0:T(8,128)(2,1)} %wq_ref.1) | copy-start | bytes 6291460
  2.3 13.0 %copy-start.4 = (bf16[1,32,1024]{2,1,0:T(8,128)(2,1)S(1)}, bf16[1,32,1024]{2,1,0:T(8,128)(2,1)}, u32[]{:S(2)}) copy-start(bf16[1,32,1024]{2,1,0:T(8,128)(2,1)} %param.10) | copy-start | bytes 196612
  2.3 13.0 %copy-start.7 = (f32[1024]{0:T(1024)S(1)}, f32[1024]{0:T(1024)}, u32[]{:S(2)}) copy-start(f32[1024]{0:T(1024)} %param.15) | copy-start | bytes 12292
  2.5 14.0 %copy-start.8 = (bf16[1,32,1024]{2,1,0:T(8,128)(2,1)S(1)}, bf16[1,32,1024]{2,1,0:T(8,128)(2,1)}, u32[]{:S(2)}) copy-start(bf16[1,32,1024]{2,1,0:T(8,128)(2,1)} %param.11) | copy-start | bytes 196612
  2.6 14.0 %copy-start.9 = (s32[32,12]{0,1:T(8,128)S(1)}, s32[32,12]{0,1:T(8,128)}, u32[]{:S(2)}) copy-start(s32[32,12]{0,1:T(8,128)} %param.16) | copy-start | bytes 4612
  2.6 14.0 %copy-start.10 = (s32[32,12]{0,1:T(8,128)S(1)}, s32[32,12]{0,1:T(8,128)}, u32[]{:S(2)}) copy-start(s32[32,12]{0,1:T(8,128)} %param.17) | copy-start | bytes 4612
  2.6 11.1 %collective-permute-start.1 = (bf16[128,1024]{1,0:T(8,128)(2,1)S(1)}, bf16[128,1024]{1,0:T(8,128)(2,1)S(1)}, u32[]{:S(2)}, u32[]{:S(2)}) collective-permute-start(bf16[128,1024]{1,0:T(8,128)(2,1)S(1)} %get-tuple-element.25.normed_ref.refs_4_), channel_id=1, source_target_pairs={{0,4},{1,5},{2,6},{3,7},{4,0},{5,1},{6,2},{7,3},{8,12},{9,13},{10,... | collective-permute-start | bytes 786440 | tf_op jit(solution)/shard_map/ppermute | solution.py:305
  4.1 7.7 %collective-permute-start.7 = (bf16[32,1024]{1,0:T(8,128)(2,1)S(1)}, bf16[32,1024]{1,0:T(8,128)(2,1)S(1)}, u32[]{:S(2)}, u32[]{:S(2)}) collective-permute-start(bf16[32,1024]{1,0:T(8,128)(2,1)S(1)} %get-tuple-element.24), channel_id=1, source_target_pairs={{4,12},{12,20},{20,28},{8,0},{16,8},{24,16},{5,13},{13,21},{21,29}... | collective-permute-start | bytes 196616 | tf_op jit(solution)/shard_map/ppermute | solution.py:317
  6.6 7.1 %collective-permute-start = (bf16[32,1024]{1,0:T(8,128)(2,1)S(1)}, bf16[32,1024]{1,0:T(8,128)(2,1)S(1)}, u32[]{:S(2)}, u32[]{:S(2)}) collective-permute-start(bf16[32,1024]{1,0:T(8,128)(2,1)S(1)} %get-tuple-element.24), channel_id=1, source_target_pairs={{4,8},{12,16},{20,24},{8,4},{16,12},{24,20},{5,9},{13,17},{21,25},... | collective-permute-start | bytes 196616 | tf_op jit(solution)/shard_map/ppermute | solution.py:311
  10.2 18.8 %collective-permute-start.8 = (bf16[128,1024]{1,0:T(8,128)(2,1)S(1)}, bf16[128,1024]{1,0:T(8,128)(2,1)S(1)}, u32[]{:S(2)}, u32[]{:S(2)}) collective-permute-start(bf16[128,1024]{1,0:T(8,128)(2,1)S(1)} %get-tuple-element.25.normed_ref.refs_4_), channel_id=1, source_target_pairs={{0,2},{1,3},{2,0},{3,1},{4,6},{5,7},{6,4},{7,5},{8,10},{9,11},{10,... | collective-permute-start | bytes 786440 | tf_op jit(solution)/shard_map/ppermute | solution.py:305
  13.7 15.3 %collective-permute-start.9 = (bf16[192,1024]{1,0:T(8,128)(2,1)S(1)}, bf16[192,1024]{1,0:T(8,128)(2,1)S(1)}, u32[]{:S(2)}, u32[]{:S(2)}) collective-permute-start(bf16[192,1024]{1,0:T(8,128)(2,1)S(1)} %pad_maximum_fusion), channel_id=1, source_target_pairs={{0,2},{1,3},{2,0},{3,1},{4,6},{5,7},{6,4},{7,5},{8,10},{9,11},{10,... | collective-permute-start | bytes 1179656 | tf_op jit(solution)/shard_map/ppermute | solution.py:305
  21.7 5.8 %collective-permute-start.4 = (bf16[48,512]{1,0:T(8,128)(2,1)S(1)}, bf16[48,512]{1,0:T(8,128)(2,1)S(1)}, u32[]{:S(2)}, u32[]{:S(2)}) collective-permute-start(bf16[48,512]{1,0:T(8,128)(2,1)S(1)} %get-tuple-element.34), channel_id=1, source_target_pairs={{0,2},{1,3},{2,0},{3,1},{4,6},{5,7},{6,4},{7,5},{8,10},{9,11},{10,... | collective-permute-start | bytes 147464 | tf_op jit(solution)/shard_map/ppermute | solution.py:305
  22.2 5.3 %collective-permute-start.5 = (bf16[48,512]{1,0:T(8,128)(2,1)S(1)}, bf16[48,512]{1,0:T(8,128)(2,1)S(1)}, u32[]{:S(2)}, u32[]{:S(2)}) collective-permute-start(bf16[48,512]{1,0:T(8,128)(2,1)S(1)} %get-tuple-element.35), channel_id=1, source_target_pairs={{0,4},{1,5},{2,6},{3,7},{4,0},{5,1},{6,2},{7,3},{8,12},{9,13},{10,... | collective-permute-start | bytes 147464 | tf_op jit(solution)/shard_map/ppermute | solution.py:305
  24.0 5.0 %collective-permute-start.6 = (bf16[48,512]{1,0:T(8,128)(2,1)S(1)}, bf16[48,512]{1,0:T(8,128)(2,1)S(1)}, u32[]{:S(2)}, u32[]{:S(2)}) collective-permute-start(bf16[48,512]{1,0:T(8,128)(2,1)S(1)} %get-tuple-element.36), channel_id=1, source_target_pairs={{0,6},{1,7},{2,4},{3,5},{4,2},{5,3},{6,0},{7,1},{8,14},{9,15},{10,... | collective-permute-start | bytes 147464 | tf_op jit(solution)/shard_map/ppermute | solution.py:305
  26.7 22.8 %copy-start.3 = (bf16[1,128,1024]{2,1,0:T(8,128)(2,1)S(1)}, bf16[1,128,1024]{2,1,0:T(8,128)(2,1)}, u32[]{:S(2)}) copy-start(bf16[1,128,1024]{2,1,0:T(8,128)(2,1)} %param.9) | copy-start | bytes 786436
  26.7 22.8 %copy-start.6 = (f32[1024]{0:T(1024)S(1)}, f32[1024]{0:T(1024)}, u32[]{:S(2)}) copy-start(f32[1024]{0:T(1024)} %param.14) | copy-start | bytes 12292
  30.7 2.0 %collective-permute-start.10 = (bf16[256,1024]{1,0:T(8,128)(2,1)S(1)}, bf16[256,1024]{1,0:T(8,128)(2,1)S(1)}, u32[]{:S(2)}, u32[]{:S(2)}) collective-permute-start(bf16[256,1024]{1,0:T(8,128)(2,1)S(1)} %product_send.1), channel_id=1, source_target_pairs={{0,1},{1,0},{2,3},{3,2},{4,5},{5,4},{6,7},{7,6},{8,9},{9,8},{10,11... | collective-permute-start | bytes 1572872 | tf_op jit(solution)/shard_map/ppermute | solution.py:305
  32.7 18.0 %collective-permute-start.11 = (bf16[64,1024]{1,0:T(8,128)(2,1)S(1)}, bf16[64,1024]{1,0:T(8,128)(2,1)S(1)}, u32[]{:S(2)}, u32[]{:S(2)}) collective-permute-start(bf16[64,1024]{1,0:T(8,128)(2,1)S(1)} %get-tuple-element.42), channel_id=1, source_target_pairs={{0,8},{1,9},{2,10},{3,11},{4,12},{5,13},{6,14},{7,15},{8,0},{9,1},... | collective-permute-start | bytes 393224 | tf_op jit(solution)/shard_map/ppermute | solution.py:305
  33.4 17.3 %collective-permute-start.12 = (bf16[64,1024]{1,0:T(8,128)(2,1)S(1)}, bf16[64,1024]{1,0:T(8,128)(2,1)S(1)}, u32[]{:S(2)}, u32[]{:S(2)}) collective-permute-start(bf16[64,1024]{1,0:T(8,128)(2,1)S(1)} %get-tuple-element.43), channel_id=1, source_target_pairs={{0,16},{1,17},{2,18},{3,19},{4,20},{5,21},{6,22},{7,23},{8,24},{9,... | collective-permute-start | bytes 393224 | tf_op jit(solution)/shard_map/ppermute | solution.py:305
  34.7 16.0 %collective-permute-start.13 = (bf16[64,1024]{1,0:T(8,128)(2,1)S(1)}, bf16[64,1024]{1,0:T(8,128)(2,1)S(1)}, u32[]{:S(2)}, u32[]{:S(2)}) collective-permute-start(bf16[64,1024]{1,0:T(8,128)(2,1)S(1)} %get-tuple-element.44), channel_id=1, source_target_pairs={{0,24},{1,25},{2,26},{3,27},{4,28},{5,29},{6,30},{7,31},{8,16},{9,... | collective-permute-start | bytes 393224 | tf_op jit(solution)/shard_map/ppermute | solution.py:305
  36.3 4.3 %collective-permute-start.2 = (bf16[32,1024]{1,0:T(8,128)(2,1)S(1)}, bf16[32,1024]{1,0:T(8,128)(2,1)S(1)}, u32[]{:S(2)}, u32[]{:S(2)}) collective-permute-start(bf16[32,1024]{1,0:T(8,128)(2,1)S(1)} %get-tuple-element.31), channel_id=1, source_target_pairs={{0,4},{1,5},{2,6},{3,7},{4,0},{5,1},{6,2},{7,3},{8,12},{9,13},{10,... | collective-permute-start | bytes 196616 | tf_op jit(solution)/shard_map/ppermute | solution.py:305
  36.9 12.7 %collective-permute-start.3 = (bf16[32,1024]{1,0:T(8,128)(2,1)S(1)}, bf16[32,1024]{1,0:T(8,128)(2,1)S(1)}, u32[]{:S(2)}, u32[]{:S(2)}) collective-permute-start(bf16[32,1024]{1,0:T(8,128)(2,1)S(1)} %get-tuple-element.32), channel_id=1, source_target_pairs={{4,8},{12,16},{20,24},{8,4},{16,12},{24,20},{5,9},{13,17},{21,25},... | collective-permute-start | bytes 196616 | tf_op jit(solution)/shard_map/ppermute | solution.py:311
